TPU v7x, 32 devices: a whole 2x2x4 slice. The times are simulated.
32 devices in a mesh: azi: 8 (over z, core), ax: 2 (over y), rad: 2 (over x).
Axes of the slice: x: 2, y: 2, z: 4, core: 2. Of those that a mesh axis runs over, the one named last changes fastest.
Arguments:
- fields: float32 [2, 512, 32, 1024], P(None, 'azi', 'ax', 'rad'), may hold values from 0 to 1.5
- swirl_speed: float32 [512, 32, 1024], P('azi', 'ax', 'rad'), may hold values from 0.05 to 0.35
- ghost_mask: int32 [512, 32, 1024], P('azi', 'ax', 'rad'), may hold values 0 or 1
- tile_flags: int32 [32, 32], P('azi', 'ax'), may hold values 0 or 1
- outlet_gain: float32 [2, 32], replicated, may hold values from 0.25 to 1
- feed_rate: float32 [8, 8, 8], P('azi'), may hold values from 0.05 to 0.5
- plenum: float32 [8, 8, 8, 1024], P('azi', None, None, 'rad'), may hold values from 0.5 to 1.5
- feed_target: int32 [8, 8, 8], P('azi'), may hold values from -1 to 255, as said below
Outputs:
- new_fields: float32 [2, 512, 32, 1024], P(None, 'azi', 'ax', 'rad')
Inputs may be any that keep to these rules, and one draw needn't show every extreme that they name: `feed_target`: entry i >= 0 names azimuthal cell i // 4 and axial cell i mod 4 of sector d; -1 marks an empty slot, and the used slots of a pair come first. At most 8 slots per pair are used; in every draw one sector receives 8 from every sector.
All inputs are finite; a program needn't handle non-finite values. No bound on the sum of `ghost_mask` or of `tile_flags` on one device may be relied on, other than what follows from the above.
Results may differ from a plain program's by a relative error of at most 0.00005.
Values sent between devices are 32-bit elements; how exact they have to be, the bound alone decides.
No kernel may reach another device: no remote copies, remote signals or barrier semaphores. Data moves between devices by JAX's collectives and lax.ppermute only.
A program may use at most 64 MiB of HBM per device.

v0:
```python
import math

import jax
import jax.numpy as jnp
from jax import lax
from jax.sharding import PartitionSpec as P

K = 32
TILE = 16
HEAD = 4


def with_halo(block, sides, width, periodic):
    for axis, dim in sides:
        count = lax.axis_size(axis)
        forward = [(i, i + 1) for i in range(count - 1)]
        if periodic:
            forward.append((count - 1, 0))
        backward = [(target, source) for source, target in forward]
        low = lax.ppermute(
            lax.slice_in_dim(block, block.shape[dim] - width, None, axis=dim), axis, forward
        )
        high = lax.ppermute(lax.slice_in_dim(block, 0, width, axis=dim), axis, backward)
        block = jnp.concatenate([low, block, high], axis=dim)
    return block


def phase_table(length, first_cell, cell_count, mode_count):
    theta_index = first_cell + jnp.arange(cell_count, dtype=jnp.int32)
    mode_order = jnp.arange(1, mode_count + 1, dtype=jnp.int32)
    phase_int = mode_order[:, None] * theta_index[None, :] % length
    angles = phase_int.astype(jnp.float32) * (2.0 * math.pi / length)
    return jnp.concatenate([jnp.cos(angles), jnp.sin(angles)], axis=0)


def body(fields, swirl_speed, ghost_mask, tile_flags, outlet_gain, feed_rate, plenum, feed_target):
    sectors = lax.axis_size("azi")
    sector = lax.axis_index("azi")
    slab_index = lax.axis_index("ax")
    slab_count = lax.axis_size("ax")
    sector_cells = fields.shape[1]
    depth_cells = fields.shape[2]
    radial_cells = fields.shape[3]
    length = sector_cells * sectors
    phase_rows = phase_table(length, sector * sector_cells, sector_cells, K)
    outlet_plane = fields[:, :, -1, :]
    partial_value = jnp.einsum(
        "mt,ctr->cmr", phase_rows, outlet_plane, precision=lax.Precision.HIGHEST
    )
    gain_both = jnp.concatenate([outlet_gain, outlet_gain], axis=1)
    mode_sums = lax.psum(partial_value, "azi")
    rebuilt = jnp.einsum(
        "mt,cmr->ctr",
        phase_rows,
        mode_sums * gain_both[:, :, None],
        precision=lax.Precision.HIGHEST,
    )
    ghost_plane = outlet_plane - rebuilt * (2.0 / math.sqrt(K * length))
    azimuth_pad = with_halo(fields, (("azi", 1),), 1, True)
    face_pad = with_halo(fields, (("ax", 2), ("rad", 3)), 1, False)
    theta_prev = azimuth_pad[:, :-2]
    theta_next = azimuth_pad[:, 2:]
    axial_prev = face_pad[:, :, :-2, 1:-1]
    axial_inner = face_pad[:, :, 2:, 1:-1]
    radial_prev = face_pad[:, :, 1:-1, :-2]
    radial_next = face_pad[:, :, 1:-1, 2:]
    is_outlet = slab_index == slab_count - 1
    top_layer = jnp.where(is_outlet, ghost_plane, axial_inner[:, :, -1, :])
    axial_next = jnp.concatenate([axial_inner[:, :, :-1, :], top_layer[:, :, None, :]], axis=2)
    laplace_term = (
        theta_prev + theta_next + axial_prev + axial_next + radial_prev + radial_next - 6.0 * fields
    )
    upwind_term = swirl_speed[None] * (fields - theta_prev)
    energy = fields[0]
    fuel_part = fields[1]
    tile_on = jnp.repeat(tile_flags, TILE, axis=0).astype(jnp.float32)
    inert = ghost_mask.astype(jnp.float32)
    reaction = (
        0.5 * tile_on[:, :, None] * (1.0 - inert) * fuel_part * jax.nn.sigmoid(4.0 * (energy - 0.5))
    )
    payload = feed_rate[0][:, :, None] * plenum[0]
    arrived = lax.all_to_all(payload, "azi", split_axis=0, concat_axis=0, tiled=True)
    targets = feed_target[0]
    occupied = targets >= 0
    row_index = jnp.where(
        occupied, targets // HEAD * depth_cells + targets % HEAD, sector_cells * depth_cells
    )
    feed_term = jnp.zeros((sector_cells * depth_cells, radial_cells), jnp.float32)
    feed_term = feed_term.at[row_index.reshape(-1)].add(
        arrived.reshape(-1, radial_cells), mode="drop"
    )
    feed_term = feed_term.reshape(sector_cells, depth_cells, radial_cells) * (
        slab_index == 0
    ).astype(jnp.float32)
    new_energy = energy - upwind_term[0] + 0.1 * laplace_term[0] + 2.0 * reaction
    new_fuel = fuel_part - upwind_term[1] + 0.1 * laplace_term[1] - reaction + feed_term
    return jnp.stack([new_energy, new_fuel], axis=0)


def solution(mesh):
    return jax.shard_map(
        body,
        mesh=mesh,
        in_specs=(
            P(None, "azi", "ax", "rad"),
            P("azi", "ax", "rad"),
            P("azi", "ax", "rad"),
            P("azi", "ax"),
            P(),
            P("azi", None, None),
            P("azi", None, None, "rad"),
            P("azi", None, None),
        ),
        out_specs=P(None, "azi", "ax", "rad"),
        check_vma=False,
    )
```

profile of v0, /device:TPU:0, one launch (start us, length us, event | category | flops | bytes accessed | tf_op | source)
XLA Modules:
  0.0 102.9 jit_solution(10300405495476792824)
XLA Ops:
  6.5 2.8 %fusion.38 = (f32[2,64,1,512]{3,2,1,0:T(1,128)S(1)}, f32[2,64,1,512]{3,2,1,0:T(1,128)S(1)}) fusion(f32[2,64,16,512]{3,2,1,0:T(8,128)} %param.8), kind=kLoop, calls=%fused_computation.80 | loop fusion | bytes 1048576 | tf_op jit(solution)/shard_map/slice | solution.py:21
  9.3 0.2 fusion.31
  9.5 1.1 %convolution_bitcast_fusion = f32[2,64,512]{2,1,0:T(8,128)} fusion(f32[32,64]{1,0:T(8,128)S(1)} %get-tuple-element.14, f32[32,64]{1,0:T(8,128)S(1)} %get-tuple-element.13, f32[2,64,1,512]{3,2,1,0:T(1,128)S(1)} %get-tuple-element.11), kind=kOutput, calls=%fused_computation.41 | convolution fusion | flops 50335744 | bytes 540672 | tf_op jit(solution)/shard_map/mt,ctr->cmr/dot_general | solution.py:47
  10.6 0.0 all-reduce.2.cloned.1.call-update
  10.6 1.3 %collective-permute-start.3 = (f32[2,64,1,512]{3,1,0,2:T(8,128)S(1)}, f32[2,64,1,512]{3,1,0,2:T(8,128)S(1)}, u32[]{:S(2)}, u32[]{:S(2)}) collective-permute-start(f32[2,64,1,512]{3,1,0,2:T(8,128)S(1)} %copy.56), channel_id=1, source_target_pairs={{2,0},{3,1},{6,4},{7,5},{10,8},{11,9},{14,12},{15,13},{18,16},{19,... | collective-permute-start | bytes 786440 | tf_op jit(solution)/shard_map/ppermute | solution.py:23
  11.9 0.7 copy.55
  12.7 4.9 %collective-permute-start.2 = (f32[2,64,1,512]{3,1,0,2:T(8,128)}, f32[2,64,1,512]{3,1,0,2:T(8,128)S(1)}, u32[]{:S(2)}, u32[]{:S(2)}) collective-permute-start(f32[2,64,1,512]{3,1,0,2:T(8,128)} %copy.55), channel_id=1, source_target_pairs={{0,2},{1,3},{4,6},{5,7},{8,10},{9,11},{12,14},{13,15},{16,18},{17,... | collective-permute-start | bytes 786440 | tf_op jit(solution)/shard_map/ppermute | solution.py:20
  17.6 1.5 %fusion.37 = (f32[2,1,16,512]{3,2,1,0:T(8,128)S(1)}, f32[2,1,16,512]{3,2,1,0:T(8,128)}) fusion(f32[2,64,16,512]{3,2,1,0:T(8,128)} %param.8), kind=kLoop, calls=%fused_computation.79 | loop fusion | bytes 262144 | tf_op jit(solution)/shard_map/slice | solution.py:21
  19.1 0.0 collective-permute-start
  19.1 3.6 %collective-permute-start.1 = (f32[2,1,16,512]{3,2,1,0:T(8,128)}, f32[2,1,16,512]{3,2,1,0:T(8,128)}, u32[]{:S(2)}, u32[]{:S(2)}) collective-permute-start(f32[2,1,16,512]{3,2,1,0:T(8,128)} %get-tuple-element.10), channel_id=1, source_target_pairs={{4,0},{8,4},{12,8},{16,12},{20,16},{24,20},{28,24},{0,28},{5,1},{9... | collective-permute-start | bytes 196616 | tf_op jit(solution)/shard_map/ppermute | solution.py:23
  22.7 0.0 copy-done.10
  22.7 0.7 bitcast_multiply_fusion.2
  23.5 4.1 %all-to-all-start = ((f32[8,8,512]{2,1,0:T(8,128)}), f32[8,8,512]{2,1,0:T(8,128)S(1)}, u32[]{:S(2)}, u32[]{:S(2)}) async-start(f32[8,8,512]{2,1,0:T(8,128)} %bitcast_multiply_fusion.2), calls=%async_computation | async-start | bytes 262144 | tf_op jit(solution)/shard_map/all_to_all | solution.py:82
  27.6 0.0 copy-start.11
  27.6 0.0 copy-start.13
  27.6 0.0 copy-start.7
  27.6 5.2 %slice.74 = f32[2,64,15,512]{3,2,1,0:T(8,128)} slice(f32[2,64,16,512]{3,2,1,0:T(8,128)} %param.8), slice={[0:2], [0:64], [1:16], [0:512]} | slice | bytes 7864320 | tf_op jit(solution)/shard_map/slice | solution.py:69
  32.9 0.1 squeeze.26
  33.0 0.1 pad_maximum_fusion.13
  33.1 0.0 collective-permute-done
  33.1 6.9 %fusion.7 = f32[2,64,16,512]{3,2,1,0:T(8,128)} fusion(f32[2,64,16,512]{3,2,1,0:T(8,128)} %param.8, f32[2,1,16,512]{3,2,1,0:T(8,128)S(1)} %collective-permute-done, f32[64,16,512]{2,1,0:T(8,128)S(1)} %copy-done.7), kind=kLoop, calls=%fused_computation.17 | loop fusion | flops 3145728 | bytes 10551296 | tf_op jit(solution)/shard_map/mul | solution.py:73
  40.0 0.0 all-to-all-done
  40.0 1.5 %scatter_custom_fusion = f32[1024,512]{1,0:T(8,128)S(1)} fusion(s32[64]{0:T(128)S(1)} %fusion.33, f32[]{:T(128)} %constant.78.clone.1, f32[8,8,512]{2,1,0:T(8,128)S(1)} %all-to-all-done), kind=kCustom, calls=%fused_computation.43 | custom fusion | flops 32768 | bytes 2228228 | tf_op jit(solution)/shard_map/scatter-add | solution.py:89
  41.5 0.0 copy-start
  41.5 1.6 %broadcast_multiply_fusion = f32[1024,512]{1,0:T(8,128)} fusion(f32[1024,512]{1,0:T(8,128)S(1)} %scatter_custom_fusion, f32[]{:T(128)S(6)} %convert_element_type.21), kind=kLoop, calls=%fused_computation.42 | loop fusion | flops 524288 | bytes 4194308 | tf_op jit(solution)/shard_map/mul | solution.py:92
  43.1 0.0 collective-permute-done.2
  43.1 0.3 copy.43
  43.4 0.0 collective-permute-done.3
  43.4 0.7 copy-done.8
  44.1 0.3 copy.48
  44.4 0.3 copy-done
  44.7 1.0 pad_maximum_fusion.12
  45.7 0.5 copy.49
  46.1 3.7 %collective-permute-start.4 = (f32[2,64,18,1]{1,0,3,2:T(2,128)S(1)}, f32[2,64,18,1]{1,0,3,2:T(2,128)S(1)}, u32[]{:S(2)}, u32[]{:S(2)}) collective-permute-start(f32[2,64,18,1]{1,0,3,2:T(2,128)S(1)} %copy.49), channel_id=1, source_target_pairs={{0,1},{2,3},{4,5},{6,7},{8,9},{10,11},{12,13},{14,15},{16,17},{18,... | collective-permute-start | bytes 27656 | tf_op jit(solution)/shard_map/ppermute | solution.py:20
  49.9 0.5 copy.51
  50.3 1.5 %collective-permute-start.5 = (f32[2,64,18,1]{1,0,3,2:T(2,128)S(1)}, f32[2,64,18,1]{1,0,3,2:T(2,128)S(1)}, u32[]{:S(2)}, u32[]{:S(2)}) collective-permute-start(f32[2,64,18,1]{1,0,3,2:T(2,128)S(1)} %copy.51), channel_id=1, source_target_pairs={{1,0},{3,2},{5,4},{7,6},{9,8},{11,10},{13,12},{15,14},{17,16},{19,... | collective-permute-start | bytes 27656 | tf_op jit(solution)/shard_map/ppermute | solution.py:23
  51.8 17.9 %all-reduce.2.cloned.1.call-done = f32[2,64,512]{2,1,0:T(8,128)} async-done(((f32[2,64,512]{2,1,0:T(8,128)}), f32[2,64,512]{2,1,0:T(8,128)}) %all-reduce.2.cloned.1.call-update) | async-done | bytes 262160 | tf_op jit(solution)/shard_map/psum | solution.py:51
  69.7 1.5 %fusion.22 = f32[2,64,1,512]{3,1,0,2:T(8,128)S(1)} fusion(f32[2,64,1,512]{3,1,0,2:T(8,128)} %copy-done.8, f32[2,64,512]{2,1,0:T(8,128)} %all-reduce.2.cloned.1.call-done, f32[2,64]{1,0:T(2,128)S(1)} %pad_maximum_fusion.13, pred[]{:T(512)S(6)} %eq.10, f32[32,64]{1,0:T(8,128)S(1)} %get-tuple-element.14, f32[32,64]{1,0:T(8,128)S(1)} %get-tuple-element.13, ...), kind=kOutput, calls=%fused_computation.46 | convolution fusion | flops 50597888 | bytes 1065473 | tf_op jit(solution)/shard_map/mt,cmr->ctr/dot_general | solution.py:52
  71.2 1.0 copy.46
  72.1 0.0 collective-permute-done.4
  72.2 0.6 copy.50
  72.7 0.0 collective-permute-done.5
  72.8 1.7 %copy.52 = f32[2,64,18,1]{3,2,1,0:T(8,128)} copy(f32[2,64,18,1]{1,0,3,2:T(2,128)S(1)} %collective-permute-done.5) | data formatting | bytes 18432 | tf_op jit(solution)/shard_map/ppermute | solution.py:23
  74.4 0.0 collective-permute-done.1
  74.5 15.2 %fusion.1 = f32[2,64,16,512]{3,2,1,0:T(8,128)S(1)} fusion(f32[2,64,18,1]{3,2,1,0:T(8,128)} %copy.52, f32[2,64,1,512]{3,2,1,0:T(1,128)} %copy-done.6, f32[2,64,16,512]{3,2,1,0:T(8,128)} %param.8, f32[2,64,1,512]{3,2,1,0:T(1,128)S(1)} %copy-done.5, f32[2,64,18,1]{3,2,1,0:T(8,128)S(1)} %copy.50, f32[2,1,16,512]{3,2,1,0:T(8,128)} %collective-permute-done.1, ...), kind=kLoop, calls=%fused_computation.3 | loop fusion | flops 17825792 | bytes 13256704 | tf_op jit(solution)/shard_map/sub | solution.py:71
  89.7 2.5 %fusion.17 = (f32[1,64,16,512]{3,2,1,0:T(8,128)S(1)}, f32[64,16,512]{2,1,0:T(8,128)S(1)}) fusion(f32[2,64,16,512]{3,2,1,0:T(8,128)S(1)} %fusion.1, f32[2,64,16,512]{3,2,1,0:T(8,128)S(1)} %copy-done.2, f32[2,64,16,512]{3,2,1,0:T(8,128)S(1)} %copy-done.1, s32[64,16,512]{2,1,0:T(8,128)} %param.10, f32[64,16]{1,0:T(8,128)S(1)} %bitcast.71), kind=kLoop, calls=%fused_computation.31 | loop fusion | flops 7864320 | bytes 14684160 | tf_op jit(solution)/shard_map/stack | solution.py:97
  92.2 1.3 %fusion.12 = f32[1,64,16,512]{3,2,1,0:T(8,128)S(1)} fusion(f32[64,16,512]{2,1,0:T(8,128)S(1)} %bitcast.70, f32[64,16,512]{2,1,0:T(8,128)S(1)} %get-tuple-element.6, f32[2,64,16,512]{3,2,1,0:T(8,128)S(1)} %fusion.1, f32[2,64,16,512]{3,2,1,0:T(8,128)S(1)} %copy-done.2, f32[2,64,16,512]{3,2,1,0:T(8,128)S(1)} %copy-done.1), kind=kLoop, calls=%fused_computation.24 | loop fusion | flops 2621440 | bytes 12582912 | tf_op jit(solution)/shard_map/stack | solution.py:97
  93.6 2.5 %pad_maximum_fusion.9 = f32[2,64,16,512]{3,2,1,0:T(8,128)} fusion(f32[1,64,16,512]{3,2,1,0:T(8,128)S(1)} %fusion.12, f32[1,64,16,512]{3,2,1,0:T(8,128)S(1)} %get-tuple-element.5), kind=kLoop, calls=%fused_computation.18 | loop fusion | flops 1048576 | bytes 8388608 | tf_op jit(solution)/shard_map/stack | solution.py:97
  (28 shorter events, 0.1 us)
Async XLA Ops:
  6.5 16.2 %copy-start.10 = (f32[1,8,8]{2,1,0:T(8,128)S(1)}, f32[1,8,8]{2,1,0:T(8,128)}, u32[]{:S(2)}) copy-start(f32[1,8,8]{2,1,0:T(8,128)} %param.13) | copy-start | bytes 772
  6.5 16.2 %copy-start.9 = (f32[1,8,8,512]{3,2,1,0:T(8,128)S(1)}, f32[1,8,8,512]{3,2,1,0:T(8,128)}, u32[]{:S(2)}) copy-start(f32[1,8,8,512]{3,2,1,0:T(8,128)} %param.14) | copy-start | bytes 393220
  6.5 63.1 %all-reduce.2.cloned.1.call-start = ((), (), s32[]{:S(2)}) async-start(), calls=%async_computation.1 | async-start | bytes 524288 | tf_op jit(solution)/shard_map/psum | solution.py:51
  10.6 32.8 %collective-permute-start.3 = (f32[2,64,1,512]{3,1,0,2:T(8,128)S(1)}, f32[2,64,1,512]{3,1,0,2:T(8,128)S(1)}, u32[]{:S(2)}, u32[]{:S(2)}) collective-permute-start(f32[2,64,1,512]{3,1,0,2:T(8,128)S(1)} %copy.56), channel_id=1, source_target_pairs={{2,0},{3,1},{6,4},{7,5},{10,8},{11,9},{14,12},{15,13},{18,16},{19,... | collective-permute-start | bytes 786440 | tf_op jit(solution)/shard_map/ppermute | solution.py:23
  12.7 30.4 %collective-permute-start.2 = (f32[2,64,1,512]{3,1,0,2:T(8,128)}, f32[2,64,1,512]{3,1,0,2:T(8,128)S(1)}, u32[]{:S(2)}, u32[]{:S(2)}) collective-permute-start(f32[2,64,1,512]{3,1,0,2:T(8,128)} %copy.55), channel_id=1, source_target_pairs={{0,2},{1,3},{4,6},{5,7},{8,10},{9,11},{12,14},{13,15},{16,18},{17,... | collective-permute-start | bytes 786440 | tf_op jit(solution)/shard_map/ppermute | solution.py:20
  19.1 14.0 %collective-permute-start = (f32[2,1,16,512]{3,2,1,0:T(8,128)S(1)}, f32[2,1,16,512]{3,2,1,0:T(8,128)S(1)}, u32[]{:S(2)}, u32[]{:S(2)}) collective-permute-start(f32[2,1,16,512]{3,2,1,0:T(8,128)S(1)} %get-tuple-element.9), channel_id=1, source_target_pairs={{0,4},{4,8},{8,12},{12,16},{16,20},{20,24},{24,28},{28,0},{1,5},{5... | collective-permute-start | bytes 196616 | tf_op jit(solution)/shard_map/ppermute | solution.py:20
  19.1 55.3 %collective-permute-start.1 = (f32[2,1,16,512]{3,2,1,0:T(8,128)}, f32[2,1,16,512]{3,2,1,0:T(8,128)}, u32[]{:S(2)}, u32[]{:S(2)}) collective-permute-start(f32[2,1,16,512]{3,2,1,0:T(8,128)} %get-tuple-element.10), channel_id=1, source_target_pairs={{4,0},{8,4},{12,8},{16,12},{20,16},{24,20},{28,24},{0,28},{5,1},{9... | collective-permute-start | bytes 196616 | tf_op jit(solution)/shard_map/ppermute | solution.py:23
  23.5 16.6 %all-to-all-start = ((f32[8,8,512]{2,1,0:T(8,128)}), f32[8,8,512]{2,1,0:T(8,128)S(1)}, u32[]{:S(2)}, u32[]{:S(2)}) async-start(f32[8,8,512]{2,1,0:T(8,128)} %bitcast_multiply_fusion.2), calls=%async_computation | async-start | bytes 262144 | tf_op jit(solution)/shard_map/all_to_all | solution.py:82
  27.6 5.3 %copy-start.12 = (s32[4,16]{1,0:T(4,128)S(1)}, s32[4,16]{1,0:T(4,128)}, u32[]{:S(2)}) copy-start(s32[4,16]{1,0:T(4,128)} %param.11) | copy-start | bytes 772
  27.6 5.3 %copy-start.11 = (s32[1,8,8]{2,1,0:T(8,128)S(1)}, s32[1,8,8]{2,1,0:T(8,128)}, u32[]{:S(2)}) copy-start(s32[1,8,8]{2,1,0:T(8,128)} %param.15) | copy-start | bytes 772
  27.6 5.4 %copy-start.13 = (f32[2,32]{1,0:T(2,128)S(1)}, f32[2,32]{1,0:T(2,128)}, u32[]{:S(2)}) copy-start(f32[2,32]{1,0:T(2,128)} %param.12) | copy-start | bytes 772
  27.6 5.5 %copy-start.7 = (f32[64,16,512]{2,1,0:T(8,128)S(1)}, f32[64,16,512]{2,1,0:T(8,128)}, u32[]{:S(2)}) copy-start(f32[64,16,512]{2,1,0:T(8,128)} %param.9) | copy-start | bytes 6291460
  41.5 3.1 %copy-start = (f32[2,64,16,512]{3,2,1,0:T(8,128)S(1)}, f32[2,64,16,512]{3,2,1,0:T(8,128)}, u32[]{:S(2)}) copy-start(f32[2,64,16,512]{3,2,1,0:T(8,128)} %param.8) | copy-start | bytes 12582916
  43.4 2.3 %copy-start.4 = (f32[2,64,1,512]{3,2,1,0:T(1,128)}, f32[2,64,1,512]{3,2,1,0:T(1,128)S(1)}, u32[]{:S(2)}) copy-start(f32[2,64,1,512]{3,2,1,0:T(1,128)S(1)} %copy.43) | copy-start | bytes 786436
  43.4 0.7 copy-start.8
  44.7 1.0 copy-start.6
  46.1 26.0 %collective-permute-start.4 = (f32[2,64,18,1]{1,0,3,2:T(2,128)S(1)}, f32[2,64,18,1]{1,0,3,2:T(2,128)S(1)}, u32[]{:S(2)}, u32[]{:S(2)}) collective-permute-start(f32[2,64,18,1]{1,0,3,2:T(2,128)S(1)} %copy.49), channel_id=1, source_target_pairs={{0,1},{2,3},{4,5},{6,7},{8,9},{10,11},{12,13},{14,15},{16,17},{18,... | collective-permute-start | bytes 27656 | tf_op jit(solution)/shard_map/ppermute | solution.py:20
  50.3 22.4 %collective-permute-start.5 = (f32[2,64,18,1]{1,0,3,2:T(2,128)S(1)}, f32[2,64,18,1]{1,0,3,2:T(2,128)S(1)}, u32[]{:S(2)}, u32[]{:S(2)}) collective-permute-start(f32[2,64,18,1]{1,0,3,2:T(2,128)S(1)} %copy.51), channel_id=1, source_target_pairs={{1,0},{3,2},{5,4},{7,6},{9,8},{11,10},{13,12},{15,14},{17,16},{19,... | collective-permute-start | bytes 27656 | tf_op jit(solution)/shard_map/ppermute | solution.py:23
  71.2 3.3 %copy-start.5 = (f32[2,64,1,512]{3,2,1,0:T(1,128)S(1)}, f32[2,64,1,512]{3,2,1,0:T(1,128)}, u32[]{:S(2)}) copy-start(f32[2,64,1,512]{3,2,1,0:T(1,128)} %copy-done.4) | copy-start | bytes 786436
  74.4 15.2 %copy-start.2 = (f32[2,64,16,512]{3,2,1,0:T(8,128)S(1)}, f32[2,64,16,512]{3,2,1,0:T(8,128)}, u32[]{:S(2)}) copy-start(f32[2,64,16,512]{3,2,1,0:T(8,128)} %fusion.7) | copy-start | bytes 12582916
  74.4 15.2 %copy-start.1 = (f32[2,64,16,512]{3,2,1,0:T(8,128)S(1)}, f32[2,64,16,512]{3,2,1,0:T(8,128)}, u32[]{:S(2)}) copy-start(f32[2,64,16,512]{3,2,1,0:T(8,128)} %param.8) | copy-start | bytes 12582916
  89.7 2.5 %copy-start.3 = (f32[1024,512]{1,0:T(8,128)S(1)}, f32[1024,512]{1,0:T(8,128)}, u32[]{:S(2)}) copy-start(f32[1024,512]{1,0:T(8,128)} %broadcast_multiply_fusion) | copy-start | bytes 6291460
Sparse Core Ops, SparseCore 0:
  10.7 58.8 all-reduce.1
where the time goes:
time: 103 us
  other arithmetic  33.4 us (32%)
  starting transfers between devices  19.1 us (19%)
  waiting for transfers between devices  17.9 us (17%)
  local copies, waits for them, and re-layouts  16.1 us (16%)
  between operations  13.7 us (13%)
  matrix products  2.57 us (2%)
    psum x1, waiting for transfers between devices, body(): mode_sums = lax.psum(partial_value, 'azi')  17.9 us
    sub x1, other arithmetic, body(): theta_prev + theta_next + axial_prev + axial_next + radial_prev  15.2 us
    ppermute x3, starting transfers between devices, with_halo(): lax.ppermute(lax.slice_in_dim(block, block.shape[dim] - width, None, axis...  8.62 us
    mul x1, other arithmetic, body(): upwind_term = swirl_speed[None] * (fields - theta_prev)  6.95 us
    ppermute x3, starting transfers between devices, with_halo(): lax.ppermute(lax.slice_in_dim(block, 0, width, axis=dim), axis, backward)  6.36 us
    another operation x3, other arithmetic, body(): return jnp.stack([new_energy, new_fuel], axis=0)  6.28 us
    slice x1, local copies, waits for them, and re-layouts, body(): axial_inner[:, :, :-1, :]  5.25 us
    slice x3, local copies, waits for them, and re-layouts, with_halo(): lax.slice_in_dim(block, block.shape[dim] - width, None, axis=dim)  4.75 us
  transfers between devices with their start and end apart: 8, of which 1 were waited for; matrix products, arithmetic and copies ran while one was open for 25% of the time, Pallas kernels for 0%

commit v1 on v0

v1 whole, which is shorter than its diff:
```python
import functools
import math

import jax
import jax.numpy as jnp
from jax import lax
from jax.experimental import pallas as pl
from jax.experimental.pallas import tpu as pltpu
from jax.sharding import PartitionSpec as P

TILE = 16
HEAD = 4
LANES = 128
SUB = 8
HIGH = lax.Precision.HIGHEST
VMEM = pl.BlockSpec(memory_space=pltpu.VMEM)
SMEM = pl.BlockSpec(memory_space=pltpu.SMEM)
HBM = pl.BlockSpec(memory_space=pltpu.HBM)
f32 = jnp.float32


def params(mib):
    return pltpu.CompilerParams(vmem_limit_bytes=mib << 20)


def cost(flops, size):
    return pl.CostEstimate(flops=flops, bytes_accessed=size, transcendentals=0)


def phases(length, first_cell, cell_count, mode_count):
    cells = first_cell + jnp.arange(cell_count, dtype=jnp.int32)
    order = jnp.arange(1, mode_count + 1, dtype=jnp.int32)
    angle = (order[:, None] * cells[None, :] % length).astype(f32) * (2.0 * math.pi / length)
    turned = (cells[:, None] * order[None, :] % length).astype(f32) * (2.0 * math.pi / length)
    return (
        jnp.concatenate([jnp.cos(angle), jnp.sin(angle)], axis=0),
        jnp.concatenate([jnp.cos(turned), jnp.sin(turned)], axis=1),
    )


def prepare(
    chunk, fields, phase, rate, plenum, keep, send, shift, row_top, row_out, column, local, tile, sem
):
    azi, ax, rad = lax.axis_index("azi"), lax.axis_index("ax"), lax.axis_index("rad")
    last_ax = lax.axis_size("ax") - 1
    count, cells, depth, width = fields.shape
    sectors = plenum.shape[0]
    slots = plenum.shape[1]
    pairs = sectors // 2
    parity, place = azi % 2, azi // 2
    base = pairs * chunk
    t_pair = jnp.where(parity == 0, cells - 1, 0)
    t_shift = jnp.where(parity == 0, 0, cells - 1)
    row_sent = jnp.where(ax == 0, depth - 1, 0)
    side = jnp.where(rad == 0, width - LANES, 0)
    first = pltpu.make_async_copy(fields.at[:, :, depth - 1, :], row_top, sem.at[0])
    first.start()
    copies = []
    for c in range(count):
        rows = slice(base + c * depth, base + (c + 1) * depth)
        copies.append(pltpu.make_async_copy(fields.at[c, t_pair], send.at[rows], sem.at[1 + 2 * c]))
        rows = slice(c * depth, (c + 1) * depth)
        copies.append(pltpu.make_async_copy(fields.at[c, t_shift], shift.at[rows], sem.at[2 + 2 * c]))
    edge = pltpu.make_async_copy(
        fields.at[:, :, :, pl.ds(pl.multiple_of(side, LANES), LANES)], tile, sem.at[1 + 2 * count]
    )
    for one in copies:
        one.start()
    edge.start()
    face = pltpu.make_async_copy(fields.at[:, :, row_sent, :], row_out, sem.at[2 + 2 * count])
    face.start()
    whole = pltpu.make_async_copy(fields, local, sem.at[3 + 2 * count])
    whole.start()

    @pl.when(ax == last_ax)
    def _():
        first.wait()
        sums = [
            jnp.dot(phase[...], row_top[c], precision=HIGH, preferred_element_type=f32)
            for c in range(count)
        ]
        modes = phase.shape[0]
        length = count * modes // sectors
        blocks = []
        for s in range(sectors):
            c, m = divmod(s * length, modes)
            blocks.append(sums[c][m : m + length])
        for q in range(pairs):
            even, odd = blocks[2 * q], blocks[2 * q + 1]
            at = pl.multiple_of((q ^ place) * chunk, SUB)
            keep[pl.ds(at, length)] = jnp.where(parity == 0, even, odd)
            send[pl.ds(at, length)] = jnp.where(parity == 0, odd, even)
            if chunk > length:
                rest = pl.multiple_of(at + length, SUB)
                keep[pl.ds(rest, chunk - length)] = jnp.zeros((chunk - length, width), f32)
                send[pl.ds(rest, chunk - length)] = jnp.zeros((chunk - length, width), f32)

    @pl.when(ax != last_ax)
    def _():
        first.wait()
        for q in range(pairs):
            at = pl.multiple_of((q ^ place) * chunk, SUB)
            even = rate[2 * q] * plenum[2 * q]
            odd = rate[2 * q + 1] * plenum[2 * q + 1]
            own = jnp.where(parity == 0, even, odd)
            other = jnp.where(parity == 0, odd, even)
            for p in range(2):
                rows = pl.ds(pl.multiple_of(at + p * slots, SUB), slots)
                keep[rows] = jnp.where(parity == p, own, 0.0)
                send[rows] = jnp.where(parity == p, other, 0.0)
            if chunk > 2 * slots:
                rest = pl.ds(pl.multiple_of(at + 2 * slots, SUB), chunk - 2 * slots)
                keep[rest] = jnp.zeros((chunk - 2 * slots, width), f32)
                send[rest] = jnp.zeros((chunk - 2 * slots, width), f32)

    edge.wait()
    lane = lax.broadcasted_iota(jnp.int32, (SUB, LANES), 1)
    halves = depth // SUB
    source = jnp.where(rad == 0, LANES - 1, 0)
    for g in range(column.shape[0]):
        acc = jnp.zeros((SUB, LANES), f32)
        for j in range(LANES):
            c, rest = divmod(g * LANES + j, cells * halves)
            t, h = divmod(rest, halves)
            piece = tile[c, t, h * SUB : (h + 1) * SUB, :]
            turned = pltpu.roll(piece, jnp.where(rad == 0, (j + 1) % LANES, j), 1)
            acc = jnp.where(lane == j, turned, acc)
        column[g] = acc
    for one in copies:
        one.wait()
    face.wait()
    whole.wait()


def stencil(fields, swirl, mask, tiles, near, shift, column, out):
    azi, rad = lax.axis_index("azi"), lax.axis_index("rad")
    last_rad = lax.axis_size("rad") - 1
    count, cells, depth, width = fields.shape
    base = near.shape[0] - count * depth
    parity = azi % 2
    halves = depth // SUB
    blocks = width // LANES
    lane = lax.broadcasted_iota(jnp.int32, (depth, LANES), 1)
    row = lax.broadcasted_iota(jnp.int32, (depth, LANES), 0)
    at_left, at_right = lane == 0, lane == LANES - 1
    at_low, at_high = row == 0, row == depth - 1

    def slab(t, before, after):
        tile_row = tiles[t // TILE]
        x, s, prev = [], [], []
        for c in range(count):
            parts = [fields[c, t, :, l * LANES : (l + 1) * LANES] for l in range(blocks)]
            edge_low, edge_high = [], []
            for h in range(halves):
                n = (c * cells + t) * halves + h
                g, j = n // LANES, n % LANES
                values = column[g]
                edge_low.append(pltpu.roll(values, (LANES - j) % LANES, 1))
                edge_high.append(pltpu.roll(values, LANES - 1 - j, 1))
            left_edge = jnp.where(rad > 0, jnp.concatenate(edge_low, axis=0), 0.0)
            right_edge = jnp.where(rad < last_rad, jnp.concatenate(edge_high, axis=0), 0.0)
            ups = [pltpu.roll(v, 1, 1) for v in parts]
            downs = [pltpu.roll(v, LANES - 1, 1) for v in parts]
            total, previous = [], []
            for l in range(blocks):
                left = jnp.where(at_left, ups[l - 1] if l else left_edge, ups[l])
                right = jnp.where(at_right, downs[l + 1] if l + 1 < blocks else right_edge, downs[l])
                low = jnp.where(at_low, 0.0, pltpu.roll(parts[l], 1, 0))
                high = jnp.where(at_high, 0.0, pltpu.roll(parts[l], depth - 1, 0))
                total.append((left + right) + (low + high) + after(c, l))
                previous.append(before(c, l))
            x.append(parts)
            s.append(total)
            prev.append(previous)
        for l in range(blocks):
            lanes = slice(l * LANES, (l + 1) * LANES)
            speed = swirl[t, :, lanes]
            inert = mask[t, :, lanes].astype(f32)
            energy, fuel = x[0][l], x[1][l]
            burn = tile_row * (1.0 - inert) * fuel * (1.0 + jnp.tanh(2.0 * energy - 1.0))
            stay, come = 0.4 - speed, speed + 0.1
            out[0, t, :, lanes] = energy * stay + 0.1 * s[0][l] + come * prev[0][l] + 2.0 * burn
            out[1, t, :, lanes] = fuel * stay + 0.1 * s[1][l] + come * prev[1][l] - burn

    def halo(use_near):
        def value(c, l):
            lanes = slice(l * LANES, (l + 1) * LANES)
            a = near[base + c * depth : base + (c + 1) * depth, lanes]
            b = shift[c * depth : (c + 1) * depth, lanes]
            return jnp.where(use_near, a, b)

        return value

    def inside(t):
        return lambda c, l: fields[c, t, :, l * LANES : (l + 1) * LANES]

    slab(0, halo(parity == 1), inside(1))

    def step(t, carry):
        slab(t, inside(t - 1), inside(t + 1))
        return carry

    lax.fori_loop(1, cells - 1, step, 0)
    slab(cells - 1, inside(cells - 2), halo(parity == 0))


def feed_rows(chunk, slots, targets, *refs):
    *arrived, feed = refs
    place = lax.axis_index("azi") // 2
    rows = feed.shape[0] - SUB
    feed[...] = jnp.zeros(feed.shape, f32)

    @pl.when(lax.axis_index("ax") == 0)
    def _():
        for k, block in enumerate(arrived):
            for p in range(2):
                for j in range(slots):
                    target = targets[2 * (place ^ k) + p, j]
                    at = jnp.where(target >= 0, target // HEAD * SUB + target % HEAD, rows)
                    r = p * slots + j
                    feed[pl.ds(at, 1), :] += block[r : r + 1, :]


def finish(chunk, length, axial, row_top, own, other, weights, feed, before, out, modes, high, result, sem):
    azi, ax = lax.axis_index("azi"), lax.axis_index("ax")
    last_ax = lax.axis_size("ax") - 1
    count, cells, depth, width = before.shape
    parity, place = azi % 2, azi // 2
    pairs = own.shape[0] // chunk

    @pl.when(ax == last_ax)
    def _():
        for k in range(pairs):
            for ref, p in ((own, parity), (other, 1 - parity)):
                at = pl.multiple_of((2 * (place ^ k) + p) * length, SUB)
                modes[pl.ds(at, length)] = ref[k * chunk : k * chunk + length]
        per = modes.shape[0] // count
        for c in range(count):
            rebuilt = jnp.dot(
                weights[c], modes[c * per : (c + 1) * per], precision=HIGH, preferred_element_type=f32
            )
            high[c] = 0.1 * row_top[c] - rebuilt

    @pl.when(ax != last_ax)
    def _():
        for c in range(count):
            high[c] = 0.1 * axial[c]

    scale = jnp.where(ax > 0, 0.1, 0.0)
    row = lax.broadcasted_iota(jnp.int32, (SUB, width), 0)
    group = SUB
    copies = []
    for b in range(cells // group):
        for c in range(count):
            low_rows = scale * axial[c, b * group : (b + 1) * group]
            high_rows = high[c, b * group : (b + 1) * group]
            for i in range(group):
                t = b * group + i
                head = before[c, t, :SUB] + jnp.where(row == 0, low_rows[i : i + 1], 0.0)
                if c == 1:
                    head = head + feed[t * SUB : (t + 1) * SUB]
                result[c, t, :SUB] = head
                if depth > 2 * SUB:
                    result[c, t, SUB : depth - SUB] = before[c, t, SUB : depth - SUB]
                tail = before[c, t, depth - SUB :]
                result[c, t, depth - SUB :] = tail + jnp.where(row == SUB - 1, high_rows[i : i + 1], 0.0)
            cells_at = pl.ds(b * group, group)
            copy = pltpu.make_async_copy(result.at[c, cells_at], out.at[c, cells_at], sem.at[c, b])
            copy.start()
            copies.append(copy)
    for copy in copies:
        copy.wait()


def body(fields, swirl_speed, ghost_mask, tile_flags, outlet_gain, feed_rate, plenum, feed_target):
    sectors, slabs, radials = lax.axis_size("azi"), lax.axis_size("ax"), lax.axis_size("rad")
    count, cells, depth, width = fields.shape
    half_modes = outlet_gain.shape[1]
    modes = 2 * half_modes
    slots = plenum.shape[2]
    length = count * modes // sectors
    chunk = max(length, 2 * slots)
    pairs = sectors // 2
    total_cells = cells * sectors
    phase, phase_t = phases(total_cells, lax.axis_index("azi") * cells, cells, half_modes)
    gain = jnp.concatenate([outlet_gain, outlet_gain], axis=1)
    weights = phase_t[None] * gain[:, None, :] * (0.1 * 2.0 / math.sqrt(half_modes * total_cells))
    rate = jnp.broadcast_to(feed_rate[0][:, :, None], (sectors, slots, width))
    tiles = jnp.broadcast_to(0.25 * tile_flags.astype(f32)[:, :, None], tile_flags.shape + (LANES,))
    groups = count * cells * depth // SUB // LANES

    struct = jax.ShapeDtypeStruct
    keep, send, shift, row_top, row_out, column, local = pl.pallas_call(
        functools.partial(prepare, chunk),
        out_shape=(
            struct((pairs * chunk, width), f32),
            struct((pairs * chunk + count * depth, width), f32),
            struct((count * depth, width), f32),
            struct((count, cells, width), f32),
            struct((count, cells, width), f32),
            struct((groups, SUB, LANES), f32),
            struct(fields.shape, f32),
        ),
        in_specs=[HBM, VMEM, VMEM, VMEM],
        out_specs=[VMEM] * 7,
        scratch_shapes=[
            pltpu.VMEM((count, cells, depth, LANES), f32),
            pltpu.SemaphoreType.DMA((2 * count + 4,)),
        ],
        compiler_params=params(12),
        cost_estimate=cost(1 << 26, 1 << 21),
        name="prepare",
    )(pltpu.with_memory_space_constraint(fields, pltpu.HBM), phase, rate, plenum[0])

    def swap(x, k):
        return lax.ppermute(x, "azi", [(i, i ^ k) for i in range(sectors)])

    near = swap(send, 1)
    offset = [(i, (i + 1) % sectors if i % 2 else (i - 1) % sectors) for i in range(sectors)]
    far = lax.ppermute(shift, "azi", offset)
    axial = lax.ppermute(row_out, "ax", [(0, 1), (1, 0)])
    edge = lax.ppermute(column, "rad", [(0, 1), (1, 0)])

    mixed = keep + near[: pairs * chunk]
    parts = [mixed[k * chunk : (k + 1) * chunk] for k in range(pairs)]
    arrived = [parts[0]] + [swap(parts[k], 2 * k) for k in range(1, pairs)]
    summed = functools.reduce(jnp.add, arrived)

    before = pl.pallas_call(
        stencil,
        out_shape=struct(fields.shape, f32),
        in_specs=[VMEM] * 7,
        out_specs=VMEM,
        compiler_params=params(12),
        cost_estimate=cost(1 << 28, 1 << 23),
        name="stencil",
    )(local, swirl_speed, ghost_mask, tiles, near, far, edge)

    feed = pl.pallas_call(
        functools.partial(feed_rows, chunk, slots),
        out_shape=struct((cells * SUB + SUB, width), f32),
        in_specs=[SMEM] + [VMEM] * pairs,
        out_specs=VMEM,
        compiler_params=params(8),
        cost_estimate=cost(1 << 25, 1 << 20),
        name="feed",
    )(feed_target[0], *arrived)

    gathered = jnp.concatenate([summed] + [swap(summed, 2 * k) for k in range(1, pairs)], axis=0)
    other = swap(gathered, 1)

    return pl.pallas_call(
        functools.partial(finish, chunk, length),
        out_shape=struct(fields.shape, f32),
        in_specs=[VMEM] * 7,
        out_specs=HBM,
        scratch_shapes=[
            pltpu.VMEM((count * modes, width), f32),
            pltpu.VMEM((count, cells, width), f32),
            pltpu.VMEM(fields.shape, f32),
            pltpu.SemaphoreType.DMA((count, cells // SUB)),
        ],
        compiler_params=params(16),
        cost_estimate=cost(1 << 26, 1 << 23),
        name="finish",
    )(axial, row_top, gathered, other, weights, feed, before)


def solution(mesh):
    return jax.shard_map(
        body,
        mesh=mesh,
        in_specs=(
            P(None, "azi", "ax", "rad"),
            P("azi", "ax", "rad"),
            P("azi", "ax", "rad"),
            P("azi", "ax"),
            P(),
            P("azi", None, None),
            P("azi", None, None, "rad"),
            P("azi", None, None),
        ),
        out_specs=P(None, "azi", "ax", "rad"),
        check_vma=False,
    )
```

time: 103 us -> 39.9 us (0.39)
  other arithmetic: 33.4 us -> 0.58 us
  Pallas kernels: 0 us -> 15.1 us
  local copies, waits for them, and re-layouts: 16.1 us -> 2.09 us
  between operations: 13.7 us -> 0.16 us
  waiting for transfers between devices: 17.9 us -> 6.39 us
  starting transfers between devices: 19.1 us -> 15.4 us
  matrix products: 2.57 us -> 0 us
    psum x1 -> x0, waiting for transfers between devices: 17.9 us -> none  [body(): mode_sums = lax.psum(partial_value, 'azi')]
    sub x1 -> x0, other arithmetic: 15.2 us -> none  [body(): theta_prev + theta_next + axial_prev + axial_next + radial_prev]
    pallas_call x0 -> x4, Pallas kernels: none -> 15.1 us  [the longest x1 8.84 us: body(): pl.pallas_call(stencil, out_shape=struct(fields.shape, f32), in_specs=[VM...]
    slice x5 -> x1, local copies, waits for them, and re-layouts: 10.5 us -> 0.01 us  [body(): parts = [mixed[k * chunk:(k + 1) * chunk] for k in range(pairs)]]
    mul x4 -> x2, other arithmetic: 9.25 us -> 0.01 us  [the longest x1 0.01 us: body(): phase_t[None] * gain[:, None, :]]
    ppermute x6 -> x11, waiting for transfers between devices: 0.02 us -> 6.39 us  [the longest x8 6.38 us: swap(): return lax.ppermute(x, 'azi', [(i, i ^ k) for i in range(sectors)])]
    another operation x3 -> x0, other arithmetic: 6.28 us -> none  [body(): return jnp.stack([new_energy, new_fuel], axis=0)]
    all_to_all x1 -> x0, starting transfers between devices: 4.14 us -> none  [body(): lax.all_to_all(payload, 'azi', split_axis=0, concat_axis=0, tiled=True)]
  transfers between devices with their start and end apart: 8 -> 11, of which waited for: 1 -> 5; matrix products, arithmetic and copies ran while one was open for 25% -> 1% of each run, Pallas kernels for 0% -> 25%
where the time goes in v1:
time: 39.9 us; the launch traced here: 39.7 us
  starting transfers between devices  15.4 us (39%)
  Pallas kernels  15.1 us (38%)
  waiting for transfers between devices  6.39 us (16%)
  local copies, waits for them, and re-layouts  2.09 us (5%)
  other arithmetic  0.58 us (1%)
    pallas_call x1, Pallas kernels, body(): pl.pallas_call(stencil, out_shape=struct(fields.shape, f32), in_specs=[VM...  8.84 us
    ppermute x8, starting transfers between devices, swap(): return lax.ppermute(x, 'azi', [(i, i ^ k) for i in range(sectors)])  8.08 us
    ppermute x8, waiting for transfers between devices, swap(): return lax.ppermute(x, 'azi', [(i, i ^ k) for i in range(sectors)])  6.38 us
    ppermute x1, starting transfers between devices, body(): edge = lax.ppermute(column, 'rad', [(0, 1), (1, 0)])  3.03 us
    pallas_call x1, Pallas kernels, body(): pl.pallas_call(functools.partial(prepare, chunk), out_shape=(struct((pair...  2.9 us
    ppermute x1, starting transfers between devices, body(): far = lax.ppermute(shift, 'azi', offset)  2.76 us
    pallas_call x1, Pallas kernels, body(): pl.pallas_call(functools.partial(finish, chunk, length), out_shape=struct...  2.21 us
    ppermute x1, starting transfers between devices, body(): axial = lax.ppermute(row_out, 'ax', [(0, 1), (1, 0)])  1.52 us
  transfers between devices with their start and end apart: 11, of which 5 were waited for; matrix products, arithmetic and copies ran while one was open for 1% of the time, Pallas kernels for 25%

profile of v1, /device:TPU:0, one launch (start us, length us, event | category | flops | bytes accessed | tf_op | source)
XLA Modules:
  0.0 39.7 jit_solution(6930234787093987879)
XLA Ops:
  0.0 0.0 copy-start
  0.0 0.0 copy-start.1
  0.0 0.2 fusion.9
  0.2 0.9 %broadcast_in_dim.7.rate = f32[8,8,512]{2,1,0:T(8,128)S(1)} broadcast(f32[8,8]{1,0:T(8,128)} %bitcast.5), dimensions={0,1} | broadcast | bytes 131328 | tf_op jit(solution)/shard_map/broadcast_in_dim | solution.py:288
  1.1 0.0 copy-start.2
  1.1 1.1 %copy-done.2 = f32[1,8,8,512]{3,2,1,0:T(8,128)S(1)} copy-done((f32[1,8,8,512]{3,2,1,0:T(8,128)S(1)}, f32[1,8,8,512]{3,2,1,0:T(8,128)}, u32[]{:S(2)}) %copy-start.2) | copy-done | bytes 131096
  2.2 0.0 copy-start.5
  2.2 0.0 copy-start.4
  2.2 2.9 %prepare.1 = (f32[64,512]{1,0:T(8,128)S(1)}, f32[96,512]{1,0:T(8,128)S(1)}, f32[32,512]{1,0:T(8,128)S(1)}, f32[2,64,512]{2,1,0:T(8,128)S(1)}, f32[2,64,512]{2,1,...) custom-call(f32[2,64,16,512]{3,2,1,0:T(8,128)} %fields.1, ...), custom_call_target="tpu_custom_call" | custom-call | flops 67108864 | bytes 2097152 | tf_op jit(solution)/shard_map/prepare/pallas_call | solution.py:293
  5.1 3.0 %collective-permute-start.10 = (f32[2,8,128]{2,1,0:T(8,128)S(1)}, f32[2,8,128]{2,1,0:T(8,128)S(1)}, u32[]{:S(2)}, u32[]{:S(2)}) collective-permute-start(f32[2,8,128]{2,1,0:T(8,128)S(1)} %get-tuple-element.18), channel_id=1, source_target_pairs={{0,1},{1,0},{2,3},{3,2},{4,5},{5,4},{6,7},{7,6},{8,9},{9,8},{10,11... | collective-permute-start | bytes 24584 | tf_op jit(solution)/shard_map/ppermute | solution.py:322
  8.1 2.8 %collective-permute-start.9 = (f32[32,512]{1,0:T(8,128)S(1)}, f32[32,512]{1,0:T(8,128)S(1)}, u32[]{:S(2)}, u32[]{:S(2)}) collective-permute-start(f32[32,512]{1,0:T(8,128)S(1)} %get-tuple-element.17), channel_id=1, source_target_pairs={{0,28},{4,8},{8,4},{12,16},{16,12},{20,24},{24,20},{28,0},{1,29},{... | collective-permute-start | bytes 196616 | tf_op jit(solution)/shard_map/ppermute | solution.py:320
  10.9 0.0 collective-permute-start.1
  10.9 0.2 fusion.7
  11.1 0.1 pad_maximum_fusion.2
  11.2 1.1 %collective-permute-done.1.near = f32[96,512]{1,0:T(8,128)S(1)} collective-permute-done((f32[96,512]{1,0:T(8,128)S(1)}, f32[96,512]{1,0:T(8,128)S(1)}, u32[]{:S(2)}, u32[]{:S(2)}) %collective-permute-start.1) | collective-permute-done | bytes 196640 | tf_op jit(solution)/shard_map/ppermute | solution.py:316
  12.4 0.2 collective-permute-start.2
  12.6 2.5 %collective-permute-start.4 = (f32[16,512]{1,0:T(8,128)S(1)}, f32[16,512]{1,0:T(8,128)S(1)}, u32[]{:S(2)}, u32[]{:S(2)}) collective-permute-start(f32[16,512]{1,0:T(8,128)S(1)} %get-tuple-element.22), channel_id=1, source_target_pairs={{0,24},{4,28},{8,16},{12,20},{16,8},{20,12},{24,0},{28,4},{1,25},{... | collective-permute-start | bytes 98312 | tf_op jit(solution)/shard_map/ppermute | solution.py:316
  15.0 0.9 %collective-permute-start.3 = (f32[16,512]{1,0:T(8,128)S(1)}, f32[16,512]{1,0:T(8,128)S(1)}, u32[]{:S(2)}, u32[]{:S(2)}) collective-permute-start(f32[16,512]{1,0:T(8,128)S(1)} %get-tuple-element.23), channel_id=1, source_target_pairs={{0,16},{4,20},{8,24},{12,28},{16,0},{20,4},{24,8},{28,12},{1,17},{... | collective-permute-start | bytes 98312 | tf_op jit(solution)/shard_map/ppermute | solution.py:316
  15.9 0.0 copy-done.5
  15.9 0.1 pad_maximum_fusion.3
  16.0 0.3 collective-permute-done.2.refs_1_
  16.3 1.9 %collective-permute-done.4.refs_3_ = f32[16,512]{1,0:T(8,128)S(1)} collective-permute-done((f32[16,512]{1,0:T(8,128)S(1)}, f32[16,512]{1,0:T(8,128)S(1)}, u32[]{:S(2)}, u32[]{:S(2)}) %collective-permute-start.4) | collective-permute-done | bytes 32800 | tf_op jit(solution)/shard_map/ppermute | solution.py:316
  18.3 1.6 %collective-permute-done.3.refs_2_ = f32[16,512]{1,0:T(8,128)S(1)} collective-permute-done((f32[16,512]{1,0:T(8,128)S(1)}, f32[16,512]{1,0:T(8,128)S(1)}, u32[]{:S(2)}, u32[]{:S(2)}) %collective-permute-start.3) | collective-permute-done | bytes 32800 | tf_op jit(solution)/shard_map/ppermute | solution.py:316
  19.9 1.5 %collective-permute-start.7 = (f32[16,512]{1,0:T(8,128)S(1)}, f32[16,512]{1,0:T(8,128)S(1)}, u32[]{:S(2)}, u32[]{:S(2)}) collective-permute-start(f32[16,512]{1,0:T(8,128)S(1)} %get-tuple-element.20), channel_id=1, source_target_pairs={{0,24},{4,28},{8,16},{12,20},{16,8},{20,12},{24,0},{28,4},{1,25},{... | collective-permute-start | bytes 98312 | tf_op jit(solution)/shard_map/ppermute | solution.py:316
  21.4 0.0 collective-permute-start.6
  21.4 3.0 %collective-permute-start.5 = (f32[16,512]{1,0:T(8,128)S(1)}, f32[16,512]{1,0:T(8,128)S(1)}, u32[]{:S(2)}, u32[]{:S(2)}) collective-permute-start(f32[16,512]{1,0:T(8,128)S(1)} %get-tuple-element.20), channel_id=1, source_target_pairs={{0,8},{4,12},{8,0},{12,4},{16,24},{20,28},{24,16},{28,20},{1,9},{5... | collective-permute-start | bytes 98312 | tf_op jit(solution)/shard_map/ppermute | solution.py:316
  24.3 1.4 %collective-permute-done.7 = f32[16,512]{1,0:T(8,128)S(1)} collective-permute-done((f32[16,512]{1,0:T(8,128)S(1)}, f32[16,512]{1,0:T(8,128)S(1)}, u32[]{:S(2)}, u32[]{:S(2)}) %collective-permute-start.7) | collective-permute-done | bytes 32800 | tf_op jit(solution)/shard_map/ppermute | solution.py:316
  25.7 1.5 %collective-permute-start = (f32[2,64,512]{2,1,0:T(8,128)S(1)}, f32[2,64,512]{2,1,0:T(8,128)S(1)}, u32[]{:S(2)}, u32[]{:S(2)}) collective-permute-start(f32[2,64,512]{2,1,0:T(8,128)S(1)} %get-tuple-element.12), channel_id=1, source_target_pairs={{0,2},{2,0},{1,3},{3,1},{4,6},{6,4},{5,7},{7,5},{8,10},{10,8},{9,1... | collective-permute-start | bytes 786440 | tf_op jit(solution)/shard_map/ppermute | solution.py:321
  27.2 0.0 collective-permute-done.6
  27.2 0.0 collective-permute-done.5
  27.2 0.1 collective-permute-start.8
  27.3 0.0 copy-done.4
  27.3 0.0 collective-permute-done.10.column
  27.4 0.0 collective-permute-done.9.shift
  27.4 0.1 broadcast_in_dim.8.tiles
  27.4 0.0 copy-done
  27.4 0.0 copy-done.1
  27.4 0.0 copy-start.3
  27.5 8.8 %stencil.1.before = f32[2,64,16,512]{3,2,1,0:T(8,128)S(1)} custom-call(f32[2,64,16,512]{3,2,1,0:T(8,128)S(1)} %get-tuple-element.16.fields, f32[64,16,512]{2,1,0:T(8,128)S(1)} %copy-done, s32[64,16,512]{2,1,0:T(8,128)S(1)} %copy-done.1, f32[4,16,128]{2,1,0:T(8,128)S(1)} %broadcast_in_dim.8.tiles, f32[96,512]{1,0:T(8,128)S(1)} %collective-permute-done.1.near, ...), custom_call_target="tpu_custom_call" | custom-call | flops 268435456 | bytes 8388608 | tf_op jit(solution)/shard_map/stencil/pallas_call | solution.py:329
  36.3 0.0 copy-done.3
  36.3 1.2 %feed.1 = f32[520,512]{1,0:T(8,128)S(1)} custom-call(s32[8,8]{1,0:T(8,128)S(1)} %bitcast.4, f32[16,512]{1,0:T(8,128)S(1)} %get-tuple-element.19.refs_0_, f32[16,512]{1,0:T(8,128)S(1)} %collective-permute-done.2.refs_1_, f32[16,512]{1,0:T(8,128)S(1)} %collective-permute-done.3.refs_2_, f32[16,512]{1,0:T(8,128)S(1)} %collective-permute-done.4.refs_3_), custom_call_target="tpu_custom_call" | custom-call | flops 33554432 | bytes 1048576 | tf_op jit(solution)/shard_map/feed/pallas_call | solution.py:339
  37.5 0.0 collective-permute-done.axial
  37.5 0.0 collective-permute-done.8.other
  37.5 2.2 %finish.1 = f32[2,64,16,512]{3,2,1,0:T(8,128)} custom-call(f32[2,64,512]{2,1,0:T(8,128)S(1)} %collective-permute-done.axial, f32[2,64,512]{2,1,0:T(8,128)S(1)} %get-tuple-element.13.row_top, f32[64,512]{1,0:T(8,128)S(1)} %pad_maximum_fusion.own, f32[64,512]{1,0:T(8,128)S(1)} %collective-permute-done.8.other, f32[2,64,64]{2,1,0:T(8,128)S(1)} %multiply_multiply_fusion.weights, ...), custom_call_target="tpu_custom_call" | custom-call | flops 67108864 | bytes 8388608 | tf_op jit(solution)/shard_map/finish/pallas_call | solution.py:352
  (9 shorter events, 0.1 us)
Async XLA Ops:
  0.0 27.4 %copy-start = (f32[64,16,512]{2,1,0:T(8,128)S(1)}, f32[64,16,512]{2,1,0:T(8,128)}, u32[]{:S(2)}) copy-start(f32[64,16,512]{2,1,0:T(8,128)} %swirl.1) | copy-start | bytes 6291460
  0.0 27.4 %copy-start.1 = (s32[64,16,512]{2,1,0:T(8,128)S(1)}, s32[64,16,512]{2,1,0:T(8,128)}, u32[]{:S(2)}) copy-start(s32[64,16,512]{2,1,0:T(8,128)} %mask.1) | copy-start | bytes 6291460
  1.1 1.1 %copy-start.2 = (f32[1,8,8,512]{3,2,1,0:T(8,128)S(1)}, f32[1,8,8,512]{3,2,1,0:T(8,128)}, u32[]{:S(2)}) copy-start(f32[1,8,8,512]{3,2,1,0:T(8,128)} %param.14) | copy-start | bytes 393220
  2.2 13.7 %copy-start.5 = (f32[2,32]{1,0:T(2,128)S(1)}, f32[2,32]{1,0:T(2,128)}, u32[]{:S(2)}) copy-start(f32[2,32]{1,0:T(2,128)} %param.12) | copy-start | bytes 772
  2.2 25.1 %copy-start.4 = (s32[4,16]{1,0:T(4,128)S(1)}, s32[4,16]{1,0:T(4,128)}, u32[]{:S(2)}) copy-start(s32[4,16]{1,0:T(4,128)} %param.11) | copy-start | bytes 772
  5.1 22.3 %collective-permute-start.10 = (f32[2,8,128]{2,1,0:T(8,128)S(1)}, f32[2,8,128]{2,1,0:T(8,128)S(1)}, u32[]{:S(2)}, u32[]{:S(2)}) collective-permute-start(f32[2,8,128]{2,1,0:T(8,128)S(1)} %get-tuple-element.18), channel_id=1, source_target_pairs={{0,1},{1,0},{2,3},{3,2},{4,5},{5,4},{6,7},{7,6},{8,9},{9,8},{10,11... | collective-permute-start | bytes 24584 | tf_op jit(solution)/shard_map/ppermute | solution.py:322
  8.1 19.2 %collective-permute-start.9 = (f32[32,512]{1,0:T(8,128)S(1)}, f32[32,512]{1,0:T(8,128)S(1)}, u32[]{:S(2)}, u32[]{:S(2)}) collective-permute-start(f32[32,512]{1,0:T(8,128)S(1)} %get-tuple-element.17), channel_id=1, source_target_pairs={{0,28},{4,8},{8,4},{12,16},{16,12},{20,24},{24,20},{28,0},{1,29},{... | collective-permute-start | bytes 196616 | tf_op jit(solution)/shard_map/ppermute | solution.py:320
  10.9 1.4 %collective-permute-start.1 = (f32[96,512]{1,0:T(8,128)S(1)}, f32[96,512]{1,0:T(8,128)S(1)}, u32[]{:S(2)}, u32[]{:S(2)}) collective-permute-start(f32[96,512]{1,0:T(8,128)S(1)} %get-tuple-element.15), channel_id=1, source_target_pairs={{0,4},{4,0},{8,12},{12,8},{16,20},{20,16},{24,28},{28,24},{1,5},{5... | collective-permute-start | bytes 589832 | tf_op jit(solution)/shard_map/ppermute | solution.py:316
  12.4 4.0 %collective-permute-start.2 = (f32[16,512]{1,0:T(8,128)S(1)}, f32[16,512]{1,0:T(8,128)S(1)}, u32[]{:S(2)}, u32[]{:S(2)}) collective-permute-start(f32[16,512]{1,0:T(8,128)S(1)} %get-tuple-element.21), channel_id=1, source_target_pairs={{0,8},{4,12},{8,0},{12,4},{16,24},{20,28},{24,16},{28,20},{1,9},{5... | collective-permute-start | bytes 98312 | tf_op jit(solution)/shard_map/ppermute | solution.py:316
  12.6 5.7 %collective-permute-start.4 = (f32[16,512]{1,0:T(8,128)S(1)}, f32[16,512]{1,0:T(8,128)S(1)}, u32[]{:S(2)}, u32[]{:S(2)}) collective-permute-start(f32[16,512]{1,0:T(8,128)S(1)} %get-tuple-element.22), channel_id=1, source_target_pairs={{0,24},{4,28},{8,16},{12,20},{16,8},{20,12},{24,0},{28,4},{1,25},{... | collective-permute-start | bytes 98312 | tf_op jit(solution)/shard_map/ppermute | solution.py:316
  15.0 4.8 %collective-permute-start.3 = (f32[16,512]{1,0:T(8,128)S(1)}, f32[16,512]{1,0:T(8,128)S(1)}, u32[]{:S(2)}, u32[]{:S(2)}) collective-permute-start(f32[16,512]{1,0:T(8,128)S(1)} %get-tuple-element.23), channel_id=1, source_target_pairs={{0,16},{4,20},{8,24},{12,28},{16,0},{20,4},{24,8},{28,12},{1,17},{... | collective-permute-start | bytes 98312 | tf_op jit(solution)/shard_map/ppermute | solution.py:316
  19.9 5.8 %collective-permute-start.7 = (f32[16,512]{1,0:T(8,128)S(1)}, f32[16,512]{1,0:T(8,128)S(1)}, u32[]{:S(2)}, u32[]{:S(2)}) collective-permute-start(f32[16,512]{1,0:T(8,128)S(1)} %get-tuple-element.20), channel_id=1, source_target_pairs={{0,24},{4,28},{8,16},{12,20},{16,8},{20,12},{24,0},{28,4},{1,25},{... | collective-permute-start | bytes 98312 | tf_op jit(solution)/shard_map/ppermute | solution.py:316
  21.4 5.9 %collective-permute-start.6 = (f32[16,512]{1,0:T(8,128)S(1)}, f32[16,512]{1,0:T(8,128)S(1)}, u32[]{:S(2)}, u32[]{:S(2)}) collective-permute-start(f32[16,512]{1,0:T(8,128)S(1)} %get-tuple-element.20), channel_id=1, source_target_pairs={{0,16},{4,20},{8,24},{12,28},{16,0},{20,4},{24,8},{28,12},{1,17},{... | collective-permute-start | bytes 98312 | tf_op jit(solution)/shard_map/ppermute | solution.py:316
  21.4 5.9 %collective-permute-start.5 = (f32[16,512]{1,0:T(8,128)S(1)}, f32[16,512]{1,0:T(8,128)S(1)}, u32[]{:S(2)}, u32[]{:S(2)}) collective-permute-start(f32[16,512]{1,0:T(8,128)S(1)} %get-tuple-element.20), channel_id=1, source_target_pairs={{0,8},{4,12},{8,0},{12,4},{16,24},{20,28},{24,16},{28,20},{1,9},{5... | collective-permute-start | bytes 98312 | tf_op jit(solution)/shard_map/ppermute | solution.py:316
  25.7 11.8 %collective-permute-start = (f32[2,64,512]{2,1,0:T(8,128)S(1)}, f32[2,64,512]{2,1,0:T(8,128)S(1)}, u32[]{:S(2)}, u32[]{:S(2)}) collective-permute-start(f32[2,64,512]{2,1,0:T(8,128)S(1)} %get-tuple-element.12), channel_id=1, source_target_pairs={{0,2},{2,0},{1,3},{3,1},{4,6},{6,4},{5,7},{7,5},{8,10},{10,8},{9,1... | collective-permute-start | bytes 786440 | tf_op jit(solution)/shard_map/ppermute | solution.py:321
  27.2 10.2 %collective-permute-start.8 = (f32[64,512]{1,0:T(8,128)S(1)}, f32[64,512]{1,0:T(8,128)S(1)}, u32[]{:S(2)}, u32[]{:S(2)}) collective-permute-start(f32[64,512]{1,0:T(8,128)S(1)} %pad_maximum_fusion.own), channel_id=1, source_target_pairs={{0,4},{4,0},{8,12},{12,8},{16,20},{20,16},{24,28},{28,24},{1,5},{5... | collective-permute-start | bytes 393224 | tf_op jit(solution)/shard_map/ppermute | solution.py:316
  27.4 8.9 %copy-start.3 = (s32[1,8,8]{2,1,0:T(8,128)S(1)}, s32[1,8,8]{2,1,0:T(8,128)}, u32[]{:S(2)}) copy-start(s32[1,8,8]{2,1,0:T(8,128)} %param.15) | copy-start | bytes 772

commit v2 on v1

--- a/solution.py
+++ b/solution.py
@@ -7,6 +7,7 @@
 from jax.experimental import pallas as pl
 from jax.experimental.pallas import tpu as pltpu
 from jax.sharding import PartitionSpec as P
+
 
 TILE = 16
 HEAD = 4
@@ -27,6 +28,10 @@
     return pl.CostEstimate(flops=flops, bytes_accessed=size, transcendentals=0)
 
 
+def in_hbm(x):
+    return pltpu.with_memory_space_constraint(x, pltpu.HBM)
+
+
 def phases(length, first_cell, cell_count, mode_count):
     cells = first_cell + jnp.arange(cell_count, dtype=jnp.int32)
     order = jnp.arange(1, mode_count + 1, dtype=jnp.int32)
@@ -39,20 +44,22 @@
 
 
 def prepare(
-    chunk, fields, phase, rate, plenum, keep, send, shift, row_top, row_out, column, local, tile, sem
+    chunk, fields, phase, rate, profile, keep, send, shift, row_top, row_out, column, plenum, tile, sem
 ):
     azi, ax, rad = lax.axis_index("azi"), lax.axis_index("ax"), lax.axis_index("rad")
     last_ax = lax.axis_size("ax") - 1
     count, cells, depth, width = fields.shape
-    sectors = plenum.shape[0]
-    slots = plenum.shape[1]
+    sectors, slots, _ = profile.shape
     pairs = sectors // 2
     parity, place = azi % 2, azi // 2
     base = pairs * chunk
     t_pair = jnp.where(parity == 0, cells - 1, 0)
     t_shift = jnp.where(parity == 0, 0, cells - 1)
-    row_sent = jnp.where(ax == 0, depth - 1, 0)
-    side = jnp.where(rad == 0, width - LANES, 0)
+    row_sent = jnp.where((ax == 0) & (last_ax == 1), depth - 1, 0)
+    if lax.axis_size("rad") == 2:
+        sides = [(jnp.where(rad == 0, width - LANES, 0), jnp.where(rad == 0, LANES - 1, 0))]
+    else:
+        sides = [(width - LANES, LANES - 1), (0, 0)]
     first = pltpu.make_async_copy(fields.at[:, :, depth - 1, :], row_top, sem.at[0])
     first.start()
     copies = []
@@ -61,20 +68,25 @@
         copies.append(pltpu.make_async_copy(fields.at[c, t_pair], send.at[rows], sem.at[1 + 2 * c]))
         rows = slice(c * depth, (c + 1) * depth)
         copies.append(pltpu.make_async_copy(fields.at[c, t_shift], shift.at[rows], sem.at[2 + 2 * c]))
-    edge = pltpu.make_async_copy(
-        fields.at[:, :, :, pl.ds(pl.multiple_of(side, LANES), LANES)], tile, sem.at[1 + 2 * count]
-    )
+    edges = [
+        pltpu.make_async_copy(
+            fields.at[:, :, :, pl.ds(pl.multiple_of(side, LANES), LANES)], tile.at[e], sem.at[4 + 2 * count + e]
+        )
+        for e, (side, _) in enumerate(sides)
+    ]
     for one in copies:
         one.start()
-    edge.start()
+    for edge in edges:
+        edge.start()
     face = pltpu.make_async_copy(fields.at[:, :, row_sent, :], row_out, sem.at[2 + 2 * count])
     face.start()
-    whole = pltpu.make_async_copy(fields, local, sem.at[3 + 2 * count])
-    whole.start()
+    supply = pltpu.make_async_copy(profile, plenum, sem.at[3 + 2 * count])
+    supply.start()
 
     @pl.when(ax == last_ax)
     def _():
         first.wait()
+        supply.wait()
         sums = [
             jnp.dot(phase[...], row_top[c], precision=HIGH, preferred_element_type=f32)
             for c in range(count)
@@ -87,21 +99,22 @@
             blocks.append(sums[c][m : m + length])
         for q in range(pairs):
             even, odd = blocks[2 * q], blocks[2 * q + 1]
-            at = pl.multiple_of((q ^ place) * chunk, SUB)
-            keep[pl.ds(at, length)] = jnp.where(parity == 0, even, odd)
-            send[pl.ds(at, length)] = jnp.where(parity == 0, odd, even)
+            at = q * chunk
+            keep[at : at + length] = jnp.where(parity == 0, even, odd)
+            send[at : at + length] = jnp.where(parity == 0, odd, even)
             if chunk > length:
-                rest = pl.multiple_of(at + length, SUB)
-                keep[pl.ds(rest, chunk - length)] = jnp.zeros((chunk - length, width), f32)
-                send[pl.ds(rest, chunk - length)] = jnp.zeros((chunk - length, width), f32)
+                keep[at + length : at + chunk] = jnp.zeros((chunk - length, width), f32)
+                send[at + length : at + chunk] = jnp.zeros((chunk - length, width), f32)
 
     @pl.when(ax != last_ax)
     def _():
         first.wait()
+        supply.wait()
+        turned = rate[...].T
         for q in range(pairs):
             at = pl.multiple_of((q ^ place) * chunk, SUB)
-            even = rate[2 * q] * plenum[2 * q]
-            odd = rate[2 * q + 1] * plenum[2 * q + 1]
+            even = turned[:, 2 * q : 2 * q + 1] * plenum[2 * q]
+            odd = turned[:, 2 * q + 1 : 2 * q + 2] * plenum[2 * q + 1]
             own = jnp.where(parity == 0, even, odd)
             other = jnp.where(parity == 0, odd, even)
             for p in range(2):
@@ -113,26 +126,24 @@
                 keep[rest] = jnp.zeros((chunk - 2 * slots, width), f32)
                 send[rest] = jnp.zeros((chunk - 2 * slots, width), f32)
 
-    edge.wait()
     lane = lax.broadcasted_iota(jnp.int32, (SUB, LANES), 1)
     halves = depth // SUB
-    source = jnp.where(rad == 0, LANES - 1, 0)
-    for g in range(column.shape[0]):
-        acc = jnp.zeros((SUB, LANES), f32)
-        for j in range(LANES):
-            c, rest = divmod(g * LANES + j, cells * halves)
-            t, h = divmod(rest, halves)
-            piece = tile[c, t, h * SUB : (h + 1) * SUB, :]
-            turned = pltpu.roll(piece, jnp.where(rad == 0, (j + 1) % LANES, j), 1)
-            acc = jnp.where(lane == j, turned, acc)
-        column[g] = acc
+    for e, (_, source) in enumerate(sides):
+        edges[e].wait()
+        for g in range(column.shape[1]):
+            acc = jnp.zeros((SUB, LANES), f32)
+            for j in range(LANES):
+                c, rest = divmod(g * LANES + j, cells * halves)
+                t, h = divmod(rest, halves)
+                piece = tile[e, c, t, h * SUB : (h + 1) * SUB, :]
+                acc = jnp.where(lane == j, pltpu.roll(piece, (j - source) % LANES, 1), acc)
+            column[e, g] = acc
     for one in copies:
         one.wait()
     face.wait()
-    whole.wait()
-
-
-def stencil(fields, swirl, mask, tiles, near, shift, column, out):
+
+
+def stencil(fields, swirl, mask, tiles, near, shift, column_low, column_high, out):
     azi, rad = lax.axis_index("azi"), lax.axis_index("rad")
     last_rad = lax.axis_size("rad") - 1
     count, cells, depth, width = fields.shape
@@ -154,9 +165,8 @@
             for h in range(halves):
                 n = (c * cells + t) * halves + h
                 g, j = n // LANES, n % LANES
-                values = column[g]
-                edge_low.append(pltpu.roll(values, (LANES - j) % LANES, 1))
-                edge_high.append(pltpu.roll(values, LANES - 1 - j, 1))
+                edge_low.append(pltpu.roll(column_low[g], (LANES - j) % LANES, 1))
+                edge_high.append(pltpu.roll(column_high[g], LANES - 1 - j, 1))
             left_edge = jnp.where(rad > 0, jnp.concatenate(edge_low, axis=0), 0.0)
             right_edge = jnp.where(rad < last_rad, jnp.concatenate(edge_high, axis=0), 0.0)
             ups = [pltpu.roll(v, 1, 1) for v in parts]
@@ -204,7 +214,7 @@
     slab(cells - 1, inside(cells - 2), halo(parity == 0))
 
 
-def feed_rows(chunk, slots, targets, *refs):
+def feed_rows(slots, targets, *refs):
     *arrived, feed = refs
     place = lax.axis_index("azi") // 2
     rows = feed.shape[0] - SUB
@@ -221,18 +231,18 @@
                     feed[pl.ds(at, 1), :] += block[r : r + 1, :]
 
 
-def finish(chunk, length, axial, row_top, own, other, weights, feed, before, out, modes, high, result, sem):
+def finish(chunk, length, axial_low, axial_high, row_top, own, other, weights, feed, before, out, modes, high, result, sem):
     azi, ax = lax.axis_index("azi"), lax.axis_index("ax")
     last_ax = lax.axis_size("ax") - 1
     count, cells, depth, width = before.shape
-    parity, place = azi % 2, azi // 2
+    parity = azi % 2
     pairs = own.shape[0] // chunk
 
     @pl.when(ax == last_ax)
     def _():
         for k in range(pairs):
             for ref, p in ((own, parity), (other, 1 - parity)):
-                at = pl.multiple_of((2 * (place ^ k) + p) * length, SUB)
+                at = pl.multiple_of((2 * k + p) * length, SUB)
                 modes[pl.ds(at, length)] = ref[k * chunk : k * chunk + length]
         per = modes.shape[0] // count
         for c in range(count):
@@ -244,7 +254,7 @@
     @pl.when(ax != last_ax)
     def _():
         for c in range(count):
-            high[c] = 0.1 * axial[c]
+            high[c] = 0.1 * axial_high[c]
 
     scale = jnp.where(ax > 0, 0.1, 0.0)
     row = lax.broadcasted_iota(jnp.int32, (SUB, width), 0)
@@ -252,7 +262,7 @@
     copies = []
     for b in range(cells // group):
         for c in range(count):
-            low_rows = scale * axial[c, b * group : (b + 1) * group]
+            low_rows = scale * axial_low[c, b * group : (b + 1) * group]
             high_rows = high[c, b * group : (b + 1) * group]
             for i in range(group):
                 t = b * group + i
@@ -273,7 +283,7 @@
 
 
 def body(fields, swirl_speed, ghost_mask, tile_flags, outlet_gain, feed_rate, plenum, feed_target):
-    sectors, slabs, radials = lax.axis_size("azi"), lax.axis_size("ax"), lax.axis_size("rad")
+    sectors, radials = lax.axis_size("azi"), lax.axis_size("rad")
     count, cells, depth, width = fields.shape
     half_modes = outlet_gain.shape[1]
     modes = 2 * half_modes
@@ -285,12 +295,11 @@
     phase, phase_t = phases(total_cells, lax.axis_index("azi") * cells, cells, half_modes)
     gain = jnp.concatenate([outlet_gain, outlet_gain], axis=1)
     weights = phase_t[None] * gain[:, None, :] * (0.1 * 2.0 / math.sqrt(half_modes * total_cells))
-    rate = jnp.broadcast_to(feed_rate[0][:, :, None], (sectors, slots, width))
     tiles = jnp.broadcast_to(0.25 * tile_flags.astype(f32)[:, :, None], tile_flags.shape + (LANES,))
     groups = count * cells * depth // SUB // LANES
 
     struct = jax.ShapeDtypeStruct
-    keep, send, shift, row_top, row_out, column, local = pl.pallas_call(
+    keep, send, shift, row_top, row_out, column = pl.pallas_call(
         functools.partial(prepare, chunk),
         out_shape=(
             struct((pairs * chunk, width), f32),
@@ -298,46 +307,58 @@
             struct((count * depth, width), f32),
             struct((count, cells, width), f32),
             struct((count, cells, width), f32),
-            struct((groups, SUB, LANES), f32),
-            struct(fields.shape, f32),
+            struct((1 if radials == 2 else 2, groups, SUB, LANES), f32),
         ),
-        in_specs=[HBM, VMEM, VMEM, VMEM],
-        out_specs=[VMEM] * 7,
+        in_specs=[HBM, VMEM, VMEM, HBM],
+        out_specs=[VMEM] * 6,
         scratch_shapes=[
-            pltpu.VMEM((count, cells, depth, LANES), f32),
-            pltpu.SemaphoreType.DMA((2 * count + 4,)),
+            pltpu.VMEM((sectors, slots, width), f32),
+            pltpu.VMEM((1 if radials == 2 else 2, count, cells, depth, LANES), f32),
+            pltpu.SemaphoreType.DMA((2 * count + 6,)),
         ],
         compiler_params=params(12),
         cost_estimate=cost(1 << 26, 1 << 21),
         name="prepare",
-    )(pltpu.with_memory_space_constraint(fields, pltpu.HBM), phase, rate, plenum[0])
+    )(in_hbm(fields), phase, feed_rate[0], in_hbm(plenum[0]))
 
     def swap(x, k):
         return lax.ppermute(x, "azi", [(i, i ^ k) for i in range(sectors)])
 
+    def across(axis, to_high, to_low, to_only):
+        size = lax.axis_size(axis)
+        if size == 2:
+            received = lax.ppermute(to_only, axis, [(0, 1), (1, 0)])
+            return received, received
+        ups = [(i, i + 1) for i in range(size - 1)]
+        return lax.ppermute(to_high, axis, ups), lax.ppermute(to_low, axis, [(b, a) for a, b in ups])
+
+    offset = [(i, (i + 1) % sectors if i % 2 else (i - 1) % sectors) for i in range(sectors)]
     near = swap(send, 1)
-    offset = [(i, (i + 1) % sectors if i % 2 else (i - 1) % sectors) for i in range(sectors)]
     far = lax.ppermute(shift, "azi", offset)
-    axial = lax.ppermute(row_out, "ax", [(0, 1), (1, 0)])
-    edge = lax.ppermute(column, "rad", [(0, 1), (1, 0)])
+    axial_low, axial_high = across("ax", row_top, row_out, row_out)
+    edge_low, edge_high = across("rad", column[0], column[-1], column[0])
 
     mixed = keep + near[: pairs * chunk]
     parts = [mixed[k * chunk : (k + 1) * chunk] for k in range(pairs)]
-    arrived = [parts[0]] + [swap(parts[k], 2 * k) for k in range(1, pairs)]
-    summed = functools.reduce(jnp.add, arrived)
+    arrived = [mixed]
+    for k in range(1, pairs):
+        arrived.append(swap(jnp.concatenate(parts[k:] + parts[:k], axis=0), 2 * k))
+    summed = functools.reduce(
+        jnp.add, [mixed] + [jnp.concatenate([x[(pairs - k) * chunk :], x[: (pairs - k) * chunk]], axis=0) for k, x in enumerate(arrived) if k]
+    )
 
     before = pl.pallas_call(
         stencil,
         out_shape=struct(fields.shape, f32),
-        in_specs=[VMEM] * 7,
+        in_specs=[VMEM] * 8,
         out_specs=VMEM,
         compiler_params=params(12),
         cost_estimate=cost(1 << 28, 1 << 23),
         name="stencil",
-    )(local, swirl_speed, ghost_mask, tiles, near, far, edge)
+    )(fields, swirl_speed, ghost_mask, tiles, near, far, edge_low, edge_high)
 
     feed = pl.pallas_call(
-        functools.partial(feed_rows, chunk, slots),
+        functools.partial(feed_rows, slots),
         out_shape=struct((cells * SUB + SUB, width), f32),
         in_specs=[SMEM] + [VMEM] * pairs,
         out_specs=VMEM,
@@ -346,13 +367,12 @@
         name="feed",
     )(feed_target[0], *arrived)
 
-    gathered = jnp.concatenate([summed] + [swap(summed, 2 * k) for k in range(1, pairs)], axis=0)
-    other = swap(gathered, 1)
+    other = swap(summed, 1)
 
     return pl.pallas_call(
         functools.partial(finish, chunk, length),
         out_shape=struct(fields.shape, f32),
-        in_specs=[VMEM] * 7,
+        in_specs=[VMEM] * 8,
         out_specs=HBM,
         scratch_shapes=[
             pltpu.VMEM((count * modes, width), f32),
@@ -363,7 +383,7 @@
         compiler_params=params(16),
         cost_estimate=cost(1 << 26, 1 << 23),
         name="finish",
-    )(axial, row_top, gathered, other, weights, feed, before)
+    )(axial_low, axial_high, row_top, summed, other, weights, feed, before)
 
 
 def solution(mesh):

time: 39.9 us -> 39.9 us (level)
  starting transfers between devices: 15.4 us -> 12.2 us
  waiting for transfers between devices: 6.39 us -> 8.1 us
  other arithmetic: 0.58 us -> 1.38 us
  local copies, waits for them, and re-layouts: 2.09 us -> 2.58 us
    ppermute x8 -> x5, starting transfers between devices: 8.08 us -> 4.66 us  [swap(): return lax.ppermute(x, 'azi', [(i, i ^ k) for i in range(sectors)])]
    ppermute x8 -> x5, waiting for transfers between devices: 6.38 us -> 8.09 us  [swap(): return lax.ppermute(x, 'azi', [(i, i ^ k) for i in range(sectors)])]
    unnamed x12, local copies, waits for them, and re-layouts: 1.1 us -> 2.44 us
    broadcast_in_dim x1 -> x0, local copies, waits for them, and re-layouts: 0.91 us -> none  [body(): rate = jnp.broadcast_to(feed_rate[0][:, :, None], (sectors, slots, width))]
    concatenate x1, other arithmetic: 0.07 us -> 0.83 us  [body(): gain = jnp.concatenate([outlet_gain, outlet_gain], axis=1)]
  transfers between devices with their start and end apart: 11 -> 8, of which waited for: 5 -> 2; matrix products, arithmetic and copies ran while one was open for 1% -> 3% of each run, Pallas kernels for 25% -> 26%
where the time goes in v2:
time: 39.9 us; the launch traced here: 39.7 us
  Pallas kernels  15.2 us (38%)
  starting transfers between devices  12.2 us (31%)
  waiting for transfers between devices  8.1 us (20%)
  local copies, waits for them, and re-layouts  2.58 us (6%)
  other arithmetic  1.38 us (3%)
    pallas_call x1, Pallas kernels, body(): pl.pallas_call(stencil, out_shape=struct(fields.shape, f32), in_specs=[VM...  9.01 us
    ppermute x5, waiting for transfers between devices, swap(): return lax.ppermute(x, 'azi', [(i, i ^ k) for i in range(sectors)])  8.09 us
    ppermute x2, starting transfers between devices, across(): received = lax.ppermute(to_only, axis, [(0, 1), (1, 0)])  4.77 us
    ppermute x5, starting transfers between devices, swap(): return lax.ppermute(x, 'azi', [(i, i ^ k) for i in range(sectors)])  4.66 us
    pallas_call x1, Pallas kernels, body(): pl.pallas_call(functools.partial(prepare, chunk), out_shape=(struct((pair...  2.84 us
    ppermute x1, starting transfers between devices, body(): far = lax.ppermute(shift, 'azi', offset)  2.76 us
    unnamed x12, local copies, waits for them, and re-layouts  2.44 us
    pallas_call x1, Pallas kernels, body(): pl.pallas_call(functools.partial(finish, chunk, length), out_shape=struct...  2.21 us
  transfers between devices with their start and end apart: 8, of which 2 were waited for; matrix products, arithmetic and copies ran while one was open for 3% of the time, Pallas kernels for 26%

profile of v2, /device:TPU:0, one launch (start us, length us, event | category | flops | bytes accessed | tf_op | source)
XLA Modules:
  0.0 39.7 jit_solution(12782407254104828598)
XLA Ops:
  0.0 0.0 copy-start.1
  0.0 0.0 copy-start
  0.0 0.2 fusion.11
  0.2 0.0 copy-start.3
  0.2 0.8 %copy-done.3 = f32[1,8,8]{2,1,0:T(8,128)S(1)} copy-done((f32[1,8,8]{2,1,0:T(8,128)S(1)}, f32[1,8,8]{2,1,0:T(8,128)}, u32[]{:S(2)}) %copy-start.3) | copy-done | bytes 280
  1.0 0.0 copy-start.5
  1.0 2.8 %prepare.1 = (f32[64,512]{1,0:T(8,128)S(1)}, f32[96,512]{1,0:T(8,128)S(1)}, f32[32,512]{1,0:T(8,128)S(1)}, f32[2,64,512]{2,1,0:T(8,128)S(1)}, f32[2,64,512]{2,1,0:T(8,128)S(1)}, /*index=5*/f32[1,2,8,128]{3,2,1,0:T(8,128)S(1)}) custom-call(f32[2,64,16,512]{3,2,1,0:T(8,128)} %fields.3, f32[64,64]{1,0:T(8,128)S(1)} %pad_maximum_fusion.3.phase, ...), custom_call_target="tpu_custom_call" | custom-call | flops 67108864 | bytes 2097152 | tf_op jit(solution)/shard_map/prepare/pallas_call | solution.py:302
  3.9 3.1 %collective-permute-start.7 = (f32[2,8,128]{2,1,0:T(8,128)S(1)}, f32[2,8,128]{2,1,0:T(8,128)S(1)}, u32[]{:S(2)}, u32[]{:S(2)}) collective-permute-start(f32[2,8,128]{2,1,0:T(8,128)S(1)} %bitcast.6), channel_id=1, source_target_pairs={{0,1},{1,0},{2,3},{3,2},{4,5},{5,4},{6,7},{7,6},{8,9},{9,8},{10,11... | collective-permute-start | bytes 24584 | tf_op jit(solution)/shard_map/ppermute | solution.py:330
  6.9 2.8 %collective-permute-start.6 = (f32[32,512]{1,0:T(8,128)S(1)}, f32[32,512]{1,0:T(8,128)S(1)}, u32[]{:S(2)}, u32[]{:S(2)}) collective-permute-start(f32[32,512]{1,0:T(8,128)S(1)} %get-tuple-element.15), channel_id=1, source_target_pairs={{0,28},{4,8},{8,4},{12,16},{16,12},{20,24},{24,20},{28,0},{1,29},{... | collective-permute-start | bytes 196616 | tf_op jit(solution)/shard_map/ppermute | solution.py:337
  9.7 0.0 collective-permute-start.1
  9.7 0.2 fusion.9
  9.9 0.8 %pad_maximum_fusion.5 = f32[2,64]{1,0:T(2,128)S(1)} fusion(f32[2,32]{1,0:T(2,128)} %param.12), kind=kLoop, calls=%fused_computation.31 | loop fusion | flops 128 | bytes 768 | tf_op jit(solution)/shard_map/concatenate | solution.py:296
  10.7 0.1 pad_maximum_fusion.4
  10.8 0.3 collective-permute-done.1.near
  11.2 1.3 %collective-permute-start.3 = (f32[64,512]{1,0:T(8,128)S(1)}, f32[64,512]{1,0:T(8,128)S(1)}, u32[]{:S(2)}, u32[]{:S(2)}) collective-permute-start(f32[64,512]{1,0:T(8,128)S(1)} %pad_maximum_fusion.1), channel_id=1, source_target_pairs={{0,16},{4,20},{8,24},{12,28},{16,0},{20,4},{24,8},{28,12},{1,17},{... | collective-permute-start | bytes 393224 | tf_op jit(solution)/shard_map/ppermute | solution.py:325
  12.5 0.3 collective-permute-start.2
  12.8 3.0 %collective-permute-start.4 = (f32[64,512]{1,0:T(8,128)S(1)}, f32[64,512]{1,0:T(8,128)S(1)}, u32[]{:S(2)}, u32[]{:S(2)}) collective-permute-start(f32[64,512]{1,0:T(8,128)S(1)} %pad_maximum_fusion.2), channel_id=1, source_target_pairs={{0,24},{4,28},{8,16},{12,20},{16,8},{20,12},{24,0},{28,4},{1,25},{... | collective-permute-start | bytes 393224 | tf_op jit(solution)/shard_map/ppermute | solution.py:325
  15.8 7.8 %collective-permute-done.2.refs_1_ = f32[64,512]{1,0:T(8,128)S(1)} collective-permute-done((f32[64,512]{1,0:T(8,128)S(1)}, f32[64,512]{1,0:T(8,128)S(1)}, u32[]{:S(2)}, u32[]{:S(2)}) %collective-permute-start.2) | collective-permute-done | bytes 131104 | tf_op jit(solution)/shard_map/ppermute | solution.py:325
  23.6 1.7 %collective-permute-start = (f32[2,64,512]{2,1,0:T(8,128)S(1)}, f32[2,64,512]{2,1,0:T(8,128)S(1)}, u32[]{:S(2)}, u32[]{:S(2)}) collective-permute-start(f32[2,64,512]{2,1,0:T(8,128)S(1)} %get-tuple-element.11), channel_id=1, source_target_pairs={{0,2},{2,0},{1,3},{3,1},{4,6},{6,4},{5,7},{7,5},{8,10},{10,8},{9,1... | collective-permute-start | bytes 786440 | tf_op jit(solution)/shard_map/ppermute | solution.py:330
  25.3 0.0 collective-permute-done.4.refs_3_
  25.4 0.0 collective-permute-done.3.refs_2_
  25.5 0.1 collective-permute-start.5
  25.5 0.0 copy-done.5
  25.6 0.0 collective-permute-done.7.column_low.column_high
  25.6 0.0 collective-permute-done.6.shift
  25.6 0.1 broadcast_in_dim.2.tiles
  25.7 0.0 copy-done.1
  25.7 0.0 copy-done
  25.7 0.0 copy-start.2
  25.7 1.6 %copy-done.2 = s32[64,16,512]{2,1,0:T(8,128)S(1)} copy-done((s32[64,16,512]{2,1,0:T(8,128)S(1)}, s32[64,16,512]{2,1,0:T(8,128)}, u32[]{:S(2)}) %copy-start.2) | copy-done | bytes 2097176
  27.3 0.0 copy-start.4
  27.3 9.0 %stencil.1.before = f32[2,64,16,512]{3,2,1,0:T(8,128)S(1)} custom-call(f32[2,64,16,512]{3,2,1,0:T(8,128)S(1)} %copy-done, f32[64,16,512]{2,1,0:T(8,128)S(1)} %copy-done.1, s32[64,16,512]{2,1,0:T(8,128)S(1)} %copy-done.2, f32[4,16,128]{2,1,0:T(8,128)S(1)} %broadcast_in_dim.2.tiles, f32[96,512]{1,0:T(8,128)S(1)} %collective-permute-done.1.near, ...), custom_call_target="tpu_custom_call" | custom-call | flops 268435456 | bytes 8388608 | tf_op jit(solution)/shard_map/stencil/pallas_call | solution.py:350
  36.3 0.0 copy-done.4
  36.3 1.2 %feed.1 = f32[520,512]{1,0:T(8,128)S(1)} custom-call(s32[8,8]{1,0:T(8,128)S(1)} %bitcast.5, f32[64,512]{1,0:T(8,128)S(1)} %slice_add_fusion.refs_0_, f32[64,512]{1,0:T(8,128)S(1)} %collective-permute-done.2.refs_1_, f32[64,512]{1,0:T(8,128)S(1)} %collective-permute-done.3.refs_2_, f32[64,512]{1,0:T(8,128)S(1)} %collective-permute-done.4.refs_3_), custom_call_target="tpu_custom_call" | custom-call | flops 33554432 | bytes 1048576 | tf_op jit(solution)/shard_map/feed/pallas_call | solution.py:360
  37.4 0.0 collective-permute-done.axial_low.axial_high
  37.5 0.0 collective-permute-done.5.other
  37.5 2.2 %finish.1 = f32[2,64,16,512]{3,2,1,0:T(8,128)} custom-call(f32[2,64,512]{2,1,0:T(8,128)S(1)} %collective-permute-done.axial_low.axial_high, f32[2,64,512]{2,1,0:T(8,128)S(1)} %collective-permute-done.axial_low.axial_high, f32[2,64,512]{2,1,0:T(8,128)S(1)} %get-tuple-element.12.row_top, f32[64,512]{1,0:T(8,128)S(1)} %fusion.1.own, ...), custom_call_target="tpu_custom_call" | custom-call | flops 67108864 | bytes 8388608 | tf_op jit(solution)/shard_map/finish/pallas_call | solution.py:372
  (18 shorter events, 0.2 us)
Async XLA Ops:
  0.0 25.7 %copy-start.1 = (f32[64,16,512]{2,1,0:T(8,128)S(1)}, f32[64,16,512]{2,1,0:T(8,128)}, u32[]{:S(2)}) copy-start(f32[64,16,512]{2,1,0:T(8,128)} %swirl.1) | copy-start | bytes 6291460
  0.0 25.7 %copy-start = (f32[2,64,16,512]{3,2,1,0:T(8,128)S(1)}, f32[2,64,16,512]{3,2,1,0:T(8,128)}, u32[]{:S(2)}) copy-start(f32[2,64,16,512]{3,2,1,0:T(8,128)} %fields.3) | copy-start | bytes 12582916
  0.2 0.8 %copy-start.3 = (f32[1,8,8]{2,1,0:T(8,128)S(1)}, f32[1,8,8]{2,1,0:T(8,128)}, u32[]{:S(2)}) copy-start(f32[1,8,8]{2,1,0:T(8,128)} %param.13) | copy-start | bytes 772
  1.0 24.5 %copy-start.5 = (s32[4,16]{1,0:T(4,128)S(1)}, s32[4,16]{1,0:T(4,128)}, u32[]{:S(2)}) copy-start(s32[4,16]{1,0:T(4,128)} %param.11) | copy-start | bytes 772
  3.9 21.7 %collective-permute-start.7 = (f32[2,8,128]{2,1,0:T(8,128)S(1)}, f32[2,8,128]{2,1,0:T(8,128)S(1)}, u32[]{:S(2)}, u32[]{:S(2)}) collective-permute-start(f32[2,8,128]{2,1,0:T(8,128)S(1)} %bitcast.6), channel_id=1, source_target_pairs={{0,1},{1,0},{2,3},{3,2},{4,5},{5,4},{6,7},{7,6},{8,9},{9,8},{10,11... | collective-permute-start | bytes 24584 | tf_op jit(solution)/shard_map/ppermute | solution.py:330
  6.9 18.7 %collective-permute-start.6 = (f32[32,512]{1,0:T(8,128)S(1)}, f32[32,512]{1,0:T(8,128)S(1)}, u32[]{:S(2)}, u32[]{:S(2)}) collective-permute-start(f32[32,512]{1,0:T(8,128)S(1)} %get-tuple-element.15), channel_id=1, source_target_pairs={{0,28},{4,8},{8,4},{12,16},{16,12},{20,24},{24,20},{28,0},{1,29},{... | collective-permute-start | bytes 196616 | tf_op jit(solution)/shard_map/ppermute | solution.py:337
  9.7 1.4 %collective-permute-start.1 = (f32[96,512]{1,0:T(8,128)S(1)}, f32[96,512]{1,0:T(8,128)S(1)}, u32[]{:S(2)}, u32[]{:S(2)}) collective-permute-start(f32[96,512]{1,0:T(8,128)S(1)} %get-tuple-element.14), channel_id=1, source_target_pairs={{0,4},{4,0},{8,12},{12,8},{16,20},{20,16},{24,28},{28,24},{1,5},{5... | collective-permute-start | bytes 589832 | tf_op jit(solution)/shard_map/ppermute | solution.py:325
  11.2 14.2 %collective-permute-start.3 = (f32[64,512]{1,0:T(8,128)S(1)}, f32[64,512]{1,0:T(8,128)S(1)}, u32[]{:S(2)}, u32[]{:S(2)}) collective-permute-start(f32[64,512]{1,0:T(8,128)S(1)} %pad_maximum_fusion.1), channel_id=1, source_target_pairs={{0,16},{4,20},{8,24},{12,28},{16,0},{20,4},{24,8},{28,12},{1,17},{... | collective-permute-start | bytes 393224 | tf_op jit(solution)/shard_map/ppermute | solution.py:325
  12.5 11.1 %collective-permute-start.2 = (f32[64,512]{1,0:T(8,128)S(1)}, f32[64,512]{1,0:T(8,128)S(1)}, u32[]{:S(2)}, u32[]{:S(2)}) collective-permute-start(f32[64,512]{1,0:T(8,128)S(1)} %pad_maximum_fusion), channel_id=1, source_target_pairs={{0,8},{4,12},{8,0},{12,4},{16,24},{20,28},{24,16},{28,20},{1,9},{5... | collective-permute-start | bytes 393224 | tf_op jit(solution)/shard_map/ppermute | solution.py:325
  12.8 12.5 %collective-permute-start.4 = (f32[64,512]{1,0:T(8,128)S(1)}, f32[64,512]{1,0:T(8,128)S(1)}, u32[]{:S(2)}, u32[]{:S(2)}) collective-permute-start(f32[64,512]{1,0:T(8,128)S(1)} %pad_maximum_fusion.2), channel_id=1, source_target_pairs={{0,24},{4,28},{8,16},{12,20},{16,8},{20,12},{24,0},{28,4},{1,25},{... | collective-permute-start | bytes 393224 | tf_op jit(solution)/shard_map/ppermute | solution.py:325
  23.6 13.8 %collective-permute-start = (f32[2,64,512]{2,1,0:T(8,128)S(1)}, f32[2,64,512]{2,1,0:T(8,128)S(1)}, u32[]{:S(2)}, u32[]{:S(2)}) collective-permute-start(f32[2,64,512]{2,1,0:T(8,128)S(1)} %get-tuple-element.11), channel_id=1, source_target_pairs={{0,2},{2,0},{1,3},{3,1},{4,6},{6,4},{5,7},{7,5},{8,10},{10,8},{9,1... | collective-permute-start | bytes 786440 | tf_op jit(solution)/shard_map/ppermute | solution.py:330
  25.5 12.0 %collective-permute-start.5 = (f32[64,512]{1,0:T(8,128)S(1)}, f32[64,512]{1,0:T(8,128)S(1)}, u32[]{:S(2)}, u32[]{:S(2)}) collective-permute-start(f32[64,512]{1,0:T(8,128)S(1)} %fusion.1.own), channel_id=1, source_target_pairs={{0,4},{4,0},{8,12},{12,8},{16,20},{20,16},{24,28},{28,24},{1,5},{5... | collective-permute-start | bytes 393224 | tf_op jit(solution)/shard_map/ppermute | solution.py:325
  25.7 1.6 %copy-start.2 = (s32[64,16,512]{2,1,0:T(8,128)S(1)}, s32[64,16,512]{2,1,0:T(8,128)}, u32[]{:S(2)}) copy-start(s32[64,16,512]{2,1,0:T(8,128)} %mask.1) | copy-start | bytes 6291460
  27.3 9.0 %copy-start.4 = (s32[1,8,8]{2,1,0:T(8,128)S(1)}, s32[1,8,8]{2,1,0:T(8,128)}, u32[]{:S(2)}) copy-start(s32[1,8,8]{2,1,0:T(8,128)} %param.15) | copy-start | bytes 772

commit v3 on v2

--- a/solution.py
+++ b/solution.py
@@ -12,6 +12,7 @@
 TILE = 16
 HEAD = 4
 LANES = 128
+UNROLL = 4
 SUB = 8
 HIGH = lax.Precision.HIGHEST
 VMEM = pl.BlockSpec(memory_space=pltpu.VMEM)
@@ -44,7 +45,7 @@
 
 
 def prepare(
-    chunk, fields, phase, rate, profile, keep, send, shift, row_top, row_out, column, plenum, tile, sem
+    chunk, fields, phase, rates, profile, keep, send, shift, row_top, row_out, column, local, rate, plenum, tile, sem
 ):
     azi, ax, rad = lax.axis_index("azi"), lax.axis_index("ax"), lax.axis_index("rad")
     last_ax = lax.axis_size("ax") - 1
@@ -57,9 +58,10 @@
     t_shift = jnp.where(parity == 0, 0, cells - 1)
     row_sent = jnp.where((ax == 0) & (last_ax == 1), depth - 1, 0)
     if lax.axis_size("rad") == 2:
-        sides = [(jnp.where(rad == 0, width - LANES, 0), jnp.where(rad == 0, LANES - 1, 0))]
+        more = jnp.where(rad == 0, 1, 0)
+        sides = [(jnp.where(rad == 0, width - LANES, 0), lambda j: (j + more) if j < LANES - 1 else j * (1 - more))]
     else:
-        sides = [(width - LANES, LANES - 1), (0, 0)]
+        sides = [(width - LANES, lambda j: (j + 1) % LANES), (0, lambda j: j)]
     first = pltpu.make_async_copy(fields.at[:, :, depth - 1, :], row_top, sem.at[0])
     first.start()
     copies = []
@@ -70,7 +72,7 @@
         copies.append(pltpu.make_async_copy(fields.at[c, t_shift], shift.at[rows], sem.at[2 + 2 * c]))
     edges = [
         pltpu.make_async_copy(
-            fields.at[:, :, :, pl.ds(pl.multiple_of(side, LANES), LANES)], tile.at[e], sem.at[4 + 2 * count + e]
+            fields.at[:, :, :, pl.ds(pl.multiple_of(side, LANES), LANES)], tile.at[e], sem.at[6 + 2 * count + e]
         )
         for e, (side, _) in enumerate(sides)
     ]
@@ -82,11 +84,16 @@
     face.start()
     supply = pltpu.make_async_copy(profile, plenum, sem.at[3 + 2 * count])
     supply.start()
+    factor = pltpu.make_async_copy(rates, rate, sem.at[4 + 2 * count])
+    factor.start()
+    whole = pltpu.make_async_copy(fields, local, sem.at[5 + 2 * count])
+    whole.start()
 
     @pl.when(ax == last_ax)
     def _():
         first.wait()
         supply.wait()
+        factor.wait()
         sums = [
             jnp.dot(phase[...], row_top[c], precision=HIGH, preferred_element_type=f32)
             for c in range(count)
@@ -110,6 +117,7 @@
     def _():
         first.wait()
         supply.wait()
+        factor.wait()
         turned = rate[...].T
         for q in range(pairs):
             at = pl.multiple_of((q ^ place) * chunk, SUB)
@@ -128,7 +136,7 @@
 
     lane = lax.broadcasted_iota(jnp.int32, (SUB, LANES), 1)
     halves = depth // SUB
-    for e, (_, source) in enumerate(sides):
+    for e, (_, by) in enumerate(sides):
         edges[e].wait()
         for g in range(column.shape[1]):
             acc = jnp.zeros((SUB, LANES), f32)
@@ -136,14 +144,15 @@
                 c, rest = divmod(g * LANES + j, cells * halves)
                 t, h = divmod(rest, halves)
                 piece = tile[e, c, t, h * SUB : (h + 1) * SUB, :]
-                acc = jnp.where(lane == j, pltpu.roll(piece, (j - source) % LANES, 1), acc)
+                acc = jnp.where(lane == j, pltpu.roll(piece, by(j), 1), acc)
             column[e, g] = acc
     for one in copies:
         one.wait()
     face.wait()
-
-
-def stencil(fields, swirl, mask, tiles, near, shift, column_low, column_high, out):
+    whole.wait()
+
+
+def stencil(fields, swirl, mask, flags, near, shift, column_low, column_high, out):
     azi, rad = lax.axis_index("azi"), lax.axis_index("rad")
     last_rad = lax.axis_size("rad") - 1
     count, cells, depth, width = fields.shape
@@ -151,67 +160,79 @@
     parity = azi % 2
     halves = depth // SUB
     blocks = width // LANES
-    lane = lax.broadcasted_iota(jnp.int32, (depth, LANES), 1)
-    row = lax.broadcasted_iota(jnp.int32, (depth, LANES), 0)
+    lane = lax.broadcasted_iota(jnp.int32, (SUB, LANES), 1)
+    row = lax.broadcasted_iota(jnp.int32, (SUB, LANES), 0)
     at_left, at_right = lane == 0, lane == LANES - 1
-    at_low, at_high = row == 0, row == depth - 1
-
-    def slab(t, before, after):
-        tile_row = tiles[t // TILE]
-        x, s, prev = [], [], []
+    at_low, at_high = row == 0, row == SUB - 1
+    has_left, has_right = rad > 0, rad < last_rad
+    turned = (0.5 * flags[...].astype(f32)).T
+
+    def cut(h, l):
+        return slice(h * SUB, (h + 1) * SUB), slice(l * LANES, (l + 1) * LANES)
+
+    def slab(t, tile, before, after):
+        levels = [jnp.broadcast_to(tile[h], (SUB, LANES)) for h in range(halves)]
         for c in range(count):
-            parts = [fields[c, t, :, l * LANES : (l + 1) * LANES] for l in range(blocks)]
-            edge_low, edge_high = [], []
+            edges = []
             for h in range(halves):
                 n = (c * cells + t) * halves + h
                 g, j = n // LANES, n % LANES
-                edge_low.append(pltpu.roll(column_low[g], (LANES - j) % LANES, 1))
-                edge_high.append(pltpu.roll(column_high[g], LANES - 1 - j, 1))
-            left_edge = jnp.where(rad > 0, jnp.concatenate(edge_low, axis=0), 0.0)
-            right_edge = jnp.where(rad < last_rad, jnp.concatenate(edge_high, axis=0), 0.0)
-            ups = [pltpu.roll(v, 1, 1) for v in parts]
-            downs = [pltpu.roll(v, LANES - 1, 1) for v in parts]
-            total, previous = [], []
+                edges.append((
+                    jnp.where(has_left, pltpu.roll(column_low[g], (LANES - j) % LANES, 1), 0.0),
+                    jnp.where(has_right, pltpu.roll(column_high[g], LANES - 1 - j, 1), 0.0),
+                ))
+            parts = [[fields[(c, t) + cut(h, l)] for l in range(blocks)] for h in range(halves)]
+            ups = [[pltpu.roll(v, 1, 1) for v in p] for p in parts]
+            downs = [[pltpu.roll(v, LANES - 1, 1) for v in p] for p in parts]
             for l in range(blocks):
-                left = jnp.where(at_left, ups[l - 1] if l else left_edge, ups[l])
-                right = jnp.where(at_right, downs[l + 1] if l + 1 < blocks else right_edge, downs[l])
-                low = jnp.where(at_low, 0.0, pltpu.roll(parts[l], 1, 0))
-                high = jnp.where(at_high, 0.0, pltpu.roll(parts[l], depth - 1, 0))
-                total.append((left + right) + (low + high) + after(c, l))
-                previous.append(before(c, l))
-            x.append(parts)
-            s.append(total)
-            prev.append(previous)
-        for l in range(blocks):
-            lanes = slice(l * LANES, (l + 1) * LANES)
-            speed = swirl[t, :, lanes]
-            inert = mask[t, :, lanes].astype(f32)
-            energy, fuel = x[0][l], x[1][l]
-            burn = tile_row * (1.0 - inert) * fuel * (1.0 + jnp.tanh(2.0 * energy - 1.0))
-            stay, come = 0.4 - speed, speed + 0.1
-            out[0, t, :, lanes] = energy * stay + 0.1 * s[0][l] + come * prev[0][l] + 2.0 * burn
-            out[1, t, :, lanes] = fuel * stay + 0.1 * s[1][l] + come * prev[1][l] - burn
+                lows = [pltpu.roll(parts[h][l], 1, 0) for h in range(halves)]
+                highs = [pltpu.roll(parts[h][l], SUB - 1, 0) for h in range(halves)]
+                for h in range(halves):
+                    left = jnp.where(at_left, ups[h][l - 1] if l else edges[h][0], ups[h][l])
+                    right = jnp.where(at_right, downs[h][l + 1] if l + 1 < blocks else edges[h][1], downs[h][l])
+                    low = jnp.where(at_low, lows[h - 1] if h else 0.0, lows[h])
+                    high = jnp.where(at_high, highs[h + 1] if h + 1 < halves else 0.0, highs[h])
+                    total = (left + right) + (low + high) + after(c, h, l)
+                    speed = swirl[(t,) + cut(h, l)]
+                    value = parts[h][l] * (0.4 - speed) + before(c, h, l) * (speed + 0.1) + 0.1 * total
+                    if c == 0:
+                        out[(0, t) + cut(h, l)] = value
+                    else:
+                        live = jnp.where(mask[(t,) + cut(h, l)] == 0, levels[h], 0.0) * parts[h][l]
+                        energy = fields[(0, t) + cut(h, l)]
+                        burn = live + live * jnp.tanh(2.0 * energy - 1.0)
+                        out[(0, t) + cut(h, l)] += burn
+                        out[(1, t) + cut(h, l)] = value - 0.5 * burn
 
     def halo(use_near):
-        def value(c, l):
-            lanes = slice(l * LANES, (l + 1) * LANES)
-            a = near[base + c * depth : base + (c + 1) * depth, lanes]
-            b = shift[c * depth : (c + 1) * depth, lanes]
+        def value(c, h, l):
+            _, lanes = cut(h, l)
+            a = near[base + c * depth + h * SUB : base + c * depth + (h + 1) * SUB, lanes]
+            b = shift[c * depth + h * SUB : c * depth + (h + 1) * SUB, lanes]
             return jnp.where(use_near, a, b)
 
         return value
 
     def inside(t):
-        return lambda c, l: fields[c, t, :, l * LANES : (l + 1) * LANES]
-
-    slab(0, halo(parity == 1), inside(1))
-
-    def step(t, carry):
-        slab(t, inside(t - 1), inside(t + 1))
-        return carry
-
-    lax.fori_loop(1, cells - 1, step, 0)
-    slab(cells - 1, inside(cells - 2), halo(parity == 0))
+        return lambda c, h, l: fields[(c, t) + cut(h, l)]
+
+    tiles = [[turned[h * SUB : (h + 1) * SUB, k : k + 1] for h in range(halves)] for k in range(cells // TILE)]
+    for k in range(cells // TILE):
+        first, last = k * TILE, (k + 1) * TILE
+        if first == 0:
+            slab(0, tiles[k], halo(parity == 1), inside(1))
+            first = 1
+        if last == cells:
+            last = cells - 1
+
+        def step(t, carry, tile=tiles[k]):
+            slab(t, tile, inside(t - 1), inside(t + 1))
+            return carry
+
+        lax.fori_loop(first, last, step, 0, unroll=UNROLL)
+
+        if last == cells - 1:
+            slab(cells - 1, tiles[k], inside(cells - 2), halo(parity == 0))
 
 
 def feed_rows(slots, targets, *refs):
@@ -295,11 +316,10 @@
     phase, phase_t = phases(total_cells, lax.axis_index("azi") * cells, cells, half_modes)
     gain = jnp.concatenate([outlet_gain, outlet_gain], axis=1)
     weights = phase_t[None] * gain[:, None, :] * (0.1 * 2.0 / math.sqrt(half_modes * total_cells))
-    tiles = jnp.broadcast_to(0.25 * tile_flags.astype(f32)[:, :, None], tile_flags.shape + (LANES,))
     groups = count * cells * depth // SUB // LANES
 
     struct = jax.ShapeDtypeStruct
-    keep, send, shift, row_top, row_out, column = pl.pallas_call(
+    keep, send, shift, row_top, row_out, column, local = pl.pallas_call(
         functools.partial(prepare, chunk),
         out_shape=(
             struct((pairs * chunk, width), f32),
@@ -308,18 +328,20 @@
             struct((count, cells, width), f32),
             struct((count, cells, width), f32),
             struct((1 if radials == 2 else 2, groups, SUB, LANES), f32),
+            struct(fields.shape, f32),
         ),
-        in_specs=[HBM, VMEM, VMEM, HBM],
-        out_specs=[VMEM] * 6,
+        in_specs=[HBM, VMEM, HBM, HBM],
+        out_specs=[VMEM] * 7,
         scratch_shapes=[
+            pltpu.VMEM((sectors, slots), f32),
             pltpu.VMEM((sectors, slots, width), f32),
             pltpu.VMEM((1 if radials == 2 else 2, count, cells, depth, LANES), f32),
-            pltpu.SemaphoreType.DMA((2 * count + 6,)),
+            pltpu.SemaphoreType.DMA((2 * count + 8,)),
         ],
         compiler_params=params(12),
         cost_estimate=cost(1 << 26, 1 << 21),
         name="prepare",
-    )(in_hbm(fields), phase, feed_rate[0], in_hbm(plenum[0]))
+    )(in_hbm(fields), phase, in_hbm(feed_rate[0]), in_hbm(plenum[0]))
 
     def swap(x, k):
         return lax.ppermute(x, "azi", [(i, i ^ k) for i in range(sectors)])
@@ -355,7 +377,7 @@
         compiler_params=params(12),
         cost_estimate=cost(1 << 28, 1 << 23),
         name="stencil",
-    )(fields, swirl_speed, ghost_mask, tiles, near, far, edge_low, edge_high)
+    )(local, swirl_speed, ghost_mask, tile_flags, near, far, edge_low, edge_high)
 
     feed = pl.pallas_call(
         functools.partial(feed_rows, slots),

time: 39.9 us -> 33.5 us (0.84)
  Pallas kernels: 15.2 us -> 11.6 us
  local copies, waits for them, and re-layouts: 2.58 us -> 0.09 us
  other arithmetic: 1.38 us -> 0.62 us
  waiting for transfers between devices: 8.1 us -> 8.85 us
    pallas_call x1, Pallas kernels: 9.01 us -> 5.11 us  [body(): pl.pallas_call(stencil, out_shape=struct(fields.shape, f32), in_specs=[VM...]
    unnamed x12 -> x10, local copies, waits for them, and re-layouts: 2.44 us -> 0.02 us
    concatenate x1, other arithmetic: 0.83 us -> 0.07 us  [body(): gain = jnp.concatenate([outlet_gain, outlet_gain], axis=1)]
    ppermute x5, waiting for transfers between devices: 8.09 us -> 8.85 us  [swap(): return lax.ppermute(x, 'azi', [(i, i ^ k) for i in range(sectors)])]
  transfers between devices with their start and end apart: 8 -> 8, of which waited for: 2 -> 2; matrix products, arithmetic and copies ran while one was open for 3% -> 2% of each run, Pallas kernels for 26% -> 19%
where the time goes in v3:
time: 33.5 us; the launch traced here: 33.4 us
  starting transfers between devices  12 us (36%)
  Pallas kernels  11.6 us (35%)
  waiting for transfers between devices  8.85 us (26%)
  other arithmetic  0.62 us (2%)
    ppermute x5, waiting for transfers between devices, swap(): return lax.ppermute(x, 'azi', [(i, i ^ k) for i in range(sectors)])  8.85 us
    pallas_call x1, Pallas kernels, body(): pl.pallas_call(stencil, out_shape=struct(fields.shape, f32), in_specs=[VM...  5.11 us
    ppermute x5, starting transfers between devices, swap(): return lax.ppermute(x, 'azi', [(i, i ^ k) for i in range(sectors)])  4.66 us
    ppermute x2, starting transfers between devices, across(): received = lax.ppermute(to_only, axis, [(0, 1), (1, 0)])  4.56 us
    pallas_call x1, Pallas kernels, body(): pl.pallas_call(functools.partial(prepare, chunk), out_shape=(struct((pair...  3.09 us
    ppermute x1, starting transfers between devices, body(): far = lax.ppermute(shift, 'azi', offset)  2.76 us
    pallas_call x1, Pallas kernels, body(): pl.pallas_call(functools.partial(finish, chunk, length), out_shape=struct...  2.21 us
    pallas_call x1, Pallas kernels, body(): pl.pallas_call(functools.partial(feed_rows, slots), out_shape=struct((cel...  1.16 us
  transfers between devices with their start and end apart: 8, of which 2 were waited for; matrix products, arithmetic and copies ran while one was open for 2% of the time, Pallas kernels for 19%

profile of v3, /device:TPU:0, one launch (start us, length us, event | category | flops | bytes accessed | tf_op | source)
XLA Modules:
  0.0 33.4 jit_solution(4210317144463654819)
XLA Ops:
  0.0 0.0 copy-start.4
  0.0 0.0 copy-start.3
  0.0 0.0 copy-start
  0.0 0.0 copy-start.1
  0.0 0.2 fusion.11
  0.2 3.1 %prepare.1 = (f32[64,512]{1,0:T(8,128)S(1)}, f32[96,512]{1,0:T(8,128)S(1)}, f32[32,512]{1,0:T(8,128)S(1)}, f32[2,64,512]{2,1,0:T(8,128)S(1)}, f32[2,64,512]{2,1,...) custom-call(f32[2,64,16,512]{3,2,1,0:T(8,128)} %fields.1, ...), custom_call_target="tpu_custom_call" | custom-call | flops 67108864 | bytes 2097152 | tf_op jit(solution)/shard_map/prepare/pallas_call | solution.py:322
  3.3 3.0 %collective-permute-start.7 = (f32[2,8,128]{2,1,0:T(8,128)S(1)}, f32[2,8,128]{2,1,0:T(8,128)S(1)}, u32[]{:S(2)}, u32[]{:S(2)}) collective-permute-start(f32[2,8,128]{2,1,0:T(8,128)S(1)} %bitcast.5), channel_id=1, source_target_pairs={{0,1},{1,0},{2,3},{3,2},{4,5},{5,4},{6,7},{7,6},{8,9},{9,8},{10,11... | collective-permute-start | bytes 24584 | tf_op jit(solution)/shard_map/ppermute | solution.py:352
  6.4 2.8 %collective-permute-start.6 = (f32[32,512]{1,0:T(8,128)S(1)}, f32[32,512]{1,0:T(8,128)S(1)}, u32[]{:S(2)}, u32[]{:S(2)}) collective-permute-start(f32[32,512]{1,0:T(8,128)S(1)} %get-tuple-element.17), channel_id=1, source_target_pairs={{0,28},{4,8},{8,4},{12,16},{16,12},{20,24},{24,20},{28,0},{1,29},{... | collective-permute-start | bytes 196616 | tf_op jit(solution)/shard_map/ppermute | solution.py:359
  9.1 0.0 collective-permute-start.1
  9.1 0.2 fusion.9
  9.3 1.2 %collective-permute-done.1.near = f32[96,512]{1,0:T(8,128)S(1)} collective-permute-done((f32[96,512]{1,0:T(8,128)S(1)}, f32[96,512]{1,0:T(8,128)S(1)}, u32[]{:S(2)}, u32[]{:S(2)}) %collective-permute-start.1) | collective-permute-done | bytes 196640 | tf_op jit(solution)/shard_map/ppermute | solution.py:347
  10.7 1.2 %collective-permute-start.3 = (f32[64,512]{1,0:T(8,128)S(1)}, f32[64,512]{1,0:T(8,128)S(1)}, u32[]{:S(2)}, u32[]{:S(2)}) collective-permute-start(f32[64,512]{1,0:T(8,128)S(1)} %pad_maximum_fusion.1), channel_id=1, source_target_pairs={{0,16},{4,20},{8,24},{12,28},{16,0},{20,4},{24,8},{28,12},{1,17},{... | collective-permute-start | bytes 393224 | tf_op jit(solution)/shard_map/ppermute | solution.py:347
  11.9 0.3 collective-permute-start.2
  12.2 3.0 %collective-permute-start.4 = (f32[64,512]{1,0:T(8,128)S(1)}, f32[64,512]{1,0:T(8,128)S(1)}, u32[]{:S(2)}, u32[]{:S(2)}) collective-permute-start(f32[64,512]{1,0:T(8,128)S(1)} %pad_maximum_fusion.2), channel_id=1, source_target_pairs={{0,24},{4,28},{8,16},{12,20},{16,8},{20,12},{24,0},{28,4},{1,25},{... | collective-permute-start | bytes 393224 | tf_op jit(solution)/shard_map/ppermute | solution.py:347
  15.3 0.0 copy-done.4
  15.3 0.1 pad_maximum_fusion.5
  15.3 0.1 pad_maximum_fusion.4
  15.4 7.6 %collective-permute-done.2.refs_1_ = f32[64,512]{1,0:T(8,128)S(1)} collective-permute-done((f32[64,512]{1,0:T(8,128)S(1)}, f32[64,512]{1,0:T(8,128)S(1)}, u32[]{:S(2)}, u32[]{:S(2)}) %collective-permute-start.2) | collective-permute-done | bytes 131104 | tf_op jit(solution)/shard_map/ppermute | solution.py:347
  23.0 1.5 %collective-permute-start = (f32[2,64,512]{2,1,0:T(8,128)S(1)}, f32[2,64,512]{2,1,0:T(8,128)S(1)}, u32[]{:S(2)}, u32[]{:S(2)}) collective-permute-start(f32[2,64,512]{2,1,0:T(8,128)S(1)} %get-tuple-element.12), channel_id=1, source_target_pairs={{0,2},{2,0},{1,3},{3,1},{4,6},{6,4},{5,7},{7,5},{8,10},{10,8},{9,1... | collective-permute-start | bytes 786440 | tf_op jit(solution)/shard_map/ppermute | solution.py:352
  24.6 0.0 collective-permute-done.4.refs_3_
  24.6 0.0 collective-permute-done.3.refs_2_
  24.7 0.1 collective-permute-start.5
  24.8 0.0 collective-permute-done.7.column_low.column_high
  24.8 0.0 collective-permute-done.6.shift
  24.8 0.0 copy-done.3
  24.8 0.0 copy-done
  24.8 0.0 copy-done.1
  24.8 0.0 copy-start.2
  24.8 5.1 %stencil.1.before = f32[2,64,16,512]{3,2,1,0:T(8,128)S(1)} custom-call(f32[2,64,16,512]{3,2,1,0:T(8,128)S(1)} %get-tuple-element.16.fields, f32[64,16,512]{2,1,0:T(8,128)S(1)} %copy-done, s32[64,16,512]{2,1,0:T(8,128)S(1)} %copy-done.1, s32[4,16]{1,0:T(4,128)S(1)} %copy-done.3, f32[96,512]{1,0:T(8,128)S(1)} %collective-permute-done.1.near, ...), custom_call_target="tpu_custom_call" | custom-call | flops 268435456 | bytes 8388608 | tf_op jit(solution)/shard_map/stencil/pallas_call | solution.py:372
  30.0 0.0 copy-done.2
  30.0 1.2 %feed.1 = f32[520,512]{1,0:T(8,128)S(1)} custom-call(s32[8,8]{1,0:T(8,128)S(1)} %bitcast.4, f32[64,512]{1,0:T(8,128)S(1)} %slice_add_fusion.refs_0_, f32[64,512]{1,0:T(8,128)S(1)} %collective-permute-done.2.refs_1_, f32[64,512]{1,0:T(8,128)S(1)} %collective-permute-done.3.refs_2_, f32[64,512]{1,0:T(8,128)S(1)} %collective-permute-done.4.refs_3_), custom_call_target="tpu_custom_call" | custom-call | flops 33554432 | bytes 1048576 | tf_op jit(solution)/shard_map/feed/pallas_call | solution.py:382
  31.1 0.0 collective-permute-done.axial_low.axial_high
  31.1 0.0 collective-permute-done.5.other
  31.2 2.2 %finish.1 = f32[2,64,16,512]{3,2,1,0:T(8,128)} custom-call(f32[2,64,512]{2,1,0:T(8,128)S(1)} %collective-permute-done.axial_low.axial_high, f32[2,64,512]{2,1,0:T(8,128)S(1)} %collective-permute-done.axial_low.axial_high, f32[2,64,512]{2,1,0:T(8,128)S(1)} %get-tuple-element.13.row_top, f32[64,512]{1,0:T(8,128)S(1)} %fusion.1.own, ...), custom_call_target="tpu_custom_call" | custom-call | flops 67108864 | bytes 8388608 | tf_op jit(solution)/shard_map/finish/pallas_call | solution.py:394
  (17 shorter events, 0.2 us)
Async XLA Ops:
  0.0 15.3 %copy-start.4 = (f32[2,32]{1,0:T(2,128)S(1)}, f32[2,32]{1,0:T(2,128)}, u32[]{:S(2)}) copy-start(f32[2,32]{1,0:T(2,128)} %param.12) | copy-start | bytes 772
  0.0 24.8 %copy-start.3 = (s32[4,16]{1,0:T(4,128)S(1)}, s32[4,16]{1,0:T(4,128)}, u32[]{:S(2)}) copy-start(s32[4,16]{1,0:T(4,128)} %flags.1) | copy-start | bytes 772
  0.0 24.8 %copy-start = (f32[64,16,512]{2,1,0:T(8,128)S(1)}, f32[64,16,512]{2,1,0:T(8,128)}, u32[]{:S(2)}) copy-start(f32[64,16,512]{2,1,0:T(8,128)} %swirl.1) | copy-start | bytes 6291460
  0.0 24.8 %copy-start.1 = (s32[64,16,512]{2,1,0:T(8,128)S(1)}, s32[64,16,512]{2,1,0:T(8,128)}, u32[]{:S(2)}) copy-start(s32[64,16,512]{2,1,0:T(8,128)} %mask.1) | copy-start | bytes 6291460
  3.3 21.5 %collective-permute-start.7 = (f32[2,8,128]{2,1,0:T(8,128)S(1)}, f32[2,8,128]{2,1,0:T(8,128)S(1)}, u32[]{:S(2)}, u32[]{:S(2)}) collective-permute-start(f32[2,8,128]{2,1,0:T(8,128)S(1)} %bitcast.5), channel_id=1, source_target_pairs={{0,1},{1,0},{2,3},{3,2},{4,5},{5,4},{6,7},{7,6},{8,9},{9,8},{10,11... | collective-permute-start | bytes 24584 | tf_op jit(solution)/shard_map/ppermute | solution.py:352
  6.4 18.4 %collective-permute-start.6 = (f32[32,512]{1,0:T(8,128)S(1)}, f32[32,512]{1,0:T(8,128)S(1)}, u32[]{:S(2)}, u32[]{:S(2)}) collective-permute-start(f32[32,512]{1,0:T(8,128)S(1)} %get-tuple-element.17), channel_id=1, source_target_pairs={{0,28},{4,8},{8,4},{12,16},{16,12},{20,24},{24,20},{28,0},{1,29},{... | collective-permute-start | bytes 196616 | tf_op jit(solution)/shard_map/ppermute | solution.py:359
  9.1 1.4 %collective-permute-start.1 = (f32[96,512]{1,0:T(8,128)S(1)}, f32[96,512]{1,0:T(8,128)S(1)}, u32[]{:S(2)}, u32[]{:S(2)}) collective-permute-start(f32[96,512]{1,0:T(8,128)S(1)} %get-tuple-element.15), channel_id=1, source_target_pairs={{0,4},{4,0},{8,12},{12,8},{16,20},{20,16},{24,28},{28,24},{1,5},{5... | collective-permute-start | bytes 589832 | tf_op jit(solution)/shard_map/ppermute | solution.py:347
  10.7 14.0 %collective-permute-start.3 = (f32[64,512]{1,0:T(8,128)S(1)}, f32[64,512]{1,0:T(8,128)S(1)}, u32[]{:S(2)}, u32[]{:S(2)}) collective-permute-start(f32[64,512]{1,0:T(8,128)S(1)} %pad_maximum_fusion.1), channel_id=1, source_target_pairs={{0,16},{4,20},{8,24},{12,28},{16,0},{20,4},{24,8},{28,12},{1,17},{... | collective-permute-start | bytes 393224 | tf_op jit(solution)/shard_map/ppermute | solution.py:347
  11.9 11.2 %collective-permute-start.2 = (f32[64,512]{1,0:T(8,128)S(1)}, f32[64,512]{1,0:T(8,128)S(1)}, u32[]{:S(2)}, u32[]{:S(2)}) collective-permute-start(f32[64,512]{1,0:T(8,128)S(1)} %pad_maximum_fusion), channel_id=1, source_target_pairs={{0,8},{4,12},{8,0},{12,4},{16,24},{20,28},{24,16},{28,20},{1,9},{5... | collective-permute-start | bytes 393224 | tf_op jit(solution)/shard_map/ppermute | solution.py:347
  12.2 12.4 %collective-permute-start.4 = (f32[64,512]{1,0:T(8,128)S(1)}, f32[64,512]{1,0:T(8,128)S(1)}, u32[]{:S(2)}, u32[]{:S(2)}) collective-permute-start(f32[64,512]{1,0:T(8,128)S(1)} %pad_maximum_fusion.2), channel_id=1, source_target_pairs={{0,24},{4,28},{8,16},{12,20},{16,8},{20,12},{24,0},{28,4},{1,25},{... | collective-permute-start | bytes 393224 | tf_op jit(solution)/shard_map/ppermute | solution.py:347
  23.0 8.1 %collective-permute-start = (f32[2,64,512]{2,1,0:T(8,128)S(1)}, f32[2,64,512]{2,1,0:T(8,128)S(1)}, u32[]{:S(2)}, u32[]{:S(2)}) collective-permute-start(f32[2,64,512]{2,1,0:T(8,128)S(1)} %get-tuple-element.12), channel_id=1, source_target_pairs={{0,2},{2,0},{1,3},{3,1},{4,6},{6,4},{5,7},{7,5},{8,10},{10,8},{9,1... | collective-permute-start | bytes 786440 | tf_op jit(solution)/shard_map/ppermute | solution.py:352
  24.7 6.5 %collective-permute-start.5 = (f32[64,512]{1,0:T(8,128)S(1)}, f32[64,512]{1,0:T(8,128)S(1)}, u32[]{:S(2)}, u32[]{:S(2)}) collective-permute-start(f32[64,512]{1,0:T(8,128)S(1)} %fusion.1.own), channel_id=1, source_target_pairs={{0,4},{4,0},{8,12},{12,8},{16,20},{20,16},{24,28},{28,24},{1,5},{5... | collective-permute-start | bytes 393224 | tf_op jit(solution)/shard_map/ppermute | solution.py:347
  24.8 5.1 %copy-start.2 = (s32[1,8,8]{2,1,0:T(8,128)S(1)}, s32[1,8,8]{2,1,0:T(8,128)}, u32[]{:S(2)}) copy-start(s32[1,8,8]{2,1,0:T(8,128)} %param.15) | copy-start | bytes 772

commit v4 on v3

--- a/solution.py
+++ b/solution.py
@@ -45,7 +45,7 @@
 
 
 def prepare(
-    chunk, fields, phase, rates, profile, keep, send, shift, row_top, row_out, column, local, rate, plenum, tile, sem
+    chunk, fields, phase, rates, profile, keep, send, shift, row_top, row_out, column, rate, plenum, tile, sem
 ):
     azi, ax, rad = lax.axis_index("azi"), lax.axis_index("ax"), lax.axis_index("rad")
     last_ax = lax.axis_size("ax") - 1
@@ -72,7 +72,7 @@
         copies.append(pltpu.make_async_copy(fields.at[c, t_shift], shift.at[rows], sem.at[2 + 2 * c]))
     edges = [
         pltpu.make_async_copy(
-            fields.at[:, :, :, pl.ds(pl.multiple_of(side, LANES), LANES)], tile.at[e], sem.at[6 + 2 * count + e]
+            fields.at[:, :, :, pl.ds(pl.multiple_of(side, LANES), LANES)], tile.at[e], sem.at[5 + 2 * count + e]
         )
         for e, (side, _) in enumerate(sides)
     ]
@@ -86,8 +86,6 @@
     supply.start()
     factor = pltpu.make_async_copy(rates, rate, sem.at[4 + 2 * count])
     factor.start()
-    whole = pltpu.make_async_copy(fields, local, sem.at[5 + 2 * count])
-    whole.start()
 
     @pl.when(ax == last_ax)
     def _():
@@ -149,10 +147,9 @@
     for one in copies:
         one.wait()
     face.wait()
-    whole.wait()
-
-
-def stencil(fields, swirl, mask, flags, near, shift, column_low, column_high, out):
+
+
+def stencil(source, swirl, mask, flags, near, shift, column_low, column_high, out, fields, levels, sem):
     azi, rad = lax.axis_index("azi"), lax.axis_index("rad")
     last_rad = lax.axis_size("rad") - 1
     count, cells, depth, width = fields.shape
@@ -165,13 +162,19 @@
     at_left, at_right = lane == 0, lane == LANES - 1
     at_low, at_high = row == 0, row == SUB - 1
     has_left, has_right = rad > 0, rad < last_rad
+    pieces = [slice(k * TILE, (k + 1) * TILE) for k in range(cells // TILE)]
+    copies = [pltpu.make_async_copy(source.at[:, p], fields.at[:, p], sem.at[k]) for k, p in enumerate(pieces)]
+    for copy in copies:
+        copy.start()
     turned = (0.5 * flags[...].astype(f32)).T
+    for k in range(cells // TILE):
+        levels[k] = jnp.broadcast_to(turned[:, k : k + 1], (depth, LANES))
 
     def cut(h, l):
         return slice(h * SUB, (h + 1) * SUB), slice(l * LANES, (l + 1) * LANES)
 
-    def slab(t, tile, before, after):
-        levels = [jnp.broadcast_to(tile[h], (SUB, LANES)) for h in range(halves)]
+    def slab(t, before, after):
+        level = levels[t // TILE]
         for c in range(count):
             edges = []
             for h in range(halves):
@@ -198,7 +201,7 @@
                     if c == 0:
                         out[(0, t) + cut(h, l)] = value
                     else:
-                        live = jnp.where(mask[(t,) + cut(h, l)] == 0, levels[h], 0.0) * parts[h][l]
+                        live = jnp.where(mask[(t,) + cut(h, l)] == 0, level[h * SUB : (h + 1) * SUB], 0.0) * parts[h][l]
                         energy = fields[(0, t) + cut(h, l)]
                         burn = live + live * jnp.tanh(2.0 * energy - 1.0)
                         out[(0, t) + cut(h, l)] += burn
@@ -216,23 +219,17 @@
     def inside(t):
         return lambda c, h, l: fields[(c, t) + cut(h, l)]
 
-    tiles = [[turned[h * SUB : (h + 1) * SUB, k : k + 1] for h in range(halves)] for k in range(cells // TILE)]
-    for k in range(cells // TILE):
-        first, last = k * TILE, (k + 1) * TILE
-        if first == 0:
-            slab(0, tiles[k], halo(parity == 1), inside(1))
-            first = 1
-        if last == cells:
-            last = cells - 1
-
-        def step(t, carry, tile=tiles[k]):
-            slab(t, tile, inside(t - 1), inside(t + 1))
-            return carry
-
-        lax.fori_loop(first, last, step, 0, unroll=UNROLL)
-
-        if last == cells - 1:
-            slab(cells - 1, tiles[k], inside(cells - 2), halo(parity == 0))
+    def step(t, carry):
+        slab(t, inside(t - 1), inside(t + 1))
+        return carry
+
+    copies[0].wait()
+    slab(0, halo(parity == 1), inside(1))
+    for k, copy in enumerate(copies):
+        if k:
+            copy.wait()
+        lax.fori_loop(k * TILE - 1 if k else 1, (k + 1) * TILE - 1, step, 0, unroll=UNROLL)
+    slab(cells - 1, inside(cells - 2), halo(parity == 0))
 
 
 def feed_rows(slots, targets, *refs):
@@ -319,7 +316,7 @@
     groups = count * cells * depth // SUB // LANES
 
     struct = jax.ShapeDtypeStruct
-    keep, send, shift, row_top, row_out, column, local = pl.pallas_call(
+    keep, send, shift, row_top, row_out, column = pl.pallas_call(
         functools.partial(prepare, chunk),
         out_shape=(
             struct((pairs * chunk, width), f32),
@@ -328,15 +325,14 @@
             struct((count, cells, width), f32),
             struct((count, cells, width), f32),
             struct((1 if radials == 2 else 2, groups, SUB, LANES), f32),
-            struct(fields.shape, f32),
         ),
         in_specs=[HBM, VMEM, HBM, HBM],
-        out_specs=[VMEM] * 7,
+        out_specs=[VMEM] * 6,
         scratch_shapes=[
             pltpu.VMEM((sectors, slots), f32),
             pltpu.VMEM((sectors, slots, width), f32),
             pltpu.VMEM((1 if radials == 2 else 2, count, cells, depth, LANES), f32),
-            pltpu.SemaphoreType.DMA((2 * count + 8,)),
+            pltpu.SemaphoreType.DMA((2 * count + 7,)),
         ],
         compiler_params=params(12),
         cost_estimate=cost(1 << 26, 1 << 21),
@@ -372,12 +368,17 @@
     before = pl.pallas_call(
         stencil,
         out_shape=struct(fields.shape, f32),
-        in_specs=[VMEM] * 8,
+        in_specs=[HBM] + [VMEM] * 7,
         out_specs=VMEM,
+        scratch_shapes=[
+            pltpu.VMEM(fields.shape, f32),
+            pltpu.VMEM((cells // TILE, depth, LANES), f32),
+            pltpu.SemaphoreType.DMA((cells // TILE,)),
+        ],
         compiler_params=params(12),
         cost_estimate=cost(1 << 28, 1 << 23),
         name="stencil",
-    )(local, swirl_speed, ghost_mask, tile_flags, near, far, edge_low, edge_high)
+    )(in_hbm(fields), swirl_speed, ghost_mask, tile_flags, near, far, edge_low, edge_high)
 
     feed = pl.pallas_call(
         functools.partial(feed_rows, slots),

time: 33.5 us -> 34.1 us (1.018)
    pallas_call x1, Pallas kernels: 5.11 us -> 6.32 us  [body(): pl.pallas_call(stencil, out_shape=struct(fields.shape, f32), in_specs=[HB...]
    pallas_call x1, Pallas kernels: 3.09 us -> 2.26 us  [body(): pl.pallas_call(functools.partial(prepare, chunk), out_shape=(struct((pair...]
  transfers between devices with their start and end apart: 8 -> 8, of which waited for: 2 -> 2; matrix products, arithmetic and copies ran while one was open for 2% -> 2% of each run, Pallas kernels for 19% -> 22%
where the time goes in v4:
time: 34.1 us; the launch traced here: 34 us
  starting transfers between devices  12.2 us (36%)
  Pallas kernels  11.9 us (35%)
  waiting for transfers between devices  8.85 us (26%)
  other arithmetic  0.63 us (2%)
    ppermute x5, waiting for transfers between devices, swap(): return lax.ppermute(x, 'azi', [(i, i ^ k) for i in range(sectors)])  8.84 us
    pallas_call x1, Pallas kernels, body(): pl.pallas_call(stencil, out_shape=struct(fields.shape, f32), in_specs=[HB...  6.32 us
    ppermute x2, starting transfers between devices, across(): received = lax.ppermute(to_only, axis, [(0, 1), (1, 0)])  4.78 us
    ppermute x5, starting transfers between devices, swap(): return lax.ppermute(x, 'azi', [(i, i ^ k) for i in range(sectors)])  4.66 us
    ppermute x1, starting transfers between devices, body(): far = lax.ppermute(shift, 'azi', offset)  2.76 us
    pallas_call x1, Pallas kernels, body(): pl.pallas_call(functools.partial(prepare, chunk), out_shape=(struct((pair...  2.26 us
    pallas_call x1, Pallas kernels, body(): pl.pallas_call(functools.partial(finish, chunk, length), out_shape=struct...  2.21 us
    pallas_call x1, Pallas kernels, body(): pl.pallas_call(functools.partial(feed_rows, slots), out_shape=struct((cel...  1.16 us
  transfers between devices with their start and end apart: 8, of which 2 were waited for; matrix products, arithmetic and copies ran while one was open for 2% of the time, Pallas kernels for 22%

profile of v4, /device:TPU:0, one launch (start us, length us, event | category | flops | bytes accessed | tf_op | source)
XLA Modules:
  0.0 34.0 jit_solution(1381328825005951879)
XLA Ops:
  0.0 0.0 copy-start.4
  0.0 0.0 copy-start.3
  0.0 0.0 copy-start
  0.0 0.0 copy-start.1
  0.0 0.2 fusion.11
  0.2 2.3 %prepare.1 = (f32[64,512]{1,0:T(8,128)S(1)}, f32[96,512]{1,0:T(8,128)S(1)}, f32[32,512]{1,0:T(8,128)S(1)}, f32[2,64,512]{2,1,0:T(8,128)S(1)}, f32[2,64,512]{2,1,0:T(8,128)S(1)}, /*index=5*/f32[1,2,8,128]{3,2,1,0:T(8,128)S(1)}) custom-call(f32[2,64,16,512]{3,2,1,0:T(8,128)} %source.1, f32[64,64]{1,0:T(8,128)S(1)} %pad_maximum_fusion.3.phase, f32[8,8]{1,0:T(8,128)} %bitcast.7, ...), custom_call_target="tpu_custom_call" | custom-call | flops 67108864 | bytes 2097152 | tf_op jit(solution)/shard_map/prepare/pallas_call | solution.py:319
  2.5 3.0 %collective-permute-start.7 = (f32[2,8,128]{2,1,0:T(8,128)S(1)}, f32[2,8,128]{2,1,0:T(8,128)S(1)}, u32[]{:S(2)}, u32[]{:S(2)}) collective-permute-start(f32[2,8,128]{2,1,0:T(8,128)S(1)} %bitcast.5), channel_id=1, source_target_pairs={{0,1},{1,0},{2,3},{3,2},{4,5},{5,4},{6,7},{7,6},{8,9},{9,8},{10,11... | collective-permute-start | bytes 24584 | tf_op jit(solution)/shard_map/ppermute | solution.py:348
  5.5 2.8 %collective-permute-start.6 = (f32[32,512]{1,0:T(8,128)S(1)}, f32[32,512]{1,0:T(8,128)S(1)}, u32[]{:S(2)}, u32[]{:S(2)}) collective-permute-start(f32[32,512]{1,0:T(8,128)S(1)} %get-tuple-element.15), channel_id=1, source_target_pairs={{0,28},{4,8},{8,4},{12,16},{16,12},{20,24},{24,20},{28,0},{1,29},{... | collective-permute-start | bytes 196616 | tf_op jit(solution)/shard_map/ppermute | solution.py:355
  8.3 0.0 collective-permute-start.1
  8.3 0.2 fusion.9
  8.5 1.2 %collective-permute-done.1.near = f32[96,512]{1,0:T(8,128)S(1)} collective-permute-done((f32[96,512]{1,0:T(8,128)S(1)}, f32[96,512]{1,0:T(8,128)S(1)}, u32[]{:S(2)}, u32[]{:S(2)}) %collective-permute-start.1) | collective-permute-done | bytes 196640 | tf_op jit(solution)/shard_map/ppermute | solution.py:343
  9.8 1.2 %collective-permute-start.3 = (f32[64,512]{1,0:T(8,128)S(1)}, f32[64,512]{1,0:T(8,128)S(1)}, u32[]{:S(2)}, u32[]{:S(2)}) collective-permute-start(f32[64,512]{1,0:T(8,128)S(1)} %pad_maximum_fusion.1), channel_id=1, source_target_pairs={{0,16},{4,20},{8,24},{12,28},{16,0},{20,4},{24,8},{28,12},{1,17},{... | collective-permute-start | bytes 393224 | tf_op jit(solution)/shard_map/ppermute | solution.py:343
  11.0 0.3 collective-permute-start.2
  11.4 3.0 %collective-permute-start.4 = (f32[64,512]{1,0:T(8,128)S(1)}, f32[64,512]{1,0:T(8,128)S(1)}, u32[]{:S(2)}, u32[]{:S(2)}) collective-permute-start(f32[64,512]{1,0:T(8,128)S(1)} %pad_maximum_fusion.2), channel_id=1, source_target_pairs={{0,24},{4,28},{8,16},{12,20},{16,8},{20,12},{24,0},{28,4},{1,25},{... | collective-permute-start | bytes 393224 | tf_op jit(solution)/shard_map/ppermute | solution.py:343
  14.4 0.0 copy-done.4
  14.4 0.1 pad_maximum_fusion.5
  14.5 0.1 pad_maximum_fusion.4
  14.6 7.6 %collective-permute-done.2.refs_1_ = f32[64,512]{1,0:T(8,128)S(1)} collective-permute-done((f32[64,512]{1,0:T(8,128)S(1)}, f32[64,512]{1,0:T(8,128)S(1)}, u32[]{:S(2)}, u32[]{:S(2)}) %collective-permute-start.2) | collective-permute-done | bytes 131104 | tf_op jit(solution)/shard_map/ppermute | solution.py:343
  22.2 1.7 %collective-permute-start = (f32[2,64,512]{2,1,0:T(8,128)S(1)}, f32[2,64,512]{2,1,0:T(8,128)S(1)}, u32[]{:S(2)}, u32[]{:S(2)}) collective-permute-start(f32[2,64,512]{2,1,0:T(8,128)S(1)} %get-tuple-element.11), channel_id=1, source_target_pairs={{0,2},{2,0},{1,3},{3,1},{4,6},{6,4},{5,7},{7,5},{8,10},{10,8},{9,1... | collective-permute-start | bytes 786440 | tf_op jit(solution)/shard_map/ppermute | solution.py:348
  24.0 0.0 collective-permute-done.4.refs_3_
  24.0 0.0 collective-permute-done.3.refs_2_
  24.1 0.1 collective-permute-start.5
  24.2 0.0 copy-start.2
  24.2 0.0 collective-permute-done.7.column_low.column_high
  24.2 0.0 collective-permute-done.6.shift
  24.2 0.0 copy-done.3
  24.2 0.0 copy-done
  24.2 0.0 copy-done.1
  24.2 6.3 %stencil.1.before = f32[2,64,16,512]{3,2,1,0:T(8,128)S(1)} custom-call(f32[2,64,16,512]{3,2,1,0:T(8,128)} %source.1, f32[64,16,512]{2,1,0:T(8,128)S(1)} %copy-done, s32[64,16,512]{2,1,0:T(8,128)S(1)} %copy-done.1, s32[4,16]{1,0:T(4,128)S(1)} %copy-done.3, f32[96,512]{1,0:T(8,128)S(1)} %collective-permute-done.1.near, ...), custom_call_target="tpu_custom_call" | custom-call | flops 268435456 | bytes 8388608 | tf_op jit(solution)/shard_map/stencil/pallas_call | solution.py:368
  30.6 0.0 copy-done.2
  30.6 1.2 %feed.1 = f32[520,512]{1,0:T(8,128)S(1)} custom-call(s32[8,8]{1,0:T(8,128)S(1)} %bitcast.4, f32[64,512]{1,0:T(8,128)S(1)} %slice_add_fusion.refs_0_, f32[64,512]{1,0:T(8,128)S(1)} %collective-permute-done.2.refs_1_, f32[64,512]{1,0:T(8,128)S(1)} %collective-permute-done.3.refs_2_, f32[64,512]{1,0:T(8,128)S(1)} %collective-permute-done.4.refs_3_), custom_call_target="tpu_custom_call" | custom-call | flops 33554432 | bytes 1048576 | tf_op jit(solution)/shard_map/feed/pallas_call | solution.py:383
  31.7 0.0 collective-permute-done.axial_low.axial_high
  31.7 0.0 collective-permute-done.5.other
  31.8 2.2 %finish.1 = f32[2,64,16,512]{3,2,1,0:T(8,128)} custom-call(f32[2,64,512]{2,1,0:T(8,128)S(1)} %collective-permute-done.axial_low.axial_high, f32[2,64,512]{2,1,0:T(8,128)S(1)} %collective-permute-done.axial_low.axial_high, f32[2,64,512]{2,1,0:T(8,128)S(1)} %get-tuple-element.12.row_top, f32[64,512]{1,0:T(8,128)S(1)} %fusion.1.own, ...), custom_call_target="tpu_custom_call" | custom-call | flops 67108864 | bytes 8388608 | tf_op jit(solution)/shard_map/finish/pallas_call | solution.py:395
  (17 shorter events, 0.2 us)
Async XLA Ops:
  0.0 14.4 %copy-start.4 = (f32[2,32]{1,0:T(2,128)S(1)}, f32[2,32]{1,0:T(2,128)}, u32[]{:S(2)}) copy-start(f32[2,32]{1,0:T(2,128)} %param.12) | copy-start | bytes 772
  0.0 24.2 %copy-start.3 = (s32[4,16]{1,0:T(4,128)S(1)}, s32[4,16]{1,0:T(4,128)}, u32[]{:S(2)}) copy-start(s32[4,16]{1,0:T(4,128)} %flags.1) | copy-start | bytes 772
  0.0 24.2 %copy-start = (f32[64,16,512]{2,1,0:T(8,128)S(1)}, f32[64,16,512]{2,1,0:T(8,128)}, u32[]{:S(2)}) copy-start(f32[64,16,512]{2,1,0:T(8,128)} %swirl.1) | copy-start | bytes 6291460
  0.0 24.2 %copy-start.1 = (s32[64,16,512]{2,1,0:T(8,128)S(1)}, s32[64,16,512]{2,1,0:T(8,128)}, u32[]{:S(2)}) copy-start(s32[64,16,512]{2,1,0:T(8,128)} %mask.1) | copy-start | bytes 6291460
  2.5 21.7 %collective-permute-start.7 = (f32[2,8,128]{2,1,0:T(8,128)S(1)}, f32[2,8,128]{2,1,0:T(8,128)S(1)}, u32[]{:S(2)}, u32[]{:S(2)}) collective-permute-start(f32[2,8,128]{2,1,0:T(8,128)S(1)} %bitcast.5), channel_id=1, source_target_pairs={{0,1},{1,0},{2,3},{3,2},{4,5},{5,4},{6,7},{7,6},{8,9},{9,8},{10,11... | collective-permute-start | bytes 24584 | tf_op jit(solution)/shard_map/ppermute | solution.py:348
  5.5 18.7 %collective-permute-start.6 = (f32[32,512]{1,0:T(8,128)S(1)}, f32[32,512]{1,0:T(8,128)S(1)}, u32[]{:S(2)}, u32[]{:S(2)}) collective-permute-start(f32[32,512]{1,0:T(8,128)S(1)} %get-tuple-element.15), channel_id=1, source_target_pairs={{0,28},{4,8},{8,4},{12,16},{16,12},{20,24},{24,20},{28,0},{1,29},{... | collective-permute-start | bytes 196616 | tf_op jit(solution)/shard_map/ppermute | solution.py:355
  8.3 1.4 %collective-permute-start.1 = (f32[96,512]{1,0:T(8,128)S(1)}, f32[96,512]{1,0:T(8,128)S(1)}, u32[]{:S(2)}, u32[]{:S(2)}) collective-permute-start(f32[96,512]{1,0:T(8,128)S(1)} %get-tuple-element.14), channel_id=1, source_target_pairs={{0,4},{4,0},{8,12},{12,8},{16,20},{20,16},{24,28},{28,24},{1,5},{5... | collective-permute-start | bytes 589832 | tf_op jit(solution)/shard_map/ppermute | solution.py:343
  9.8 14.2 %collective-permute-start.3 = (f32[64,512]{1,0:T(8,128)S(1)}, f32[64,512]{1,0:T(8,128)S(1)}, u32[]{:S(2)}, u32[]{:S(2)}) collective-permute-start(f32[64,512]{1,0:T(8,128)S(1)} %pad_maximum_fusion.1), channel_id=1, source_target_pairs={{0,16},{4,20},{8,24},{12,28},{16,0},{20,4},{24,8},{28,12},{1,17},{... | collective-permute-start | bytes 393224 | tf_op jit(solution)/shard_map/ppermute | solution.py:343
  11.0 11.2 %collective-permute-start.2 = (f32[64,512]{1,0:T(8,128)S(1)}, f32[64,512]{1,0:T(8,128)S(1)}, u32[]{:S(2)}, u32[]{:S(2)}) collective-permute-start(f32[64,512]{1,0:T(8,128)S(1)} %pad_maximum_fusion), channel_id=1, source_target_pairs={{0,8},{4,12},{8,0},{12,4},{16,24},{20,28},{24,16},{28,20},{1,9},{5... | collective-permute-start | bytes 393224 | tf_op jit(solution)/shard_map/ppermute | solution.py:343
  11.4 12.6 %collective-permute-start.4 = (f32[64,512]{1,0:T(8,128)S(1)}, f32[64,512]{1,0:T(8,128)S(1)}, u32[]{:S(2)}, u32[]{:S(2)}) collective-permute-start(f32[64,512]{1,0:T(8,128)S(1)} %pad_maximum_fusion.2), channel_id=1, source_target_pairs={{0,24},{4,28},{8,16},{12,20},{16,8},{20,12},{24,0},{28,4},{1,25},{... | collective-permute-start | bytes 393224 | tf_op jit(solution)/shard_map/ppermute | solution.py:343
  22.2 9.5 %collective-permute-start = (f32[2,64,512]{2,1,0:T(8,128)S(1)}, f32[2,64,512]{2,1,0:T(8,128)S(1)}, u32[]{:S(2)}, u32[]{:S(2)}) collective-permute-start(f32[2,64,512]{2,1,0:T(8,128)S(1)} %get-tuple-element.11), channel_id=1, source_target_pairs={{0,2},{2,0},{1,3},{3,1},{4,6},{6,4},{5,7},{7,5},{8,10},{10,8},{9,1... | collective-permute-start | bytes 786440 | tf_op jit(solution)/shard_map/ppermute | solution.py:348
  24.1 7.7 %collective-permute-start.5 = (f32[64,512]{1,0:T(8,128)S(1)}, f32[64,512]{1,0:T(8,128)S(1)}, u32[]{:S(2)}, u32[]{:S(2)}) collective-permute-start(f32[64,512]{1,0:T(8,128)S(1)} %fusion.1.own), channel_id=1, source_target_pairs={{0,4},{4,0},{8,12},{12,8},{16,20},{20,16},{24,28},{28,24},{1,5},{5... | collective-permute-start | bytes 393224 | tf_op jit(solution)/shard_map/ppermute | solution.py:343
  24.2 6.4 %copy-start.2 = (s32[1,8,8]{2,1,0:T(8,128)S(1)}, s32[1,8,8]{2,1,0:T(8,128)}, u32[]{:S(2)}) copy-start(s32[1,8,8]{2,1,0:T(8,128)} %param.15) | copy-start | bytes 772

commit v5 on v4

--- a/solution.py
+++ b/solution.py
@@ -149,7 +149,7 @@
     face.wait()
 
 
-def stencil(source, swirl, mask, flags, near, shift, column_low, column_high, out, fields, levels, sem):
+def stencil(source, swirl, mask, flags, near, column_low, column_high, out, fields, levels, sem):
     azi, rad = lax.axis_index("azi"), lax.axis_index("rad")
     last_rad = lax.axis_size("rad") - 1
     count, cells, depth, width = fields.shape
@@ -210,9 +210,8 @@
     def halo(use_near):
         def value(c, h, l):
             _, lanes = cut(h, l)
-            a = near[base + c * depth + h * SUB : base + c * depth + (h + 1) * SUB, lanes]
-            b = shift[c * depth + h * SUB : c * depth + (h + 1) * SUB, lanes]
-            return jnp.where(use_near, a, b)
+            first = base + c * depth + h * SUB
+            return jnp.where(use_near, near[first : first + SUB, lanes], 0.0)
 
         return value
 
@@ -249,7 +248,7 @@
                     feed[pl.ds(at, 1), :] += block[r : r + 1, :]
 
 
-def finish(chunk, length, axial_low, axial_high, row_top, own, other, weights, feed, before, out, modes, high, result, sem):
+def finish(chunk, length, far, speed, axial_low, axial_high, row_top, own, other, weights, feed, before, out, modes, high, result, sem):
     azi, ax = lax.axis_index("azi"), lax.axis_index("ax")
     last_ax = lax.axis_size("ax") - 1
     count, cells, depth, width = before.shape
@@ -292,6 +291,12 @@
                     result[c, t, SUB : depth - SUB] = before[c, t, SUB : depth - SUB]
                 tail = before[c, t, depth - SUB :]
                 result[c, t, depth - SUB :] = tail + jnp.where(row == SUB - 1, high_rows[i : i + 1], 0.0)
+                if t in (0, cells - 1):
+                    layer = far[c * depth : (c + 1) * depth]
+                    if t:
+                        result[c, t] += jnp.where(parity == 1, 0.1 * layer, 0.0)
+                    else:
+                        result[c, t] += jnp.where(parity == 0, (speed[...] + 0.1) * layer, 0.0)
             cells_at = pl.ds(b * group, group)
             copy = pltpu.make_async_copy(result.at[c, cells_at], out.at[c, cells_at], sem.at[c, b])
             copy.start()
@@ -368,7 +373,7 @@
     before = pl.pallas_call(
         stencil,
         out_shape=struct(fields.shape, f32),
-        in_specs=[HBM] + [VMEM] * 7,
+        in_specs=[HBM] + [VMEM] * 6,
         out_specs=VMEM,
         scratch_shapes=[
             pltpu.VMEM(fields.shape, f32),
@@ -378,7 +383,7 @@
         compiler_params=params(12),
         cost_estimate=cost(1 << 28, 1 << 23),
         name="stencil",
-    )(in_hbm(fields), swirl_speed, ghost_mask, tile_flags, near, far, edge_low, edge_high)
+    )(in_hbm(fields), swirl_speed, ghost_mask, tile_flags, near, edge_low, edge_high)
 
     feed = pl.pallas_call(
         functools.partial(feed_rows, slots),
@@ -395,7 +400,7 @@
     return pl.pallas_call(
         functools.partial(finish, chunk, length),
         out_shape=struct(fields.shape, f32),
-        in_specs=[VMEM] * 8,
+        in_specs=[VMEM] * 10,
         out_specs=HBM,
         scratch_shapes=[
             pltpu.VMEM((count * modes, width), f32),
@@ -406,7 +411,7 @@
         compiler_params=params(16),
         cost_estimate=cost(1 << 26, 1 << 23),
         name="finish",
-    )(axial_low, axial_high, row_top, summed, other, weights, feed, before)
+    )(far, swirl_speed[0], axial_low, axial_high, row_top, summed, other, weights, feed, before)
 
 
 def solution(mesh):

time: 34.1 us -> 34.1 us (level)
  no operation moved by 1% of the time
where the time goes in v5:
time: 34.1 us; the launch traced here: 33.9 us
  starting transfers between devices  12.2 us (36%)
  Pallas kernels  11.9 us (35%)
  waiting for transfers between devices  8.83 us (26%)
  other arithmetic  0.63 us (2%)
    ppermute x5, waiting for transfers between devices, swap(): return lax.ppermute(x, 'azi', [(i, i ^ k) for i in range(sectors)])  8.83 us
    pallas_call x1, Pallas kernels, body(): pl.pallas_call(stencil, out_shape=struct(fields.shape, f32), in_specs=[HB...  6.31 us
    ppermute x2, starting transfers between devices, across(): received = lax.ppermute(to_only, axis, [(0, 1), (1, 0)])  4.76 us
    ppermute x5, starting transfers between devices, swap(): return lax.ppermute(x, 'azi', [(i, i ^ k) for i in range(sectors)])  4.66 us
    ppermute x1, starting transfers between devices, body(): far = lax.ppermute(shift, 'azi', offset)  2.76 us
    pallas_call x1, Pallas kernels, body(): pl.pallas_call(functools.partial(prepare, chunk), out_shape=(struct((pair...  2.25 us
    pallas_call x1, Pallas kernels, body(): pl.pallas_call(functools.partial(finish, chunk, length), out_shape=struct...  2.21 us
    pallas_call x1, Pallas kernels, body(): pl.pallas_call(functools.partial(feed_rows, slots), out_shape=struct((cel...  1.16 us
  transfers between devices with their start and end apart: 8, of which 2 were waited for; matrix products, arithmetic and copies ran while one was open for 2% of the time, Pallas kernels for 22%

profile of v5, /device:TPU:0, one launch (start us, length us, event | category | flops | bytes accessed | tf_op | source)
XLA Modules:
  0.0 33.9 jit_solution(8413289054359086240)
XLA Ops:
  0.0 0.2 fusion.11
  0.2 0.0 copy-start.4
  0.2 0.0 copy-start.1
  0.2 2.3 %prepare.1 = (f32[64,512]{1,0:T(8,128)S(1)}, f32[96,512]{1,0:T(8,128)S(1)}, f32[32,512]{1,0:T(8,128)S(1)}, f32[2,64,512]{2,1,0:T(8,128)S(1)}, f32[2,64,512]{2,1,0:T(8,128)S(1)}, /*index=5*/f32[1,2,8,128]{3,2,1,0:T(8,128)S(1)}) custom-call(f32[2,64,16,512]{3,2,1,0:T(8,128)} %source.1, f32[64,64]{1,0:T(8,128)S(1)} %pad_maximum_fusion.3.phase, f32[8,8]{1,0:T(8,128)} %bitcast.9, ...), custom_call_target="tpu_custom_call" | custom-call | flops 67108864 | bytes 2097152 | tf_op jit(solution)/shard_map/prepare/pallas_call | solution.py:324
  2.5 0.0 copy-start
  2.5 0.0 copy-start.3
  2.5 3.0 %collective-permute-start.7 = (f32[2,8,128]{2,1,0:T(8,128)S(1)}, f32[2,8,128]{2,1,0:T(8,128)S(1)}, u32[]{:S(2)}, u32[]{:S(2)}) collective-permute-start(f32[2,8,128]{2,1,0:T(8,128)S(1)} %bitcast.7), channel_id=1, source_target_pairs={{0,1},{1,0},{2,3},{3,2},{4,5},{5,4},{6,7},{7,6},{8,9},{9,8},{10,11... | collective-permute-start | bytes 24584 | tf_op jit(solution)/shard_map/ppermute | solution.py:353
  5.5 2.8 %collective-permute-start = (f32[32,512]{1,0:T(8,128)S(1)}, f32[32,512]{1,0:T(8,128)S(1)}, u32[]{:S(2)}, u32[]{:S(2)}) collective-permute-start(f32[32,512]{1,0:T(8,128)S(1)} %get-tuple-element.11), channel_id=1, source_target_pairs={{0,28},{4,8},{8,4},{12,16},{16,12},{20,24},{24,20},{28,0},{1,29},{... | collective-permute-start | bytes 196616 | tf_op jit(solution)/shard_map/ppermute | solution.py:360
  8.3 0.0 collective-permute-start.2
  8.3 0.2 fusion.9
  8.5 0.0 copy-done.4
  8.5 0.1 pad_maximum_fusion.5
  8.6 0.1 pad_maximum_fusion.4
  8.7 1.1 %collective-permute-done.2.near = f32[96,512]{1,0:T(8,128)S(1)} collective-permute-done((f32[96,512]{1,0:T(8,128)S(1)}, f32[96,512]{1,0:T(8,128)S(1)}, u32[]{:S(2)}, u32[]{:S(2)}) %collective-permute-start.2) | collective-permute-done | bytes 196640 | tf_op jit(solution)/shard_map/ppermute | solution.py:348
  9.8 1.2 %collective-permute-start.4 = (f32[64,512]{1,0:T(8,128)S(1)}, f32[64,512]{1,0:T(8,128)S(1)}, u32[]{:S(2)}, u32[]{:S(2)}) collective-permute-start(f32[64,512]{1,0:T(8,128)S(1)} %pad_maximum_fusion.1), channel_id=1, source_target_pairs={{0,16},{4,20},{8,24},{12,28},{16,0},{20,4},{24,8},{28,12},{1,17},{... | collective-permute-start | bytes 393224 | tf_op jit(solution)/shard_map/ppermute | solution.py:348
  11.0 0.3 collective-permute-start.3
  11.4 3.0 %collective-permute-start.5 = (f32[64,512]{1,0:T(8,128)S(1)}, f32[64,512]{1,0:T(8,128)S(1)}, u32[]{:S(2)}, u32[]{:S(2)}) collective-permute-start(f32[64,512]{1,0:T(8,128)S(1)} %pad_maximum_fusion.2), channel_id=1, source_target_pairs={{0,24},{4,28},{8,16},{12,20},{16,8},{20,12},{24,0},{28,4},{1,25},{... | collective-permute-start | bytes 393224 | tf_op jit(solution)/shard_map/ppermute | solution.py:348
  14.4 7.8 %collective-permute-done.3.refs_1_ = f32[64,512]{1,0:T(8,128)S(1)} collective-permute-done((f32[64,512]{1,0:T(8,128)S(1)}, f32[64,512]{1,0:T(8,128)S(1)}, u32[]{:S(2)}, u32[]{:S(2)}) %collective-permute-start.3) | collective-permute-done | bytes 131104 | tf_op jit(solution)/shard_map/ppermute | solution.py:348
  22.2 1.7 %collective-permute-start.1 = (f32[2,64,512]{2,1,0:T(8,128)S(1)}, f32[2,64,512]{2,1,0:T(8,128)S(1)}, u32[]{:S(2)}, u32[]{:S(2)}) collective-permute-start(f32[2,64,512]{2,1,0:T(8,128)S(1)} %get-tuple-element.12), channel_id=1, source_target_pairs={{0,2},{2,0},{1,3},{3,1},{4,6},{6,4},{5,7},{7,5},{8,10},{10,8},{9,1... | collective-permute-start | bytes 786440 | tf_op jit(solution)/shard_map/ppermute | solution.py:353
  23.9 0.0 collective-permute-done.5.refs_3_
  24.0 0.0 collective-permute-done.4.refs_2_
  24.1 0.1 collective-permute-start.6
  24.1 0.0 copy-done
  24.2 0.0 copy-start.2
  24.2 0.0 collective-permute-done.7.column_low.column_high
  24.2 0.0 copy-done.1
  24.2 0.0 copy-done.3
  24.2 6.3 %stencil.1.before = f32[2,64,16,512]{3,2,1,0:T(8,128)S(1)} custom-call(f32[2,64,16,512]{3,2,1,0:T(8,128)} %source.1, f32[64,16,512]{2,1,0:T(8,128)S(1)} %copy-done, s32[64,16,512]{2,1,0:T(8,128)S(1)} %copy-done.1, s32[4,16]{1,0:T(4,128)S(1)} %copy-done.3, f32[96,512]{1,0:T(8,128)S(1)} %collective-permute-done.2.near, ...), custom_call_target="tpu_custom_call" | custom-call | flops 268435456 | bytes 8388608 | tf_op jit(solution)/shard_map/stencil/pallas_call | solution.py:373
  30.5 0.0 copy-done.2
  30.5 1.2 %feed.1 = f32[520,512]{1,0:T(8,128)S(1)} custom-call(s32[8,8]{1,0:T(8,128)S(1)} %bitcast.6, f32[64,512]{1,0:T(8,128)S(1)} %slice_add_fusion.refs_0_, f32[64,512]{1,0:T(8,128)S(1)} %collective-permute-done.3.refs_1_, f32[64,512]{1,0:T(8,128)S(1)} %collective-permute-done.4.refs_2_, f32[64,512]{1,0:T(8,128)S(1)} %collective-permute-done.5.refs_3_), custom_call_target="tpu_custom_call" | custom-call | flops 33554432 | bytes 1048576 | tf_op jit(solution)/shard_map/feed/pallas_call | solution.py:388
  31.7 0.0 collective-permute-done.far
  31.7 0.0 collective-permute-done.1.axial_low.axial_high
  31.7 0.0 collective-permute-done.6.other
  31.7 2.2 %finish.1 = f32[2,64,16,512]{3,2,1,0:T(8,128)} custom-call(f32[32,512]{1,0:T(8,128)S(1)} %collective-permute-done.far, f32[16,512]{1,0:T(8,128)S(1)} %slice_bitcast_fusion.speed, f32[2,64,512]{2,1,0:T(8,128)S(1)} %collective-permute-done.1.axial_low.axial_high, f32[2,64,512]{2,1,0:T(8,128)S(1)} %collective-permute-done.1.axial_low.axial_high, ...), custom_call_target="tpu_custom_call" | custom-call | flops 67108864 | bytes 8388608 | tf_op jit(solution)/shard_map/finish/pallas_call | solution.py:400
  (18 shorter events, 0.2 us)
Async XLA Ops:
  0.2 8.3 %copy-start.4 = (f32[2,32]{1,0:T(2,128)S(1)}, f32[2,32]{1,0:T(2,128)}, u32[]{:S(2)}) copy-start(f32[2,32]{1,0:T(2,128)} %param.12) | copy-start | bytes 772
  0.2 24.0 %copy-start.1 = (s32[64,16,512]{2,1,0:T(8,128)S(1)}, s32[64,16,512]{2,1,0:T(8,128)}, u32[]{:S(2)}) copy-start(s32[64,16,512]{2,1,0:T(8,128)} %mask.1) | copy-start | bytes 6291460
  2.5 21.7 %copy-start = (f32[64,16,512]{2,1,0:T(8,128)S(1)}, f32[64,16,512]{2,1,0:T(8,128)}, u32[]{:S(2)}) copy-start(f32[64,16,512]{2,1,0:T(8,128)} %swirl.1) | copy-start | bytes 6291460
  2.5 21.7 %copy-start.3 = (s32[4,16]{1,0:T(4,128)S(1)}, s32[4,16]{1,0:T(4,128)}, u32[]{:S(2)}) copy-start(s32[4,16]{1,0:T(4,128)} %flags.1) | copy-start | bytes 772
  2.5 21.7 %collective-permute-start.7 = (f32[2,8,128]{2,1,0:T(8,128)S(1)}, f32[2,8,128]{2,1,0:T(8,128)S(1)}, u32[]{:S(2)}, u32[]{:S(2)}) collective-permute-start(f32[2,8,128]{2,1,0:T(8,128)S(1)} %bitcast.7), channel_id=1, source_target_pairs={{0,1},{1,0},{2,3},{3,2},{4,5},{5,4},{6,7},{7,6},{8,9},{9,8},{10,11... | collective-permute-start | bytes 24584 | tf_op jit(solution)/shard_map/ppermute | solution.py:353
  5.5 26.2 %collective-permute-start = (f32[32,512]{1,0:T(8,128)S(1)}, f32[32,512]{1,0:T(8,128)S(1)}, u32[]{:S(2)}, u32[]{:S(2)}) collective-permute-start(f32[32,512]{1,0:T(8,128)S(1)} %get-tuple-element.11), channel_id=1, source_target_pairs={{0,28},{4,8},{8,4},{12,16},{16,12},{20,24},{24,20},{28,0},{1,29},{... | collective-permute-start | bytes 196616 | tf_op jit(solution)/shard_map/ppermute | solution.py:360
  8.3 1.4 %collective-permute-start.2 = (f32[96,512]{1,0:T(8,128)S(1)}, f32[96,512]{1,0:T(8,128)S(1)}, u32[]{:S(2)}, u32[]{:S(2)}) collective-permute-start(f32[96,512]{1,0:T(8,128)S(1)} %get-tuple-element.15), channel_id=1, source_target_pairs={{0,4},{4,0},{8,12},{12,8},{16,20},{20,16},{24,28},{28,24},{1,5},{5... | collective-permute-start | bytes 589832 | tf_op jit(solution)/shard_map/ppermute | solution.py:348
  9.8 14.2 %collective-permute-start.4 = (f32[64,512]{1,0:T(8,128)S(1)}, f32[64,512]{1,0:T(8,128)S(1)}, u32[]{:S(2)}, u32[]{:S(2)}) collective-permute-start(f32[64,512]{1,0:T(8,128)S(1)} %pad_maximum_fusion.1), channel_id=1, source_target_pairs={{0,16},{4,20},{8,24},{12,28},{16,0},{20,4},{24,8},{28,12},{1,17},{... | collective-permute-start | bytes 393224 | tf_op jit(solution)/shard_map/ppermute | solution.py:348
  11.0 11.2 %collective-permute-start.3 = (f32[64,512]{1,0:T(8,128)S(1)}, f32[64,512]{1,0:T(8,128)S(1)}, u32[]{:S(2)}, u32[]{:S(2)}) collective-permute-start(f32[64,512]{1,0:T(8,128)S(1)} %pad_maximum_fusion), channel_id=1, source_target_pairs={{0,8},{4,12},{8,0},{12,4},{16,24},{20,28},{24,16},{28,20},{1,9},{5... | collective-permute-start | bytes 393224 | tf_op jit(solution)/shard_map/ppermute | solution.py:348
  11.4 12.6 %collective-permute-start.5 = (f32[64,512]{1,0:T(8,128)S(1)}, f32[64,512]{1,0:T(8,128)S(1)}, u32[]{:S(2)}, u32[]{:S(2)}) collective-permute-start(f32[64,512]{1,0:T(8,128)S(1)} %pad_maximum_fusion.2), channel_id=1, source_target_pairs={{0,24},{4,28},{8,16},{12,20},{16,8},{20,12},{24,0},{28,4},{1,25},{... | collective-permute-start | bytes 393224 | tf_op jit(solution)/shard_map/ppermute | solution.py:348
  22.2 9.5 %collective-permute-start.1 = (f32[2,64,512]{2,1,0:T(8,128)S(1)}, f32[2,64,512]{2,1,0:T(8,128)S(1)}, u32[]{:S(2)}, u32[]{:S(2)}) collective-permute-start(f32[2,64,512]{2,1,0:T(8,128)S(1)} %get-tuple-element.12), channel_id=1, source_target_pairs={{0,2},{2,0},{1,3},{3,1},{4,6},{6,4},{5,7},{7,5},{8,10},{10,8},{9,1... | collective-permute-start | bytes 786440 | tf_op jit(solution)/shard_map/ppermute | solution.py:353
  24.1 7.7 %collective-permute-start.6 = (f32[64,512]{1,0:T(8,128)S(1)}, f32[64,512]{1,0:T(8,128)S(1)}, u32[]{:S(2)}, u32[]{:S(2)}) collective-permute-start(f32[64,512]{1,0:T(8,128)S(1)} %fusion.1.own), channel_id=1, source_target_pairs={{0,4},{4,0},{8,12},{12,8},{16,20},{20,16},{24,28},{28,24},{1,5},{5... | collective-permute-start | bytes 393224 | tf_op jit(solution)/shard_map/ppermute | solution.py:348
  24.2 6.4 %copy-start.2 = (s32[1,8,8]{2,1,0:T(8,128)S(1)}, s32[1,8,8]{2,1,0:T(8,128)}, u32[]{:S(2)}) copy-start(s32[1,8,8]{2,1,0:T(8,128)} %param.15) | copy-start | bytes 772

commit v6 on v5

--- a/solution.py
+++ b/solution.py
@@ -149,10 +149,10 @@
     face.wait()
 
 
-def stencil(source, swirl, mask, flags, near, column_low, column_high, out, fields, levels, sem):
+def stencil(begin, end, source, swirl, inert, flags, near, column_low, column_high, out, rows, mask, levels, sem):
     azi, rad = lax.axis_index("azi"), lax.axis_index("rad")
     last_rad = lax.axis_size("rad") - 1
-    count, cells, depth, width = fields.shape
+    count, cells, depth, width = source.shape
     base = near.shape[0] - count * depth
     parity = azi % 2
     halves = depth // SUB
@@ -162,10 +162,17 @@
     at_left, at_right = lane == 0, lane == LANES - 1
     at_low, at_high = row == 0, row == SUB - 1
     has_left, has_right = rad > 0, rad < last_rad
-    pieces = [slice(k * TILE, (k + 1) * TILE) for k in range(cells // TILE)]
-    copies = [pltpu.make_async_copy(source.at[:, p], fields.at[:, p], sem.at[k]) for k, p in enumerate(pieces)]
-    for copy in copies:
-        copy.start()
+    low_row, high_row = max(begin - 1, 0), min(end + 1, cells)
+    middle = begin + (end - begin) // 2
+    cuts = [low_row, middle + 1, high_row]
+    copies = []
+    for k, (a, b) in enumerate(zip(cuts, cuts[1:])):
+        piece = rows.at[:, a - low_row : b - low_row]
+        copies.append(pltpu.make_async_copy(source.at[:, a:b], piece, sem.at[k]))
+    for k, (a, b) in enumerate(((begin, middle), (middle, end))):
+        copies.append(pltpu.make_async_copy(inert.at[a:b], mask.at[a - begin : b - begin], sem.at[2 + k]))
+    for k in (0, 2, 1, 3):
+        copies[k].start()
     turned = (0.5 * flags[...].astype(f32)).T
     for k in range(cells // TILE):
         levels[k] = jnp.broadcast_to(turned[:, k : k + 1], (depth, LANES))
@@ -184,7 +191,7 @@
                     jnp.where(has_left, pltpu.roll(column_low[g], (LANES - j) % LANES, 1), 0.0),
                     jnp.where(has_right, pltpu.roll(column_high[g], LANES - 1 - j, 1), 0.0),
                 ))
-            parts = [[fields[(c, t) + cut(h, l)] for l in range(blocks)] for h in range(halves)]
+            parts = [[rows[(c, t - low_row) + cut(h, l)] for l in range(blocks)] for h in range(halves)]
             ups = [[pltpu.roll(v, 1, 1) for v in p] for p in parts]
             downs = [[pltpu.roll(v, LANES - 1, 1) for v in p] for p in parts]
             for l in range(blocks):
@@ -199,13 +206,13 @@
                     speed = swirl[(t,) + cut(h, l)]
                     value = parts[h][l] * (0.4 - speed) + before(c, h, l) * (speed + 0.1) + 0.1 * total
                     if c == 0:
-                        out[(0, t) + cut(h, l)] = value
+                        out[(0, t - begin) + cut(h, l)] = value
                     else:
-                        live = jnp.where(mask[(t,) + cut(h, l)] == 0, level[h * SUB : (h + 1) * SUB], 0.0) * parts[h][l]
-                        energy = fields[(0, t) + cut(h, l)]
+                        live = jnp.where(mask[(t - begin,) + cut(h, l)] == 0, level[h * SUB : (h + 1) * SUB], 0.0) * parts[h][l]
+                        energy = rows[(0, t - low_row) + cut(h, l)]
                         burn = live + live * jnp.tanh(2.0 * energy - 1.0)
-                        out[(0, t) + cut(h, l)] += burn
-                        out[(1, t) + cut(h, l)] = value - 0.5 * burn
+                        out[(0, t - begin) + cut(h, l)] += burn
+                        out[(1, t - begin) + cut(h, l)] = value - 0.5 * burn
 
     def halo(use_near):
         def value(c, h, l):
@@ -216,19 +223,22 @@
         return value
 
     def inside(t):
-        return lambda c, h, l: fields[(c, t) + cut(h, l)]
+        return lambda c, h, l: rows[(c, t - low_row) + cut(h, l)]
 
     def step(t, carry):
         slab(t, inside(t - 1), inside(t + 1))
         return carry
 
     copies[0].wait()
-    slab(0, halo(parity == 1), inside(1))
-    for k, copy in enumerate(copies):
-        if k:
-            copy.wait()
-        lax.fori_loop(k * TILE - 1 if k else 1, (k + 1) * TILE - 1, step, 0, unroll=UNROLL)
-    slab(cells - 1, inside(cells - 2), halo(parity == 0))
+    copies[2].wait()
+    if begin == 0:
+        slab(0, halo(parity == 1), inside(1))
+    lax.fori_loop(max(begin, 1), middle, step, 0, unroll=UNROLL)
+    copies[1].wait()
+    copies[3].wait()
+    lax.fori_loop(middle, min(end, cells - 1), step, 0, unroll=UNROLL)
+    if end == cells:
+        slab(cells - 1, inside(cells - 2), halo(parity == 0))
 
 
 def feed_rows(slots, targets, *refs):
@@ -248,18 +258,21 @@
                     feed[pl.ds(at, 1), :] += block[r : r + 1, :]
 
 
-def finish(chunk, length, far, speed, axial_low, axial_high, row_top, own, other, weights, feed, before, out, modes, high, result, sem):
+def finish(chunk, length, far, speed, axial_low, axial_high, row_top, own, other, weights, feed, before_a, before_b, out, modes, high, result, sem):
     azi, ax = lax.axis_index("azi"), lax.axis_index("ax")
     last_ax = lax.axis_size("ax") - 1
-    count, cells, depth, width = before.shape
-    parity = azi % 2
+    count, cells, depth, width = result.shape
+    parity, fold = azi % 2, azi // 2 % 2
     pairs = own.shape[0] // chunk
+    split = before_a.shape[1]
 
     @pl.when(ax == last_ax)
     def _():
         for k in range(pairs):
+            j, same = k % (pairs // 2), k < pairs // 2
+            chip = 2 * j + (fold if same else 1 - fold)
             for ref, p in ((own, parity), (other, 1 - parity)):
-                at = pl.multiple_of((2 * k + p) * length, SUB)
+                at = pl.multiple_of((2 * chip + p) * length, SUB)
                 modes[pl.ds(at, length)] = ref[k * chunk : k * chunk + length]
         per = modes.shape[0] // count
         for c in range(count):
@@ -283,13 +296,14 @@
             high_rows = high[c, b * group : (b + 1) * group]
             for i in range(group):
                 t = b * group + i
-                head = before[c, t, :SUB] + jnp.where(row == 0, low_rows[i : i + 1], 0.0)
+                before, u = (before_a, t) if t < split else (before_b, t - split)
+                head = before[c, u, :SUB] + jnp.where(row == 0, low_rows[i : i + 1], 0.0)
                 if c == 1:
                     head = head + feed[t * SUB : (t + 1) * SUB]
                 result[c, t, :SUB] = head
                 if depth > 2 * SUB:
-                    result[c, t, SUB : depth - SUB] = before[c, t, SUB : depth - SUB]
-                tail = before[c, t, depth - SUB :]
+                    result[c, t, SUB : depth - SUB] = before[c, u, SUB : depth - SUB]
+                tail = before[c, u, depth - SUB :]
                 result[c, t, depth - SUB :] = tail + jnp.where(row == SUB - 1, high_rows[i : i + 1], 0.0)
                 if t in (0, cells - 1):
                     layer = far[c * depth : (c + 1) * depth]
@@ -306,7 +320,7 @@
 
 
 def body(fields, swirl_speed, ghost_mask, tile_flags, outlet_gain, feed_rate, plenum, feed_target):
-    sectors, radials = lax.axis_size("azi"), lax.axis_size("rad")
+    sectors, slabs, radials = lax.axis_size("azi"), lax.axis_size("ax"), lax.axis_size("rad")
     count, cells, depth, width = fields.shape
     half_modes = outlet_gain.shape[1]
     modes = 2 * half_modes
@@ -363,27 +377,44 @@
 
     mixed = keep + near[: pairs * chunk]
     parts = [mixed[k * chunk : (k + 1) * chunk] for k in range(pairs)]
-    arrived = [mixed]
-    for k in range(1, pairs):
-        arrived.append(swap(jnp.concatenate(parts[k:] + parts[:k], axis=0), 2 * k))
-    summed = functools.reduce(
-        jnp.add, [mixed] + [jnp.concatenate([x[(pairs - k) * chunk :], x[: (pairs - k) * chunk]], axis=0) for k, x in enumerate(arrived) if k]
+    is_outlet = lax.axis_index("ax") == slabs - 1
+    low_bit = lax.axis_index("azi") // 2 % 2
+    even, odd = jnp.concatenate(parts[::2], axis=0), jnp.concatenate(parts[1::2], axis=0)
+
+    def carry(modes_part, k):
+        return jnp.where(is_outlet, modes_part, jnp.concatenate([parts[k]] * (pairs // 2), axis=0))
+
+    folded = swap(carry(jnp.where(low_bit == 0, odd, even), 1), 2)
+    half = jnp.where(low_bit == 0, even, odd) + folded
+    half, *outgoing = lax.optimization_barrier([half] + [carry(half, k) for k in range(1, pairs)])
+    arrived = [half]
+    for k, block in enumerate(outgoing, 1):
+        arrived.append(swap(block, 2 * k))
+    arrived = lax.optimization_barrier(arrived)
+    summed = jnp.concatenate(
+        [functools.reduce(jnp.add, arrived[0::2]), functools.reduce(jnp.add, arrived[1::2])], axis=0
     )
-
-    before = pl.pallas_call(
-        stencil,
-        out_shape=struct(fields.shape, f32),
-        in_specs=[HBM] + [VMEM] * 6,
-        out_specs=VMEM,
-        scratch_shapes=[
-            pltpu.VMEM(fields.shape, f32),
-            pltpu.VMEM((cells // TILE, depth, LANES), f32),
-            pltpu.SemaphoreType.DMA((cells // TILE,)),
-        ],
-        compiler_params=params(12),
-        cost_estimate=cost(1 << 28, 1 << 23),
-        name="stencil",
-    )(in_hbm(fields), swirl_speed, ghost_mask, tile_flags, near, edge_low, edge_high)
+    profiles = [parts[0], folded] + arrived[2:]
+
+    split = cells // 2 + 1
+    befores = []
+    for begin, end in ((0, split), (split, cells)):
+        befores.append(
+            pl.pallas_call(
+                functools.partial(stencil, begin, end),
+                out_shape=struct((count, end - begin, depth, width), f32),
+                in_specs=[HBM, VMEM, HBM] + [VMEM] * 4,
+                out_specs=VMEM,
+                scratch_shapes=[
+                    pltpu.VMEM((count, end - begin + 1, depth, width), f32),
+                    pltpu.VMEM((end - begin, depth, width), jnp.int32),
+                    pltpu.VMEM((cells // TILE, depth, LANES), f32),
+                    pltpu.SemaphoreType.DMA((4,)),
+                ],
+                compiler_params=params(8),
+                cost_estimate=cost(1 << 27, 1 << 22),
+            )(in_hbm(fields), swirl_speed, in_hbm(ghost_mask), tile_flags, near, edge_low, edge_high)
+        )
 
     feed = pl.pallas_call(
         functools.partial(feed_rows, slots),
@@ -393,14 +424,14 @@
         compiler_params=params(8),
         cost_estimate=cost(1 << 25, 1 << 20),
         name="feed",
-    )(feed_target[0], *arrived)
+    )(feed_target[0], *profiles)
 
     other = swap(summed, 1)
 
     return pl.pallas_call(
         functools.partial(finish, chunk, length),
         out_shape=struct(fields.shape, f32),
-        in_specs=[VMEM] * 10,
+        in_specs=[VMEM] * 11,
         out_specs=HBM,
         scratch_shapes=[
             pltpu.VMEM((count * modes, width), f32),
@@ -411,7 +442,7 @@
         compiler_params=params(16),
         cost_estimate=cost(1 << 26, 1 << 23),
         name="finish",
-    )(far, swirl_speed[0], axial_low, axial_high, row_top, summed, other, weights, feed, before)
+    )(far, swirl_speed[0], axial_low, axial_high, row_top, summed, other, weights, feed, *befores)
 
 
 def solution(mesh):

time: 34.1 us -> 34.4 us (level)
  Pallas kernels: 11.9 us -> 13.8 us
  waiting for transfers between devices: 8.83 us -> 7.23 us
    pallas_call x1 -> x2, Pallas kernels: 6.31 us -> 8.23 us  [body(): pl.pallas_call(functools.partial(stencil, begin, end), out_shape=struct((...]
    ppermute x5 -> x6, waiting for transfers between devices: 8.83 us -> 7.22 us  [swap(): return lax.ppermute(x, 'azi', [(i, i ^ k) for i in range(sectors)])]
    ppermute x5 -> x6, starting transfers between devices: 4.66 us -> 4.73 us  [swap(): return lax.ppermute(x, 'azi', [(i, i ^ k) for i in range(sectors)])]
  transfers between devices with their start and end apart: 8 -> 9, of which waited for: 2 -> 3; matrix products, arithmetic and copies ran while one was open for 2% -> 1% of each run, Pallas kernels for 22% -> 27%
where the time goes in v6:
time: 34.4 us; the launch traced here: 34.2 us
  Pallas kernels  13.8 us (40%)
  starting transfers between devices  12.2 us (35%)
  waiting for transfers between devices  7.23 us (21%)
  other arithmetic  0.63 us (2%)
    pallas_call x2, Pallas kernels, body(): pl.pallas_call(functools.partial(stencil, begin, end), out_shape=struct((...  8.23 us
    ppermute x6, waiting for transfers between devices, swap(): return lax.ppermute(x, 'azi', [(i, i ^ k) for i in range(sectors)])  7.22 us
    ppermute x2, starting transfers between devices, across(): received = lax.ppermute(to_only, axis, [(0, 1), (1, 0)])  4.75 us
    ppermute x6, starting transfers between devices, swap(): return lax.ppermute(x, 'azi', [(i, i ^ k) for i in range(sectors)])  4.73 us
    ppermute x1, starting transfers between devices, body(): far = lax.ppermute(shift, 'azi', offset)  2.76 us
    pallas_call x1, Pallas kernels, body(): pl.pallas_call(functools.partial(finish, chunk, length), out_shape=struct...  2.22 us
    pallas_call x1, Pallas kernels, body(): pl.pallas_call(functools.partial(prepare, chunk), out_shape=(struct((pair...  2.2 us
    pallas_call x1, Pallas kernels, body(): pl.pallas_call(functools.partial(feed_rows, slots), out_shape=struct((cel...  1.16 us
  transfers between devices with their start and end apart: 9, of which 3 were waited for; matrix products, arithmetic and copies ran while one was open for 1% of the time, Pallas kernels for 27%

profile of v6, /device:TPU:0, one launch (start us, length us, event | category | flops | bytes accessed | tf_op | source)
XLA Modules:
  0.0 34.2 jit_solution(5789839820813606368)
XLA Ops:
  0.0 0.2 fusion.13
  0.2 0.0 copy-start.3
  0.2 2.2 %prepare.1 = (f32[64,512]{1,0:T(8,128)S(1)}, f32[96,512]{1,0:T(8,128)S(1)}, f32[32,512]{1,0:T(8,128)S(1)}, f32[2,64,512]{2,1,0:T(8,128)S(1)}, f32[2,64,512]{2,1,0:T(8,128)S(1)}, /*index=5*/f32[1,2,8,128]{3,2,1,0:T(8,128)S(1)}) custom-call(f32[2,64,16,512]{3,2,1,0:T(8,128)} %source.3, f32[64,64]{1,0:T(8,128)S(1)} %pad_maximum_fusion.6.phase, f32[8,8]{1,0:T(8,128)} %bitcast.9, ...), custom_call_target="tpu_custom_call" | custom-call | flops 67108864 | bytes 2097152 | tf_op jit(solution)/shard_map/prepare/pallas_call | solution.py:338
  2.4 0.0 copy-start
  2.4 0.0 copy-start.1
  2.4 2.9 %collective-permute-start.8 = (f32[2,8,128]{2,1,0:T(8,128)S(1)}, f32[2,8,128]{2,1,0:T(8,128)S(1)}, u32[]{:S(2)}, u32[]{:S(2)}) collective-permute-start(f32[2,8,128]{2,1,0:T(8,128)S(1)} %bitcast.7), channel_id=1, source_target_pairs={{0,1},{1,0},{2,3},{3,2},{4,5},{5,4},{6,7},{7,6},{8,9},{9,8},{10,11... | collective-permute-start | bytes 24584 | tf_op jit(solution)/shard_map/ppermute | solution.py:367
  5.4 2.8 %collective-permute-start = (f32[32,512]{1,0:T(8,128)S(1)}, f32[32,512]{1,0:T(8,128)S(1)}, u32[]{:S(2)}, u32[]{:S(2)}) collective-permute-start(f32[32,512]{1,0:T(8,128)S(1)} %get-tuple-element.19), channel_id=1, source_target_pairs={{0,28},{4,8},{8,4},{12,16},{16,12},{20,24},{24,20},{28,0},{1,29},{... | collective-permute-start | bytes 196616 | tf_op jit(solution)/shard_map/ppermute | solution.py:374
  8.1 0.0 collective-permute-start.2
  8.1 0.2 fusion.11
  8.4 0.1 pad_maximum_fusion.7
  8.5 1.1 %collective-permute-done.2.near = f32[96,512]{1,0:T(8,128)S(1)} collective-permute-done((f32[96,512]{1,0:T(8,128)S(1)}, f32[96,512]{1,0:T(8,128)S(1)}, u32[]{:S(2)}, u32[]{:S(2)}) %collective-permute-start.2) | collective-permute-done | bytes 196640 | tf_op jit(solution)/shard_map/ppermute | solution.py:362
  9.6 0.2 collective-permute-start.3
  9.8 0.0 copy-done.3
  9.8 0.1 pad_maximum_fusion.8
  9.9 4.1 %collective-permute-done.3.refs_1_ = f32[32,512]{1,0:T(8,128)S(1)} collective-permute-done((f32[32,512]{1,0:T(8,128)S(1)}, f32[32,512]{1,0:T(8,128)S(1)}, u32[]{:S(2)}, u32[]{:S(2)}) %collective-permute-start.3) | collective-permute-done | bytes 65568 | tf_op jit(solution)/shard_map/ppermute | solution.py:362
  14.0 0.3 collective-permute-start.4
  14.3 2.0 %collective-permute-start.5 = (f32[32,512]{1,0:T(8,128)S(1)}, f32[32,512]{1,0:T(8,128)S(1)}, u32[]{:S(2)}, u32[]{:S(2)}) collective-permute-start(f32[32,512]{1,0:T(8,128)S(1)} %get-tuple-element.26), channel_id=1, source_target_pairs={{0,16},{4,20},{8,24},{12,28},{16,0},{20,4},{24,8},{28,12},{1,17},{... | collective-permute-start | bytes 196616 | tf_op jit(solution)/shard_map/ppermute | solution.py:362
  16.3 2.2 %collective-permute-start.6 = (f32[32,512]{1,0:T(8,128)S(1)}, f32[32,512]{1,0:T(8,128)S(1)}, u32[]{:S(2)}, u32[]{:S(2)}) collective-permute-start(f32[32,512]{1,0:T(8,128)S(1)} %get-tuple-element.27), channel_id=1, source_target_pairs={{0,24},{4,28},{8,16},{12,20},{16,8},{20,12},{24,0},{28,4},{1,25},{... | collective-permute-start | bytes 196616 | tf_op jit(solution)/shard_map/ppermute | solution.py:362
  18.5 0.0 collective-permute-done.4
  18.5 1.8 %collective-permute-start.1 = (f32[2,64,512]{2,1,0:T(8,128)S(1)}, f32[2,64,512]{2,1,0:T(8,128)S(1)}, u32[]{:S(2)}, u32[]{:S(2)}) collective-permute-start(f32[2,64,512]{2,1,0:T(8,128)S(1)} %get-tuple-element.20), channel_id=1, source_target_pairs={{0,2},{2,0},{1,3},{3,1},{4,6},{6,4},{5,7},{7,5},{8,10},{10,8},{9,1... | collective-permute-start | bytes 786440 | tf_op jit(solution)/shard_map/ppermute | solution.py:367
  20.3 0.0 collective-permute-done.5.refs_2_
  20.3 2.1 %collective-permute-done.6.refs_3_ = f32[32,512]{1,0:T(8,128)S(1)} collective-permute-done((f32[32,512]{1,0:T(8,128)S(1)}, f32[32,512]{1,0:T(8,128)S(1)}, u32[]{:S(2)}, u32[]{:S(2)}) %collective-permute-start.6) | collective-permute-done | bytes 65568 | tf_op jit(solution)/shard_map/ppermute | solution.py:362
  22.4 0.1 collective-permute-start.7
  22.5 0.0 copy-done
  22.5 0.0 collective-permute-done.8.column_low.column_high
  22.5 0.0 copy-done.1
  22.5 4.1 %shard_map.83.before_b = f32[2,31,16,512]{3,2,1,0:T(8,128)S(1)} custom-call(f32[2,64,16,512]{3,2,1,0:T(8,128)} %source.3, f32[64,16,512]{2,1,0:T(8,128)S(1)} %copy-done, s32[64,16,512]{2,1,0:T(8,128)} %inert.3, s32[4,16]{1,0:T(4,128)S(1)} %copy-done.1, f32[96,512]{1,0:T(8,128)S(1)} %collective-permute-done.2.near, ...), custom_call_target="tpu_custom_call" | custom-call | flops 134217728 | bytes 4194304 | tf_op jit(solution)/shard_map/pallas_call | solution.py:403
  26.6 0.0 copy-start.2
  26.6 4.2 %shard_map.82.before_a = f32[2,33,16,512]{3,2,1,0:T(8,128)S(1)} custom-call(f32[2,64,16,512]{3,2,1,0:T(8,128)} %source.3, f32[64,16,512]{2,1,0:T(8,128)S(1)} %copy-done, s32[64,16,512]{2,1,0:T(8,128)} %inert.3, s32[4,16]{1,0:T(4,128)S(1)} %copy-done.1, f32[96,512]{1,0:T(8,128)S(1)} %collective-permute-done.2.near, ...), custom_call_target="tpu_custom_call" | custom-call | flops 134217728 | bytes 4194304 | tf_op jit(solution)/shard_map/pallas_call | solution.py:403
  30.8 0.0 copy-done.2
  30.8 1.2 %feed.1 = f32[520,512]{1,0:T(8,128)S(1)} custom-call(s32[8,8]{1,0:T(8,128)S(1)} %bitcast.6, f32[16,512]{1,0:T(8,128)S(1)} %get-tuple-element.35.refs_0_, f32[32,512]{1,0:T(8,128)S(1)} %collective-permute-done.3.refs_1_, f32[32,512]{1,0:T(8,128)S(1)} %collective-permute-done.5.refs_2_, f32[32,512]{1,0:T(8,128)S(1)} %collective-permute-done.6.refs_3_), custom_call_target="tpu_custom_call" | custom-call | flops 33554432 | bytes 1048576 | tf_op jit(solution)/shard_map/feed/pallas_call | solution.py:419
  31.9 0.0 collective-permute-done.far
  32.0 0.0 collective-permute-done.1.axial_low.axial_high
  32.0 0.0 collective-permute-done.7.other
  32.0 2.2 %finish.1 = f32[2,64,16,512]{3,2,1,0:T(8,128)} custom-call(f32[32,512]{1,0:T(8,128)S(1)} %collective-permute-done.far, f32[16,512]{1,0:T(8,128)S(1)} %slice_bitcast_fusion.speed, f32[2,64,512]{2,1,0:T(8,128)S(1)} %collective-permute-done.1.axial_low.axial_high, f32[2,64,512]{2,1,0:T(8,128)S(1)} %collective-permute-done.1.axial_low.axial_high, ...), custom_call_target="tpu_custom_call" | custom-call | flops 67108864 | bytes 8388608 | tf_op jit(solution)/shard_map/finish/pallas_call | solution.py:431
  (13 shorter events, 0.1 us)
Async XLA Ops:
  0.2 9.7 %copy-start.3 = (f32[2,32]{1,0:T(2,128)S(1)}, f32[2,32]{1,0:T(2,128)}, u32[]{:S(2)}) copy-start(f32[2,32]{1,0:T(2,128)} %param.12) | copy-start | bytes 772
  2.4 20.1 %copy-start = (f32[64,16,512]{2,1,0:T(8,128)S(1)}, f32[64,16,512]{2,1,0:T(8,128)}, u32[]{:S(2)}) copy-start(f32[64,16,512]{2,1,0:T(8,128)} %swirl.3) | copy-start | bytes 6291460
  2.4 20.1 %copy-start.1 = (s32[4,16]{1,0:T(4,128)S(1)}, s32[4,16]{1,0:T(4,128)}, u32[]{:S(2)}) copy-start(s32[4,16]{1,0:T(4,128)} %flags.3) | copy-start | bytes 772
  2.4 20.1 %collective-permute-start.8 = (f32[2,8,128]{2,1,0:T(8,128)S(1)}, f32[2,8,128]{2,1,0:T(8,128)S(1)}, u32[]{:S(2)}, u32[]{:S(2)}) collective-permute-start(f32[2,8,128]{2,1,0:T(8,128)S(1)} %bitcast.7), channel_id=1, source_target_pairs={{0,1},{1,0},{2,3},{3,2},{4,5},{5,4},{6,7},{7,6},{8,9},{9,8},{10,11... | collective-permute-start | bytes 24584 | tf_op jit(solution)/shard_map/ppermute | solution.py:367
  5.4 26.6 %collective-permute-start = (f32[32,512]{1,0:T(8,128)S(1)}, f32[32,512]{1,0:T(8,128)S(1)}, u32[]{:S(2)}, u32[]{:S(2)}) collective-permute-start(f32[32,512]{1,0:T(8,128)S(1)} %get-tuple-element.19), channel_id=1, source_target_pairs={{0,28},{4,8},{8,4},{12,16},{16,12},{20,24},{24,20},{28,0},{1,29},{... | collective-permute-start | bytes 196616 | tf_op jit(solution)/shard_map/ppermute | solution.py:374
  8.1 1.4 %collective-permute-start.2 = (f32[96,512]{1,0:T(8,128)S(1)}, f32[96,512]{1,0:T(8,128)S(1)}, u32[]{:S(2)}, u32[]{:S(2)}) collective-permute-start(f32[96,512]{1,0:T(8,128)S(1)} %get-tuple-element.23), channel_id=1, source_target_pairs={{0,4},{4,0},{8,12},{12,8},{16,20},{20,16},{24,28},{28,24},{1,5},{5... | collective-permute-start | bytes 589832 | tf_op jit(solution)/shard_map/ppermute | solution.py:362
  9.6 4.3 %collective-permute-start.3 = (f32[32,512]{1,0:T(8,128)S(1)}, f32[32,512]{1,0:T(8,128)S(1)}, u32[]{:S(2)}, u32[]{:S(2)}) collective-permute-start(f32[32,512]{1,0:T(8,128)S(1)} %fusion.3), channel_id=1, source_target_pairs={{0,8},{4,12},{8,0},{12,4},{16,24},{20,28},{24,16},{28,20},{1,9},{5... | collective-permute-start | bytes 196616 | tf_op jit(solution)/shard_map/ppermute | solution.py:362
  14.0 4.5 %collective-permute-start.4 = (f32[32,512]{1,0:T(8,128)S(1)}, f32[32,512]{1,0:T(8,128)S(1)}, u32[]{:S(2)}, u32[]{:S(2)}) collective-permute-start(f32[32,512]{1,0:T(8,128)S(1)} %get-tuple-element.25), channel_id=1, source_target_pairs={{0,8},{4,12},{8,0},{12,4},{16,24},{20,28},{24,16},{28,20},{1,9},{5... | collective-permute-start | bytes 196616 | tf_op jit(solution)/shard_map/ppermute | solution.py:362
  14.3 6.0 %collective-permute-start.5 = (f32[32,512]{1,0:T(8,128)S(1)}, f32[32,512]{1,0:T(8,128)S(1)}, u32[]{:S(2)}, u32[]{:S(2)}) collective-permute-start(f32[32,512]{1,0:T(8,128)S(1)} %get-tuple-element.26), channel_id=1, source_target_pairs={{0,16},{4,20},{8,24},{12,28},{16,0},{20,4},{24,8},{28,12},{1,17},{... | collective-permute-start | bytes 196616 | tf_op jit(solution)/shard_map/ppermute | solution.py:362
  16.3 6.1 %collective-permute-start.6 = (f32[32,512]{1,0:T(8,128)S(1)}, f32[32,512]{1,0:T(8,128)S(1)}, u32[]{:S(2)}, u32[]{:S(2)}) collective-permute-start(f32[32,512]{1,0:T(8,128)S(1)} %get-tuple-element.27), channel_id=1, source_target_pairs={{0,24},{4,28},{8,16},{12,20},{16,8},{20,12},{24,0},{28,4},{1,25},{... | collective-permute-start | bytes 196616 | tf_op jit(solution)/shard_map/ppermute | solution.py:362
  18.5 13.5 %collective-permute-start.1 = (f32[2,64,512]{2,1,0:T(8,128)S(1)}, f32[2,64,512]{2,1,0:T(8,128)S(1)}, u32[]{:S(2)}, u32[]{:S(2)}) collective-permute-start(f32[2,64,512]{2,1,0:T(8,128)S(1)} %get-tuple-element.20), channel_id=1, source_target_pairs={{0,2},{2,0},{1,3},{3,1},{4,6},{6,4},{5,7},{7,5},{8,10},{10,8},{9,1... | collective-permute-start | bytes 786440 | tf_op jit(solution)/shard_map/ppermute | solution.py:367
  22.4 9.6 %collective-permute-start.7 = (f32[64,512]{1,0:T(8,128)S(1)}, f32[64,512]{1,0:T(8,128)S(1)}, u32[]{:S(2)}, u32[]{:S(2)}) collective-permute-start(f32[64,512]{1,0:T(8,128)S(1)} %pad_maximum_fusion.own), channel_id=1, source_target_pairs={{0,4},{4,0},{8,12},{12,8},{16,20},{20,16},{24,28},{28,24},{1,5},{5... | collective-permute-start | bytes 393224 | tf_op jit(solution)/shard_map/ppermute | solution.py:362
  26.6 4.2 %copy-start.2 = (s32[1,8,8]{2,1,0:T(8,128)S(1)}, s32[1,8,8]{2,1,0:T(8,128)}, u32[]{:S(2)}) copy-start(s32[1,8,8]{2,1,0:T(8,128)} %param.15) | copy-start | bytes 772

commit v7 on v5

--- a/solution.py
+++ b/solution.py
@@ -45,9 +45,9 @@
 
 
 def prepare(
-    chunk, fields, phase, rates, profile, keep, send, shift, row_top, row_out, column, rate, plenum, tile, sem
+    chunk, fields, phase, rates, profile, keep, send, shift, row_top, row_out, tile, rate, plenum, sem
 ):
-    azi, ax, rad = lax.axis_index("azi"), lax.axis_index("ax"), lax.axis_index("rad")
+    azi, ax = lax.axis_index("azi"), lax.axis_index("ax")
     last_ax = lax.axis_size("ax") - 1
     count, cells, depth, width = fields.shape
     sectors, slots, _ = profile.shape
@@ -57,11 +57,6 @@
     t_pair = jnp.where(parity == 0, cells - 1, 0)
     t_shift = jnp.where(parity == 0, 0, cells - 1)
     row_sent = jnp.where((ax == 0) & (last_ax == 1), depth - 1, 0)
-    if lax.axis_size("rad") == 2:
-        more = jnp.where(rad == 0, 1, 0)
-        sides = [(jnp.where(rad == 0, width - LANES, 0), lambda j: (j + more) if j < LANES - 1 else j * (1 - more))]
-    else:
-        sides = [(width - LANES, lambda j: (j + 1) % LANES), (0, lambda j: j)]
     first = pltpu.make_async_copy(fields.at[:, :, depth - 1, :], row_top, sem.at[0])
     first.start()
     copies = []
@@ -70,18 +65,14 @@
         copies.append(pltpu.make_async_copy(fields.at[c, t_pair], send.at[rows], sem.at[1 + 2 * c]))
         rows = slice(c * depth, (c + 1) * depth)
         copies.append(pltpu.make_async_copy(fields.at[c, t_shift], shift.at[rows], sem.at[2 + 2 * c]))
-    edges = [
-        pltpu.make_async_copy(
-            fields.at[:, :, :, pl.ds(pl.multiple_of(side, LANES), LANES)], tile.at[e], sem.at[5 + 2 * count + e]
-        )
-        for e, (side, _) in enumerate(sides)
-    ]
     for one in copies:
         one.start()
-    for edge in edges:
-        edge.start()
     face = pltpu.make_async_copy(fields.at[:, :, row_sent, :], row_out, sem.at[2 + 2 * count])
     face.start()
+    for e, (block, _) in enumerate(columns_sent(width)):
+        lanes = pl.ds(pl.multiple_of(block, LANES), LANES)
+        copies.append(pltpu.make_async_copy(fields.at[:, :, :, lanes], tile.at[e], sem.at[5 + 2 * count + e]))
+        copies[-1].start()
     supply = pltpu.make_async_copy(profile, plenum, sem.at[3 + 2 * count])
     supply.start()
     factor = pltpu.make_async_copy(rates, rate, sem.at[4 + 2 * count])
@@ -90,8 +81,6 @@
     @pl.when(ax == last_ax)
     def _():
         first.wait()
-        supply.wait()
-        factor.wait()
         sums = [
             jnp.dot(phase[...], row_top[c], precision=HIGH, preferred_element_type=f32)
             for c in range(count)
@@ -111,11 +100,12 @@
                 keep[at + length : at + chunk] = jnp.zeros((chunk - length, width), f32)
                 send[at + length : at + chunk] = jnp.zeros((chunk - length, width), f32)
 
+    supply.wait()
+    factor.wait()
+
     @pl.when(ax != last_ax)
     def _():
         first.wait()
-        supply.wait()
-        factor.wait()
         turned = rate[...].T
         for q in range(pairs):
             at = pl.multiple_of((q ^ place) * chunk, SUB)
@@ -132,10 +122,24 @@
                 keep[rest] = jnp.zeros((chunk - 2 * slots, width), f32)
                 send[rest] = jnp.zeros((chunk - 2 * slots, width), f32)
 
+    for one in copies:
+        one.wait()
+    face.wait()
+
+
+def columns_sent(width):
+    if lax.axis_size("rad") != 2:
+        return [(width - LANES, lambda j: (j + 1) % LANES), (0, lambda j: j)]
+    more = jnp.where(lax.axis_index("rad") == 0, 1, 0)
+    return [(more * (width - LANES), lambda j: (j + more) if j < LANES - 1 else j * (1 - more))]
+
+
+def columns(tile, column):
+    _, cells, depth = tile.shape[1:4]
+    sides = columns_sent(LANES)
     lane = lax.broadcasted_iota(jnp.int32, (SUB, LANES), 1)
     halves = depth // SUB
     for e, (_, by) in enumerate(sides):
-        edges[e].wait()
         for g in range(column.shape[1]):
             acc = jnp.zeros((SUB, LANES), f32)
             for j in range(LANES):
@@ -144,9 +148,6 @@
                 piece = tile[e, c, t, h * SUB : (h + 1) * SUB, :]
                 acc = jnp.where(lane == j, pltpu.roll(piece, by(j), 1), acc)
             column[e, g] = acc
-    for one in copies:
-        one.wait()
-    face.wait()
 
 
 def stencil(source, swirl, mask, flags, near, column_low, column_high, out, fields, levels, sem):
@@ -321,7 +322,8 @@
     groups = count * cells * depth // SUB // LANES
 
     struct = jax.ShapeDtypeStruct
-    keep, send, shift, row_top, row_out, column = pl.pallas_call(
+    outer = 1 if radials == 2 else 2
+    keep, send, shift, row_top, row_out, tile = pl.pallas_call(
         functools.partial(prepare, chunk),
         out_shape=(
             struct((pairs * chunk, width), f32),
@@ -329,20 +331,29 @@
             struct((count * depth, width), f32),
             struct((count, cells, width), f32),
             struct((count, cells, width), f32),
-            struct((1 if radials == 2 else 2, groups, SUB, LANES), f32),
+            struct((outer, count, cells, depth, LANES), f32),
         ),
         in_specs=[HBM, VMEM, HBM, HBM],
         out_specs=[VMEM] * 6,
         scratch_shapes=[
             pltpu.VMEM((sectors, slots), f32),
             pltpu.VMEM((sectors, slots, width), f32),
-            pltpu.VMEM((1 if radials == 2 else 2, count, cells, depth, LANES), f32),
             pltpu.SemaphoreType.DMA((2 * count + 7,)),
         ],
         compiler_params=params(12),
         cost_estimate=cost(1 << 26, 1 << 21),
         name="prepare",
     )(in_hbm(fields), phase, in_hbm(feed_rate[0]), in_hbm(plenum[0]))
+
+    column = pl.pallas_call(
+        columns,
+        out_shape=struct((outer, groups, SUB, LANES), f32),
+        in_specs=[VMEM],
+        out_specs=VMEM,
+        compiler_params=params(6),
+        cost_estimate=cost(1 << 22, 1 << 19),
+        name="columns",
+    )(tile)
 
     def swap(x, k):
         return lax.ppermute(x, "azi", [(i, i ^ k) for i in range(sectors)])

time: 34.1 us -> 33.6 us (0.985)
  starting transfers between devices: 12.2 us -> 11.8 us
    ppermute x2, starting transfers between devices: 4.76 us -> 4.33 us  [across(): received = lax.ppermute(to_only, axis, [(0, 1), (1, 0)])]
    pallas_call x1, Pallas kernels: 2.25 us -> 1.84 us  [body(): pl.pallas_call(functools.partial(prepare, chunk), out_shape=(struct((pair...]
    pallas_call x0 -> x1, Pallas kernels: none -> 0.34 us  [body(): pl.pallas_call(columns, out_shape=struct((outer, groups, SUB, LANES), f32...]
where the time goes in v7:
time: 33.6 us; the launch traced here: 33.4 us
  Pallas kernels  11.9 us (35%)
  starting transfers between devices  11.8 us (35%)
  waiting for transfers between devices  8.84 us (26%)
  other arithmetic  0.62 us (2%)
    ppermute x5, waiting for transfers between devices, swap(): return lax.ppermute(x, 'azi', [(i, i ^ k) for i in range(sectors)])  8.83 us
    pallas_call x1, Pallas kernels, body(): pl.pallas_call(stencil, out_shape=struct(fields.shape, f32), in_specs=[HB...  6.31 us
    ppermute x5, starting transfers between devices, swap(): return lax.ppermute(x, 'azi', [(i, i ^ k) for i in range(sectors)])  4.66 us
    ppermute x2, starting transfers between devices, across(): received = lax.ppermute(to_only, axis, [(0, 1), (1, 0)])  4.33 us
    ppermute x1, starting transfers between devices, body(): far = lax.ppermute(shift, 'azi', offset)  2.76 us
    pallas_call x1, Pallas kernels, body(): pl.pallas_call(functools.partial(finish, chunk, length), out_shape=struct...  2.21 us
    pallas_call x1, Pallas kernels, body(): pl.pallas_call(functools.partial(prepare, chunk), out_shape=(struct((pair...  1.84 us
    pallas_call x1, Pallas kernels, body(): pl.pallas_call(functools.partial(feed_rows, slots), out_shape=struct((cel...  1.16 us
  transfers between devices with their start and end apart: 8, of which 2 were waited for; matrix products, arithmetic and copies ran while one was open for 2% of the time, Pallas kernels for 22%

profile of v7, /device:TPU:0, one launch (start us, length us, event | category | flops | bytes accessed | tf_op | source)
XLA Modules:
  0.0 33.4 jit_solution(3918543952207748994)
XLA Ops:
  0.0 0.2 fusion.11
  0.2 0.0 copy-start.4
  0.2 1.8 %prepare.1 = (f32[64,512]{1,0:T(8,128)S(1)}, f32[96,512]{1,0:T(8,128)S(1)}, f32[32,512]{1,0:T(8,128)S(1)}, f32[2,64,512]{2,1,0:T(8,128)S(1)}, f32[2,64,512]{2,1,...) custom-call(f32[2,64,16,512]{3,2,1,0:T(8,128)} %source.1, f32[64,64]{1,0:T(8,128)S(1)} %pad_maximum_fusion.3.phase, ...), custom_call_target="tpu_custom_call" | custom-call | flops 67108864 | bytes 2097152 | tf_op jit(solution)/shard_map/prepare/pallas_call | solution.py:326
  2.0 0.0 copy-start.1
  2.0 0.3 %columns.1 = f32[1,2,8,128]{3,2,1,0:T(8,128)S(1)} custom-call(f32[1,2,64,16,128]{4,3,2,1,0:T(8,128)S(1)} %get-tuple-element.16.tile), custom_call_target="tpu_custom_call" | custom-call | flops 4194304 | bytes 524288 | tf_op jit(solution)/shard_map/columns/pallas_call | solution.py:348
  2.4 0.0 copy-start
  2.4 0.0 copy-start.3
  2.4 3.0 %collective-permute-start.7 = (f32[2,8,128]{2,1,0:T(8,128)S(1)}, f32[2,8,128]{2,1,0:T(8,128)S(1)}, u32[]{:S(2)}, u32[]{:S(2)}) collective-permute-start(f32[2,8,128]{2,1,0:T(8,128)S(1)} %bitcast.6), channel_id=1, source_target_pairs={{0,1},{1,0},{2,3},{3,2},{4,5},{5,4},{6,7},{7,6},{8,9},{9,8},{10,11... | collective-permute-start | bytes 24584 | tf_op jit(solution)/shard_map/ppermute | solution.py:364
  5.4 2.8 %collective-permute-start = (f32[32,512]{1,0:T(8,128)S(1)}, f32[32,512]{1,0:T(8,128)S(1)}, u32[]{:S(2)}, u32[]{:S(2)}) collective-permute-start(f32[32,512]{1,0:T(8,128)S(1)} %get-tuple-element.11), channel_id=1, source_target_pairs={{0,28},{4,8},{8,4},{12,16},{16,12},{20,24},{24,20},{28,0},{1,29},{... | collective-permute-start | bytes 196616 | tf_op jit(solution)/shard_map/ppermute | solution.py:371
  8.2 0.0 collective-permute-start.2
  8.2 0.2 fusion.9
  8.4 0.0 copy-done.4
  8.4 0.1 pad_maximum_fusion.5
  8.5 0.1 pad_maximum_fusion.4
  8.5 1.1 %collective-permute-done.2.near = f32[96,512]{1,0:T(8,128)S(1)} collective-permute-done((f32[96,512]{1,0:T(8,128)S(1)}, f32[96,512]{1,0:T(8,128)S(1)}, u32[]{:S(2)}, u32[]{:S(2)}) %collective-permute-start.2) | collective-permute-done | bytes 196640 | tf_op jit(solution)/shard_map/ppermute | solution.py:359
  9.7 1.2 %collective-permute-start.4 = (f32[64,512]{1,0:T(8,128)S(1)}, f32[64,512]{1,0:T(8,128)S(1)}, u32[]{:S(2)}, u32[]{:S(2)}) collective-permute-start(f32[64,512]{1,0:T(8,128)S(1)} %pad_maximum_fusion.1), channel_id=1, source_target_pairs={{0,16},{4,20},{8,24},{12,28},{16,0},{20,4},{24,8},{28,12},{1,17},{... | collective-permute-start | bytes 393224 | tf_op jit(solution)/shard_map/ppermute | solution.py:359
  10.9 0.3 collective-permute-start.3
  11.3 3.0 %collective-permute-start.5 = (f32[64,512]{1,0:T(8,128)S(1)}, f32[64,512]{1,0:T(8,128)S(1)}, u32[]{:S(2)}, u32[]{:S(2)}) collective-permute-start(f32[64,512]{1,0:T(8,128)S(1)} %pad_maximum_fusion.2), channel_id=1, source_target_pairs={{0,24},{4,28},{8,16},{12,20},{16,8},{20,12},{24,0},{28,4},{1,25},{... | collective-permute-start | bytes 393224 | tf_op jit(solution)/shard_map/ppermute | solution.py:359
  14.3 7.8 %collective-permute-done.3.refs_1_ = f32[64,512]{1,0:T(8,128)S(1)} collective-permute-done((f32[64,512]{1,0:T(8,128)S(1)}, f32[64,512]{1,0:T(8,128)S(1)}, u32[]{:S(2)}, u32[]{:S(2)}) %collective-permute-start.3) | collective-permute-done | bytes 131104 | tf_op jit(solution)/shard_map/ppermute | solution.py:359
  22.1 1.4 %collective-permute-start.1 = (f32[2,64,512]{2,1,0:T(8,128)S(1)}, f32[2,64,512]{2,1,0:T(8,128)S(1)}, u32[]{:S(2)}, u32[]{:S(2)}) collective-permute-start(f32[2,64,512]{2,1,0:T(8,128)S(1)} %get-tuple-element.12), channel_id=1, source_target_pairs={{0,2},{2,0},{1,3},{3,1},{4,6},{6,4},{5,7},{7,5},{8,10},{10,8},{9,1... | collective-permute-start | bytes 786440 | tf_op jit(solution)/shard_map/ppermute | solution.py:364
  23.5 0.0 collective-permute-done.5.refs_3_
  23.5 0.0 collective-permute-done.4.refs_2_
  23.6 0.1 collective-permute-start.6
  23.6 0.0 copy-done
  23.7 0.0 copy-start.2
  23.7 0.0 collective-permute-done.7.column_low.column_high
  23.7 0.0 copy-done.1
  23.7 0.0 copy-done.3
  23.7 6.3 %stencil.1.before = f32[2,64,16,512]{3,2,1,0:T(8,128)S(1)} custom-call(f32[2,64,16,512]{3,2,1,0:T(8,128)} %source.1, f32[64,16,512]{2,1,0:T(8,128)S(1)} %copy-done, s32[64,16,512]{2,1,0:T(8,128)S(1)} %copy-done.1, s32[4,16]{1,0:T(4,128)S(1)} %copy-done.3, f32[96,512]{1,0:T(8,128)S(1)} %collective-permute-done.2.near, ...), custom_call_target="tpu_custom_call" | custom-call | flops 268435456 | bytes 8388608 | tf_op jit(solution)/shard_map/stencil/pallas_call | solution.py:384
  30.0 0.0 copy-done.2
  30.0 1.2 %feed.1 = f32[520,512]{1,0:T(8,128)S(1)} custom-call(s32[8,8]{1,0:T(8,128)S(1)} %bitcast.7, f32[64,512]{1,0:T(8,128)S(1)} %slice_add_fusion.refs_0_, f32[64,512]{1,0:T(8,128)S(1)} %collective-permute-done.3.refs_1_, f32[64,512]{1,0:T(8,128)S(1)} %collective-permute-done.4.refs_2_, f32[64,512]{1,0:T(8,128)S(1)} %collective-permute-done.5.refs_3_), custom_call_target="tpu_custom_call" | custom-call | flops 33554432 | bytes 1048576 | tf_op jit(solution)/shard_map/feed/pallas_call | solution.py:399
  31.2 0.0 collective-permute-done.far
  31.2 0.0 collective-permute-done.1.axial_low.axial_high
  31.2 0.0 collective-permute-done.6.other
  31.2 2.2 %finish.1 = f32[2,64,16,512]{3,2,1,0:T(8,128)} custom-call(f32[32,512]{1,0:T(8,128)S(1)} %collective-permute-done.far, f32[16,512]{1,0:T(8,128)S(1)} %slice_bitcast_fusion.speed, f32[2,64,512]{2,1,0:T(8,128)S(1)} %collective-permute-done.1.axial_low.axial_high, f32[2,64,512]{2,1,0:T(8,128)S(1)} %collective-permute-done.1.axial_low.axial_high, ...), custom_call_target="tpu_custom_call" | custom-call | flops 67108864 | bytes 8388608 | tf_op jit(solution)/shard_map/finish/pallas_call | solution.py:411
  (18 shorter events, 0.2 us)
Async XLA Ops:
  0.2 8.2 %copy-start.4 = (f32[2,32]{1,0:T(2,128)S(1)}, f32[2,32]{1,0:T(2,128)}, u32[]{:S(2)}) copy-start(f32[2,32]{1,0:T(2,128)} %param.12) | copy-start | bytes 772
  2.0 21.7 %copy-start.1 = (s32[64,16,512]{2,1,0:T(8,128)S(1)}, s32[64,16,512]{2,1,0:T(8,128)}, u32[]{:S(2)}) copy-start(s32[64,16,512]{2,1,0:T(8,128)} %mask.1) | copy-start | bytes 6291460
  2.4 21.2 %copy-start = (f32[64,16,512]{2,1,0:T(8,128)S(1)}, f32[64,16,512]{2,1,0:T(8,128)}, u32[]{:S(2)}) copy-start(f32[64,16,512]{2,1,0:T(8,128)} %swirl.1) | copy-start | bytes 6291460
  2.4 21.3 %copy-start.3 = (s32[4,16]{1,0:T(4,128)S(1)}, s32[4,16]{1,0:T(4,128)}, u32[]{:S(2)}) copy-start(s32[4,16]{1,0:T(4,128)} %flags.1) | copy-start | bytes 772
  2.4 21.3 %collective-permute-start.7 = (f32[2,8,128]{2,1,0:T(8,128)S(1)}, f32[2,8,128]{2,1,0:T(8,128)S(1)}, u32[]{:S(2)}, u32[]{:S(2)}) collective-permute-start(f32[2,8,128]{2,1,0:T(8,128)S(1)} %bitcast.6), channel_id=1, source_target_pairs={{0,1},{1,0},{2,3},{3,2},{4,5},{5,4},{6,7},{7,6},{8,9},{9,8},{10,11... | collective-permute-start | bytes 24584 | tf_op jit(solution)/shard_map/ppermute | solution.py:364
  5.4 25.8 %collective-permute-start = (f32[32,512]{1,0:T(8,128)S(1)}, f32[32,512]{1,0:T(8,128)S(1)}, u32[]{:S(2)}, u32[]{:S(2)}) collective-permute-start(f32[32,512]{1,0:T(8,128)S(1)} %get-tuple-element.11), channel_id=1, source_target_pairs={{0,28},{4,8},{8,4},{12,16},{16,12},{20,24},{24,20},{28,0},{1,29},{... | collective-permute-start | bytes 196616 | tf_op jit(solution)/shard_map/ppermute | solution.py:371
  8.2 1.4 %collective-permute-start.2 = (f32[96,512]{1,0:T(8,128)S(1)}, f32[96,512]{1,0:T(8,128)S(1)}, u32[]{:S(2)}, u32[]{:S(2)}) collective-permute-start(f32[96,512]{1,0:T(8,128)S(1)} %get-tuple-element.15), channel_id=1, source_target_pairs={{0,4},{4,0},{8,12},{12,8},{16,20},{20,16},{24,28},{28,24},{1,5},{5... | collective-permute-start | bytes 589832 | tf_op jit(solution)/shard_map/ppermute | solution.py:359
  9.7 13.8 %collective-permute-start.4 = (f32[64,512]{1,0:T(8,128)S(1)}, f32[64,512]{1,0:T(8,128)S(1)}, u32[]{:S(2)}, u32[]{:S(2)}) collective-permute-start(f32[64,512]{1,0:T(8,128)S(1)} %pad_maximum_fusion.1), channel_id=1, source_target_pairs={{0,16},{4,20},{8,24},{12,28},{16,0},{20,4},{24,8},{28,12},{1,17},{... | collective-permute-start | bytes 393224 | tf_op jit(solution)/shard_map/ppermute | solution.py:359
  10.9 11.2 %collective-permute-start.3 = (f32[64,512]{1,0:T(8,128)S(1)}, f32[64,512]{1,0:T(8,128)S(1)}, u32[]{:S(2)}, u32[]{:S(2)}) collective-permute-start(f32[64,512]{1,0:T(8,128)S(1)} %pad_maximum_fusion), channel_id=1, source_target_pairs={{0,8},{4,12},{8,0},{12,4},{16,24},{20,28},{24,16},{28,20},{1,9},{5... | collective-permute-start | bytes 393224 | tf_op jit(solution)/shard_map/ppermute | solution.py:359
  11.3 12.2 %collective-permute-start.5 = (f32[64,512]{1,0:T(8,128)S(1)}, f32[64,512]{1,0:T(8,128)S(1)}, u32[]{:S(2)}, u32[]{:S(2)}) collective-permute-start(f32[64,512]{1,0:T(8,128)S(1)} %pad_maximum_fusion.2), channel_id=1, source_target_pairs={{0,24},{4,28},{8,16},{12,20},{16,8},{20,12},{24,0},{28,4},{1,25},{... | collective-permute-start | bytes 393224 | tf_op jit(solution)/shard_map/ppermute | solution.py:359
  22.1 9.1 %collective-permute-start.1 = (f32[2,64,512]{2,1,0:T(8,128)S(1)}, f32[2,64,512]{2,1,0:T(8,128)S(1)}, u32[]{:S(2)}, u32[]{:S(2)}) collective-permute-start(f32[2,64,512]{2,1,0:T(8,128)S(1)} %get-tuple-element.12), channel_id=1, source_target_pairs={{0,2},{2,0},{1,3},{3,1},{4,6},{6,4},{5,7},{7,5},{8,10},{10,8},{9,1... | collective-permute-start | bytes 786440 | tf_op jit(solution)/shard_map/ppermute | solution.py:364
  23.6 7.7 %collective-permute-start.6 = (f32[64,512]{1,0:T(8,128)S(1)}, f32[64,512]{1,0:T(8,128)S(1)}, u32[]{:S(2)}, u32[]{:S(2)}) collective-permute-start(f32[64,512]{1,0:T(8,128)S(1)} %fusion.1.own), channel_id=1, source_target_pairs={{0,4},{4,0},{8,12},{12,8},{16,20},{20,16},{24,28},{28,24},{1,5},{5... | collective-permute-start | bytes 393224 | tf_op jit(solution)/shard_map/ppermute | solution.py:359
  23.7 6.4 %copy-start.2 = (s32[1,8,8]{2,1,0:T(8,128)S(1)}, s32[1,8,8]{2,1,0:T(8,128)}, u32[]{:S(2)}) copy-start(s32[1,8,8]{2,1,0:T(8,128)} %param.15) | copy-start | bytes 772

commit v8 on v7

--- a/solution.py
+++ b/solution.py
@@ -12,7 +12,7 @@
 TILE = 16
 HEAD = 4
 LANES = 128
-UNROLL = 4
+UNROLL = 8
 SUB = 8
 HIGH = lax.Precision.HIGHEST
 VMEM = pl.BlockSpec(memory_space=pltpu.VMEM)
@@ -150,10 +150,10 @@
             column[e, g] = acc
 
 
-def stencil(source, swirl, mask, flags, near, column_low, column_high, out, fields, levels, sem):
+def stencil(source, swirl, mask, flags, near, column_low, column_high, final, out, fields, levels, sem, done):
     azi, rad = lax.axis_index("azi"), lax.axis_index("rad")
     last_rad = lax.axis_size("rad") - 1
-    count, cells, depth, width = fields.shape
+    count, cells, depth, width = source.shape
     base = near.shape[0] - count * depth
     parity = azi % 2
     halves = depth // SUB
@@ -163,10 +163,22 @@
     at_left, at_right = lane == 0, lane == LANES - 1
     at_low, at_high = row == 0, row == SUB - 1
     has_left, has_right = rad > 0, rad < last_rad
-    pieces = [slice(k * TILE, (k + 1) * TILE) for k in range(cells // TILE)]
-    copies = [pltpu.make_async_copy(source.at[:, p], fields.at[:, p], sem.at[k]) for k, p in enumerate(pieces)]
-    for copy in copies:
-        copy.start()
+    groups = cells // SUB
+
+    def piece(k):
+        begin, end = (k * SUB + 1 if k else 0), min(k * SUB + SUB + 1, cells)
+        return pltpu.make_async_copy(source.at[:, begin:end], fields.at[:, begin + 1 : end + 1], sem.at[k])
+
+    def ready(k):
+        rows = pl.ds(k * SUB, SUB)
+        return pltpu.make_async_copy(out.at[:, rows], final.at[:, rows], done.at[k])
+
+    for k in range(groups):
+        piece(k).start()
+    for c in range(count):
+        layer = near[base + c * depth : base + (c + 1) * depth]
+        fields[c, 0] = jnp.where(parity == 1, layer, 0.0)
+        fields[c, cells + 1] = jnp.where(parity == 0, layer, 0.0)
     turned = (0.5 * flags[...].astype(f32)).T
     for k in range(cells // TILE):
         levels[k] = jnp.broadcast_to(turned[:, k : k + 1], (depth, LANES))
@@ -174,7 +186,7 @@
     def cut(h, l):
         return slice(h * SUB, (h + 1) * SUB), slice(l * LANES, (l + 1) * LANES)
 
-    def slab(t, before, after):
+    def slab(t, carry):
         level = levels[t // TILE]
         for c in range(count):
             edges = []
@@ -185,7 +197,7 @@
                     jnp.where(has_left, pltpu.roll(column_low[g], (LANES - j) % LANES, 1), 0.0),
                     jnp.where(has_right, pltpu.roll(column_high[g], LANES - 1 - j, 1), 0.0),
                 ))
-            parts = [[fields[(c, t) + cut(h, l)] for l in range(blocks)] for h in range(halves)]
+            parts = [[fields[(c, t + 1) + cut(h, l)] for l in range(blocks)] for h in range(halves)]
             ups = [[pltpu.roll(v, 1, 1) for v in p] for p in parts]
             downs = [[pltpu.roll(v, LANES - 1, 1) for v in p] for p in parts]
             for l in range(blocks):
@@ -196,40 +208,42 @@
                     right = jnp.where(at_right, downs[h][l + 1] if l + 1 < blocks else edges[h][1], downs[h][l])
                     low = jnp.where(at_low, lows[h - 1] if h else 0.0, lows[h])
                     high = jnp.where(at_high, highs[h + 1] if h + 1 < halves else 0.0, highs[h])
-                    total = (left + right) + (low + high) + after(c, h, l)
+                    total = (left + right) + (low + high) + fields[(c, t + 2) + cut(h, l)]
                     speed = swirl[(t,) + cut(h, l)]
-                    value = parts[h][l] * (0.4 - speed) + before(c, h, l) * (speed + 0.1) + 0.1 * total
+                    value = parts[h][l] * (0.4 - speed) + fields[(c, t) + cut(h, l)] * (speed + 0.1) + 0.1 * total
                     if c == 0:
                         out[(0, t) + cut(h, l)] = value
                     else:
                         live = jnp.where(mask[(t,) + cut(h, l)] == 0, level[h * SUB : (h + 1) * SUB], 0.0) * parts[h][l]
-                        energy = fields[(0, t) + cut(h, l)]
+                        energy = fields[(0, t + 1) + cut(h, l)]
                         burn = live + live * jnp.tanh(2.0 * energy - 1.0)
                         out[(0, t) + cut(h, l)] += burn
                         out[(1, t) + cut(h, l)] = value - 0.5 * burn
-
-    def halo(use_near):
-        def value(c, h, l):
-            _, lanes = cut(h, l)
-            first = base + c * depth + h * SUB
-            return jnp.where(use_near, near[first : first + SUB, lanes], 0.0)
-
-        return value
-
-    def inside(t):
-        return lambda c, h, l: fields[(c, t) + cut(h, l)]
-
-    def step(t, carry):
-        slab(t, inside(t - 1), inside(t + 1))
         return carry
 
-    copies[0].wait()
-    slab(0, halo(parity == 1), inside(1))
-    for k, copy in enumerate(copies):
-        if k:
-            copy.wait()
-        lax.fori_loop(k * TILE - 1 if k else 1, (k + 1) * TILE - 1, step, 0, unroll=UNROLL)
-    slab(cells - 1, inside(cells - 2), halo(parity == 0))
+    def rows(k, carry):
+        lax.fori_loop(0, SUB, lambda i, c: slab(k * SUB + i, c), 0, unroll=UNROLL)
+
+        @pl.when(k < groups - 1)
+        def _():
+            ready(k).start()
+
+        @pl.when(k < groups - 2)
+        def _():
+            begin = (k + 1) * SUB + 1
+            source_rows, own_rows = pl.ds(begin, SUB), pl.ds(begin + 1, SUB)
+            pltpu.make_async_copy(source.at[:, source_rows], fields.at[:, own_rows], sem.at[k + 1]).wait()
+
+        @pl.when(k == groups - 2)
+        def _():
+            piece(groups - 1).wait()
+
+        return carry
+
+    piece(0).wait()
+    lax.fori_loop(0, groups, rows, 0)
+    for k in range(groups - 1):
+        ready(k).wait()
 
 
 def feed_rows(slots, targets, *refs):
@@ -249,7 +263,7 @@
                     feed[pl.ds(at, 1), :] += block[r : r + 1, :]
 
 
-def finish(chunk, length, far, speed, axial_low, axial_high, row_top, own, other, weights, feed, before, out, modes, high, result, sem):
+def finish(chunk, length, far, speed, axial_low, axial_high, row_top, own, other, weights, feed, before, _, out, modes, high, result, sem):
     azi, ax = lax.axis_index("azi"), lax.axis_index("ax")
     last_ax = lax.axis_size("ax") - 1
     count, cells, depth, width = before.shape
@@ -298,10 +312,15 @@
                         result[c, t] += jnp.where(parity == 1, 0.1 * layer, 0.0)
                     else:
                         result[c, t] += jnp.where(parity == 0, (speed[...] + 0.1) * layer, 0.0)
-            cells_at = pl.ds(b * group, group)
-            copy = pltpu.make_async_copy(result.at[c, cells_at], out.at[c, cells_at], sem.at[c, b])
-            copy.start()
-            copies.append(copy)
+            at = slice(b * group, (b + 1) * group)
+            if b in (0, cells // group - 1):
+                parts = [slice(0, depth)]
+            else:
+                parts = [depth - 1, slice(0, HEAD) if c == 1 else 0]
+            for k, part in enumerate(parts):
+                copy = pltpu.make_async_copy(result.at[c, at, part], out.at[c, at, part], sem.at[c, b, k])
+                copy.start()
+                copies.append(copy)
     for copy in copies:
         copy.wait()
 
@@ -381,15 +400,16 @@
         jnp.add, [mixed] + [jnp.concatenate([x[(pairs - k) * chunk :], x[: (pairs - k) * chunk]], axis=0) for k, x in enumerate(arrived) if k]
     )
 
-    before = pl.pallas_call(
+    final, before = pl.pallas_call(
         stencil,
-        out_shape=struct(fields.shape, f32),
+        out_shape=[struct(fields.shape, f32)] * 2,
         in_specs=[HBM] + [VMEM] * 6,
-        out_specs=VMEM,
+        out_specs=[HBM, VMEM],
         scratch_shapes=[
-            pltpu.VMEM(fields.shape, f32),
+            pltpu.VMEM((count, cells + 2, depth, width), f32),
             pltpu.VMEM((cells // TILE, depth, LANES), f32),
-            pltpu.SemaphoreType.DMA((cells // TILE,)),
+            pltpu.SemaphoreType.DMA((cells // SUB,)),
+            pltpu.SemaphoreType.DMA((cells // SUB,)),
         ],
         compiler_params=params(12),
         cost_estimate=cost(1 << 28, 1 << 23),
@@ -411,18 +431,19 @@
     return pl.pallas_call(
         functools.partial(finish, chunk, length),
         out_shape=struct(fields.shape, f32),
-        in_specs=[VMEM] * 10,
+        in_specs=[VMEM] * 10 + [HBM],
         out_specs=HBM,
+        input_output_aliases={10: 0},
         scratch_shapes=[
             pltpu.VMEM((count * modes, width), f32),
             pltpu.VMEM((count, cells, width), f32),
             pltpu.VMEM(fields.shape, f32),
-            pltpu.SemaphoreType.DMA((count, cells // SUB)),
+            pltpu.SemaphoreType.DMA((count, cells // SUB, 2)),
         ],
         compiler_params=params(16),
         cost_estimate=cost(1 << 26, 1 << 23),
         name="finish",
-    )(far, swirl_speed[0], axial_low, axial_high, row_top, summed, other, weights, feed, before)
+    )(far, swirl_speed[0], axial_low, axial_high, row_top, summed, other, weights, feed, before, final)
 
 
 def solution(mesh):

time: 33.6 us -> 32.6 us (0.970)
  Pallas kernels: 11.9 us -> 10.8 us
    pallas_call x1, Pallas kernels: 6.31 us -> 5.67 us  [body(): pl.pallas_call(stencil, out_shape=[struct(fields.shape, f32)] * 2, in_spe...]
    pallas_call x1, Pallas kernels: 2.21 us -> 1.7 us  [body(): pl.pallas_call(functools.partial(finish, chunk, length), out_shape=struct...]
  transfers between devices with their start and end apart: 8 -> 8, of which waited for: 2 -> 2; matrix products, arithmetic and copies ran while one was open for 2% -> 2% of each run, Pallas kernels for 22% -> 21%
where the time goes in v8:
time: 32.6 us; the launch traced here: 32.4 us
  starting transfers between devices  11.8 us (36%)
  Pallas kernels  10.8 us (33%)
  waiting for transfers between devices  8.83 us (27%)
  other arithmetic  0.63 us (2%)
    ppermute x5, waiting for transfers between devices, swap(): return lax.ppermute(x, 'azi', [(i, i ^ k) for i in range(sectors)])  8.83 us
    pallas_call x1, Pallas kernels, body(): pl.pallas_call(stencil, out_shape=[struct(fields.shape, f32)] * 2, in_spe...  5.67 us
    ppermute x5, starting transfers between devices, swap(): return lax.ppermute(x, 'azi', [(i, i ^ k) for i in range(sectors)])  4.66 us
    ppermute x2, starting transfers between devices, across(): received = lax.ppermute(to_only, axis, [(0, 1), (1, 0)])  4.39 us
    ppermute x1, starting transfers between devices, body(): far = lax.ppermute(shift, 'azi', offset)  2.76 us
    pallas_call x1, Pallas kernels, body(): pl.pallas_call(functools.partial(prepare, chunk), out_shape=(struct((pair...  1.92 us
    pallas_call x1, Pallas kernels, body(): pl.pallas_call(functools.partial(finish, chunk, length), out_shape=struct...  1.7 us
    pallas_call x1, Pallas kernels, body(): pl.pallas_call(functools.partial(feed_rows, slots), out_shape=struct((cel...  1.16 us
  transfers between devices with their start and end apart: 8, of which 2 were waited for; matrix products, arithmetic and copies ran while one was open for 2% of the time, Pallas kernels for 21%

profile of v8, /device:TPU:0, one launch (start us, length us, event | category | flops | bytes accessed | tf_op | source)
XLA Modules:
  0.0 32.4 jit_solution(15536111035662078440)
XLA Ops:
  0.0 0.0 copy-start.4
  0.0 0.2 fusion.11
  0.2 0.0 copy-start
  0.2 0.0 copy-start.1
  0.2 0.0 copy-start.3
  0.2 1.9 %prepare.1 = (f32[64,512]{1,0:T(8,128)S(1)}, f32[96,512]{1,0:T(8,128)S(1)}, f32[32,512]{1,0:T(8,128)S(1)}, f32[2,64,512]{2,1,0:T(8,128)S(1)}, f32[2,64,512]{2,1,...) custom-call(f32[2,64,16,512]{3,2,1,0:T(8,128)} %source.1, f32[64,64]{1,0:T(8,128)S(1)} %pad_maximum_fusion.3.phase, ...), custom_call_target="tpu_custom_call" | custom-call | flops 67108864 | bytes 2097152 | tf_op jit(solution)/shard_map/prepare/pallas_call | solution.py:345
  2.1 0.3 %columns.1 = f32[1,2,8,128]{3,2,1,0:T(8,128)S(1)} custom-call(f32[1,2,64,16,128]{4,3,2,1,0:T(8,128)S(1)} %get-tuple-element.18.tile), custom_call_target="tpu_custom_call" | custom-call | flops 4194304 | bytes 524288 | tf_op jit(solution)/shard_map/columns/pallas_call | solution.py:367
  2.5 3.0 %collective-permute-start.7 = (f32[2,8,128]{2,1,0:T(8,128)S(1)}, f32[2,8,128]{2,1,0:T(8,128)S(1)}, u32[]{:S(2)}, u32[]{:S(2)}) collective-permute-start(f32[2,8,128]{2,1,0:T(8,128)S(1)} %bitcast.6), channel_id=1, source_target_pairs={{0,1},{1,0},{2,3},{3,2},{4,5},{5,4},{6,7},{7,6},{8,9},{9,8},{10,11... | collective-permute-start | bytes 24584 | tf_op jit(solution)/shard_map/ppermute | solution.py:383
  5.5 2.8 %collective-permute-start = (f32[32,512]{1,0:T(8,128)S(1)}, f32[32,512]{1,0:T(8,128)S(1)}, u32[]{:S(2)}, u32[]{:S(2)}) collective-permute-start(f32[32,512]{1,0:T(8,128)S(1)} %get-tuple-element.13), channel_id=1, source_target_pairs={{0,28},{4,8},{8,4},{12,16},{16,12},{20,24},{24,20},{28,0},{1,29},{... | collective-permute-start | bytes 196616 | tf_op jit(solution)/shard_map/ppermute | solution.py:390
  8.3 0.0 collective-permute-start.2
  8.3 0.2 fusion.9
  8.5 0.0 copy-done.4
  8.5 0.1 pad_maximum_fusion.5
  8.6 0.1 pad_maximum_fusion.4
  8.7 1.1 %collective-permute-done.2.near = f32[96,512]{1,0:T(8,128)S(1)} collective-permute-done((f32[96,512]{1,0:T(8,128)S(1)}, f32[96,512]{1,0:T(8,128)S(1)}, u32[]{:S(2)}, u32[]{:S(2)}) %collective-permute-start.2) | collective-permute-done | bytes 196640 | tf_op jit(solution)/shard_map/ppermute | solution.py:378
  9.8 1.2 %collective-permute-start.4 = (f32[64,512]{1,0:T(8,128)S(1)}, f32[64,512]{1,0:T(8,128)S(1)}, u32[]{:S(2)}, u32[]{:S(2)}) collective-permute-start(f32[64,512]{1,0:T(8,128)S(1)} %pad_maximum_fusion.1), channel_id=1, source_target_pairs={{0,16},{4,20},{8,24},{12,28},{16,0},{20,4},{24,8},{28,12},{1,17},{... | collective-permute-start | bytes 393224 | tf_op jit(solution)/shard_map/ppermute | solution.py:378
  11.1 0.3 %collective-permute-start.3 = (f32[64,512]{1,0:T(8,128)S(1)}, f32[64,512]{1,0:T(8,128)S(1)}, u32[]{:S(2)}, u32[]{:S(2)}) collective-permute-start(f32[64,512]{1,0:T(8,128)S(1)} %pad_maximum_fusion), channel_id=1, source_target_pairs={{0,8},{4,12},{8,0},{12,4},{16,24},{20,28},{24,16},{28,20},{1,9},{5... | collective-permute-start | bytes 393224 | tf_op jit(solution)/shard_map/ppermute | solution.py:378
  11.4 3.0 %collective-permute-start.5 = (f32[64,512]{1,0:T(8,128)S(1)}, f32[64,512]{1,0:T(8,128)S(1)}, u32[]{:S(2)}, u32[]{:S(2)}) collective-permute-start(f32[64,512]{1,0:T(8,128)S(1)} %pad_maximum_fusion.2), channel_id=1, source_target_pairs={{0,24},{4,28},{8,16},{12,20},{16,8},{20,12},{24,0},{28,4},{1,25},{... | collective-permute-start | bytes 393224 | tf_op jit(solution)/shard_map/ppermute | solution.py:378
  14.4 7.8 %collective-permute-done.3.refs_1_ = f32[64,512]{1,0:T(8,128)S(1)} collective-permute-done((f32[64,512]{1,0:T(8,128)S(1)}, f32[64,512]{1,0:T(8,128)S(1)}, u32[]{:S(2)}, u32[]{:S(2)}) %collective-permute-start.3) | collective-permute-done | bytes 131104 | tf_op jit(solution)/shard_map/ppermute | solution.py:378
  22.2 1.4 %collective-permute-start.1 = (f32[2,64,512]{2,1,0:T(8,128)S(1)}, f32[2,64,512]{2,1,0:T(8,128)S(1)}, u32[]{:S(2)}, u32[]{:S(2)}) collective-permute-start(f32[2,64,512]{2,1,0:T(8,128)S(1)} %get-tuple-element.14), channel_id=1, source_target_pairs={{0,2},{2,0},{1,3},{3,1},{4,6},{6,4},{5,7},{7,5},{8,10},{10,8},{9,1... | collective-permute-start | bytes 786440 | tf_op jit(solution)/shard_map/ppermute | solution.py:383
  23.6 0.0 collective-permute-done.5.refs_3_
  23.6 0.0 collective-permute-done.4.refs_2_
  23.7 0.1 collective-permute-start.6
  23.8 0.0 copy-done
  23.8 0.0 copy-start.2
  23.8 0.0 collective-permute-done.7.column_low.column_high
  23.8 0.0 copy-done.1
  23.8 0.0 copy-done.3
  23.8 5.7 %stencil.1 = (f32[2,64,16,512]{3,2,1,0:T(8,128)}, f32[2,64,16,512]{3,2,1,0:T(8,128)S(1)}) custom-call(f32[2,64,16,512]{3,2,1,0:T(8,128)} %source.1, f32[64,16,512]{2,1,0:T(8,128)S(1)} %copy-done, s32[64,16,512]{2,1,0:T(8,128)S(1)} %copy-done.1, s32[4,16]{1,0:T(4,128)S(1)} %copy-done.3, f32[96,512]{1,0:T(8,128)S(1)} %collective-permute-done.2.near, ...), custom_call_target="tpu_custom_call" | custom-call | flops 268435456 | bytes 8388608 | tf_op jit(solution)/shard_map/stencil/pallas_call | solution.py:403
  29.5 0.0 copy-done.2
  29.5 1.2 %feed.1 = f32[520,512]{1,0:T(8,128)S(1)} custom-call(s32[8,8]{1,0:T(8,128)S(1)} %bitcast.7, f32[64,512]{1,0:T(8,128)S(1)} %slice_add_fusion.refs_0_, f32[64,512]{1,0:T(8,128)S(1)} %collective-permute-done.3.refs_1_, f32[64,512]{1,0:T(8,128)S(1)} %collective-permute-done.4.refs_2_, f32[64,512]{1,0:T(8,128)S(1)} %collective-permute-done.5.refs_3_), custom_call_target="tpu_custom_call" | custom-call | flops 33554432 | bytes 1048576 | tf_op jit(solution)/shard_map/feed/pallas_call | solution.py:419
  30.7 0.0 collective-permute-done.far
  30.7 0.0 collective-permute-done.1.axial_low.axial_high
  30.7 0.0 collective-permute-done.6.other
  30.7 1.7 %finish.1 = f32[2,64,16,512]{3,2,1,0:T(8,128)} custom-call(f32[32,512]{1,0:T(8,128)S(1)} %collective-permute-done.far, f32[16,512]{1,0:T(8,128)S(1)} %slice_bitcast_fusion.speed, f32[2,64,512]{2,1,0:T(8,128)S(1)} %collective-permute-done.1.axial_low.axial_high, ...), custom_call_target="tpu_custom_call", output_to_operand_aliasing={{}: (10, {})} | custom-call | flops 67108864 | bytes 8388608 | tf_op jit(solution)/shard_map/finish/pallas_call | solution.py:431
  (18 shorter events, 0.2 us)
Async XLA Ops:
  0.0 8.5 %copy-start.4 = (f32[2,32]{1,0:T(2,128)S(1)}, f32[2,32]{1,0:T(2,128)}, u32[]{:S(2)}) copy-start(f32[2,32]{1,0:T(2,128)} %param.12) | copy-start | bytes 772
  0.2 23.6 %copy-start = (f32[64,16,512]{2,1,0:T(8,128)S(1)}, f32[64,16,512]{2,1,0:T(8,128)}, u32[]{:S(2)}) copy-start(f32[64,16,512]{2,1,0:T(8,128)} %swirl.1) | copy-start | bytes 6291460
  0.2 23.6 %copy-start.1 = (s32[64,16,512]{2,1,0:T(8,128)S(1)}, s32[64,16,512]{2,1,0:T(8,128)}, u32[]{:S(2)}) copy-start(s32[64,16,512]{2,1,0:T(8,128)} %mask.1) | copy-start | bytes 6291460
  0.2 23.6 %copy-start.3 = (s32[4,16]{1,0:T(4,128)S(1)}, s32[4,16]{1,0:T(4,128)}, u32[]{:S(2)}) copy-start(s32[4,16]{1,0:T(4,128)} %flags.1) | copy-start | bytes 772
  2.5 21.3 %collective-permute-start.7 = (f32[2,8,128]{2,1,0:T(8,128)S(1)}, f32[2,8,128]{2,1,0:T(8,128)S(1)}, u32[]{:S(2)}, u32[]{:S(2)}) collective-permute-start(f32[2,8,128]{2,1,0:T(8,128)S(1)} %bitcast.6), channel_id=1, source_target_pairs={{0,1},{1,0},{2,3},{3,2},{4,5},{5,4},{6,7},{7,6},{8,9},{9,8},{10,11... | collective-permute-start | bytes 24584 | tf_op jit(solution)/shard_map/ppermute | solution.py:383
  5.5 25.2 %collective-permute-start = (f32[32,512]{1,0:T(8,128)S(1)}, f32[32,512]{1,0:T(8,128)S(1)}, u32[]{:S(2)}, u32[]{:S(2)}) collective-permute-start(f32[32,512]{1,0:T(8,128)S(1)} %get-tuple-element.13), channel_id=1, source_target_pairs={{0,28},{4,8},{8,4},{12,16},{16,12},{20,24},{24,20},{28,0},{1,29},{... | collective-permute-start | bytes 196616 | tf_op jit(solution)/shard_map/ppermute | solution.py:390
  8.3 1.4 %collective-permute-start.2 = (f32[96,512]{1,0:T(8,128)S(1)}, f32[96,512]{1,0:T(8,128)S(1)}, u32[]{:S(2)}, u32[]{:S(2)}) collective-permute-start(f32[96,512]{1,0:T(8,128)S(1)} %get-tuple-element.17), channel_id=1, source_target_pairs={{0,4},{4,0},{8,12},{12,8},{16,20},{20,16},{24,28},{28,24},{1,5},{5... | collective-permute-start | bytes 589832 | tf_op jit(solution)/shard_map/ppermute | solution.py:378
  9.8 13.8 %collective-permute-start.4 = (f32[64,512]{1,0:T(8,128)S(1)}, f32[64,512]{1,0:T(8,128)S(1)}, u32[]{:S(2)}, u32[]{:S(2)}) collective-permute-start(f32[64,512]{1,0:T(8,128)S(1)} %pad_maximum_fusion.1), channel_id=1, source_target_pairs={{0,16},{4,20},{8,24},{12,28},{16,0},{20,4},{24,8},{28,12},{1,17},{... | collective-permute-start | bytes 393224 | tf_op jit(solution)/shard_map/ppermute | solution.py:378
  11.1 11.2 %collective-permute-start.3 = (f32[64,512]{1,0:T(8,128)S(1)}, f32[64,512]{1,0:T(8,128)S(1)}, u32[]{:S(2)}, u32[]{:S(2)}) collective-permute-start(f32[64,512]{1,0:T(8,128)S(1)} %pad_maximum_fusion), channel_id=1, source_target_pairs={{0,8},{4,12},{8,0},{12,4},{16,24},{20,28},{24,16},{28,20},{1,9},{5... | collective-permute-start | bytes 393224 | tf_op jit(solution)/shard_map/ppermute | solution.py:378
  11.4 12.2 %collective-permute-start.5 = (f32[64,512]{1,0:T(8,128)S(1)}, f32[64,512]{1,0:T(8,128)S(1)}, u32[]{:S(2)}, u32[]{:S(2)}) collective-permute-start(f32[64,512]{1,0:T(8,128)S(1)} %pad_maximum_fusion.2), channel_id=1, source_target_pairs={{0,24},{4,28},{8,16},{12,20},{16,8},{20,12},{24,0},{28,4},{1,25},{... | collective-permute-start | bytes 393224 | tf_op jit(solution)/shard_map/ppermute | solution.py:378
  22.2 8.5 %collective-permute-start.1 = (f32[2,64,512]{2,1,0:T(8,128)S(1)}, f32[2,64,512]{2,1,0:T(8,128)S(1)}, u32[]{:S(2)}, u32[]{:S(2)}) collective-permute-start(f32[2,64,512]{2,1,0:T(8,128)S(1)} %get-tuple-element.14), channel_id=1, source_target_pairs={{0,2},{2,0},{1,3},{3,1},{4,6},{6,4},{5,7},{7,5},{8,10},{10,8},{9,1... | collective-permute-start | bytes 786440 | tf_op jit(solution)/shard_map/ppermute | solution.py:383
  23.7 7.0 %collective-permute-start.6 = (f32[64,512]{1,0:T(8,128)S(1)}, f32[64,512]{1,0:T(8,128)S(1)}, u32[]{:S(2)}, u32[]{:S(2)}) collective-permute-start(f32[64,512]{1,0:T(8,128)S(1)} %fusion.1.own), channel_id=1, source_target_pairs={{0,4},{4,0},{8,12},{12,8},{16,20},{20,16},{24,28},{28,24},{1,5},{5... | collective-permute-start | bytes 393224 | tf_op jit(solution)/shard_map/ppermute | solution.py:378
  23.8 5.7 %copy-start.2 = (s32[1,8,8]{2,1,0:T(8,128)S(1)}, s32[1,8,8]{2,1,0:T(8,128)}, u32[]{:S(2)}) copy-start(s32[1,8,8]{2,1,0:T(8,128)} %param.15) | copy-start | bytes 772

commit v9 on v8

--- a/solution.py
+++ b/solution.py
@@ -59,6 +59,10 @@
     row_sent = jnp.where((ax == 0) & (last_ax == 1), depth - 1, 0)
     first = pltpu.make_async_copy(fields.at[:, :, depth - 1, :], row_top, sem.at[0])
     first.start()
+    supply = pltpu.make_async_copy(profile, plenum, sem.at[3 + 2 * count])
+    supply.start()
+    factor = pltpu.make_async_copy(rates, rate, sem.at[4 + 2 * count])
+    factor.start()
     copies = []
     for c in range(count):
         rows = slice(base + c * depth, base + (c + 1) * depth)
@@ -73,10 +77,6 @@
         lanes = pl.ds(pl.multiple_of(block, LANES), LANES)
         copies.append(pltpu.make_async_copy(fields.at[:, :, :, lanes], tile.at[e], sem.at[5 + 2 * count + e]))
         copies[-1].start()
-    supply = pltpu.make_async_copy(profile, plenum, sem.at[3 + 2 * count])
-    supply.start()
-    factor = pltpu.make_async_copy(rates, rate, sem.at[4 + 2 * count])
-    factor.start()
 
     @pl.when(ax == last_ax)
     def _():
@@ -292,7 +292,8 @@
     row = lax.broadcasted_iota(jnp.int32, (SUB, width), 0)
     group = SUB
     copies = []
-    for b in range(cells // group):
+    last = cells // group - 1
+    for b in [last] + list(range(last)):
         for c in range(count):
             low_rows = scale * axial_low[c, b * group : (b + 1) * group]
             high_rows = high[c, b * group : (b + 1) * group]
@@ -313,7 +314,7 @@
                     else:
                         result[c, t] += jnp.where(parity == 0, (speed[...] + 0.1) * layer, 0.0)
             at = slice(b * group, (b + 1) * group)
-            if b in (0, cells // group - 1):
+            if b in (0, last):
                 parts = [slice(0, depth)]
             else:
                 parts = [depth - 1, slice(0, HEAD) if c == 1 else 0]

time: 32.6 us -> 32.5 us (level)
  no operation moved by 1% of the time
where the time goes in v9:
time: 32.5 us; the launch traced here: 32.3 us
  starting transfers between devices  12 us (37%)
  Pallas kernels  10.6 us (33%)
  waiting for transfers between devices  8.83 us (27%)
  other arithmetic  0.63 us (2%)
    ppermute x5, waiting for transfers between devices, swap(): return lax.ppermute(x, 'azi', [(i, i ^ k) for i in range(sectors)])  8.83 us
    pallas_call x1, Pallas kernels, body(): pl.pallas_call(stencil, out_shape=[struct(fields.shape, f32)] * 2, in_spe...  5.67 us
    ppermute x5, starting transfers between devices, swap(): return lax.ppermute(x, 'azi', [(i, i ^ k) for i in range(sectors)])  4.66 us
    ppermute x2, starting transfers between devices, across(): received = lax.ppermute(to_only, axis, [(0, 1), (1, 0)])  4.55 us
    ppermute x1, starting transfers between devices, body(): far = lax.ppermute(shift, 'azi', offset)  2.76 us
    pallas_call x1, Pallas kernels, body(): pl.pallas_call(functools.partial(prepare, chunk), out_shape=(struct((pair...  1.82 us
    pallas_call x1, Pallas kernels, body(): pl.pallas_call(functools.partial(finish, chunk, length), out_shape=struct...  1.57 us
    pallas_call x1, Pallas kernels, body(): pl.pallas_call(functools.partial(feed_rows, slots), out_shape=struct((cel...  1.16 us
  transfers between devices with their start and end apart: 8, of which 2 were waited for; matrix products, arithmetic and copies ran while one was open for 2% of the time, Pallas kernels for 21%

profile of v9, /device:TPU:0, one launch (start us, length us, event | category | flops | bytes accessed | tf_op | source)
XLA Modules:
  0.0 32.3 jit_solution(5227623724810122117)
XLA Ops:
  0.0 0.0 copy-start.4
  0.0 0.2 fusion.11
  0.2 0.0 copy-start
  0.2 0.0 copy-start.1
  0.2 0.0 copy-start.3
  0.2 1.8 %prepare.1 = (f32[64,512]{1,0:T(8,128)S(1)}, f32[96,512]{1,0:T(8,128)S(1)}, f32[32,512]{1,0:T(8,128)S(1)}, f32[2,64,512]{2,1,0:T(8,128)S(1)}, f32[2,64,512]{2,1,...) custom-call(f32[2,64,16,512]{3,2,1,0:T(8,128)} %source.1, f32[64,64]{1,0:T(8,128)S(1)} %pad_maximum_fusion.3.phase, ...), custom_call_target="tpu_custom_call" | custom-call | flops 67108864 | bytes 2097152 | tf_op jit(solution)/shard_map/prepare/pallas_call | solution.py:346
  2.0 0.3 %columns.1 = f32[1,2,8,128]{3,2,1,0:T(8,128)S(1)} custom-call(f32[1,2,64,16,128]{4,3,2,1,0:T(8,128)S(1)} %get-tuple-element.18.tile), custom_call_target="tpu_custom_call" | custom-call | flops 4194304 | bytes 524288 | tf_op jit(solution)/shard_map/columns/pallas_call | solution.py:368
  2.4 3.0 %collective-permute-start.7 = (f32[2,8,128]{2,1,0:T(8,128)S(1)}, f32[2,8,128]{2,1,0:T(8,128)S(1)}, u32[]{:S(2)}, u32[]{:S(2)}) collective-permute-start(f32[2,8,128]{2,1,0:T(8,128)S(1)} %bitcast.6), channel_id=1, source_target_pairs={{0,1},{1,0},{2,3},{3,2},{4,5},{5,4},{6,7},{7,6},{8,9},{9,8},{10,11... | collective-permute-start | bytes 24584 | tf_op jit(solution)/shard_map/ppermute | solution.py:384
  5.4 2.8 %collective-permute-start = (f32[32,512]{1,0:T(8,128)S(1)}, f32[32,512]{1,0:T(8,128)S(1)}, u32[]{:S(2)}, u32[]{:S(2)}) collective-permute-start(f32[32,512]{1,0:T(8,128)S(1)} %get-tuple-element.13), channel_id=1, source_target_pairs={{0,28},{4,8},{8,4},{12,16},{16,12},{20,24},{24,20},{28,0},{1,29},{... | collective-permute-start | bytes 196616 | tf_op jit(solution)/shard_map/ppermute | solution.py:391
  8.2 0.0 collective-permute-start.2
  8.2 0.2 fusion.9
  8.4 0.0 copy-done.4
  8.4 0.1 pad_maximum_fusion.5
  8.5 0.1 pad_maximum_fusion.4
  8.6 1.1 %collective-permute-done.2.near = f32[96,512]{1,0:T(8,128)S(1)} collective-permute-done((f32[96,512]{1,0:T(8,128)S(1)}, f32[96,512]{1,0:T(8,128)S(1)}, u32[]{:S(2)}, u32[]{:S(2)}) %collective-permute-start.2) | collective-permute-done | bytes 196640 | tf_op jit(solution)/shard_map/ppermute | solution.py:379
  9.7 1.2 %collective-permute-start.4 = (f32[64,512]{1,0:T(8,128)S(1)}, f32[64,512]{1,0:T(8,128)S(1)}, u32[]{:S(2)}, u32[]{:S(2)}) collective-permute-start(f32[64,512]{1,0:T(8,128)S(1)} %pad_maximum_fusion.1), channel_id=1, source_target_pairs={{0,16},{4,20},{8,24},{12,28},{16,0},{20,4},{24,8},{28,12},{1,17},{... | collective-permute-start | bytes 393224 | tf_op jit(solution)/shard_map/ppermute | solution.py:379
  11.0 0.3 %collective-permute-start.3 = (f32[64,512]{1,0:T(8,128)S(1)}, f32[64,512]{1,0:T(8,128)S(1)}, u32[]{:S(2)}, u32[]{:S(2)}) collective-permute-start(f32[64,512]{1,0:T(8,128)S(1)} %pad_maximum_fusion), channel_id=1, source_target_pairs={{0,8},{4,12},{8,0},{12,4},{16,24},{20,28},{24,16},{28,20},{1,9},{5... | collective-permute-start | bytes 393224 | tf_op jit(solution)/shard_map/ppermute | solution.py:379
  11.3 3.0 %collective-permute-start.5 = (f32[64,512]{1,0:T(8,128)S(1)}, f32[64,512]{1,0:T(8,128)S(1)}, u32[]{:S(2)}, u32[]{:S(2)}) collective-permute-start(f32[64,512]{1,0:T(8,128)S(1)} %pad_maximum_fusion.2), channel_id=1, source_target_pairs={{0,24},{4,28},{8,16},{12,20},{16,8},{20,12},{24,0},{28,4},{1,25},{... | collective-permute-start | bytes 393224 | tf_op jit(solution)/shard_map/ppermute | solution.py:379
  14.3 7.8 %collective-permute-done.3.refs_1_ = f32[64,512]{1,0:T(8,128)S(1)} collective-permute-done((f32[64,512]{1,0:T(8,128)S(1)}, f32[64,512]{1,0:T(8,128)S(1)}, u32[]{:S(2)}, u32[]{:S(2)}) %collective-permute-start.3) | collective-permute-done | bytes 131104 | tf_op jit(solution)/shard_map/ppermute | solution.py:379
  22.1 1.5 %collective-permute-start.1 = (f32[2,64,512]{2,1,0:T(8,128)S(1)}, f32[2,64,512]{2,1,0:T(8,128)S(1)}, u32[]{:S(2)}, u32[]{:S(2)}) collective-permute-start(f32[2,64,512]{2,1,0:T(8,128)S(1)} %get-tuple-element.14), channel_id=1, source_target_pairs={{0,2},{2,0},{1,3},{3,1},{4,6},{6,4},{5,7},{7,5},{8,10},{10,8},{9,1... | collective-permute-start | bytes 786440 | tf_op jit(solution)/shard_map/ppermute | solution.py:384
  23.6 0.0 collective-permute-done.5.refs_3_
  23.7 0.0 collective-permute-done.4.refs_2_
  23.8 0.1 collective-permute-start.6
  23.8 0.0 copy-done
  23.9 0.0 copy-start.2
  23.9 0.0 collective-permute-done.7.column_low.column_high
  23.9 0.0 copy-done.1
  23.9 0.0 copy-done.3
  23.9 5.7 %stencil.1 = (f32[2,64,16,512]{3,2,1,0:T(8,128)}, f32[2,64,16,512]{3,2,1,0:T(8,128)S(1)}) custom-call(f32[2,64,16,512]{3,2,1,0:T(8,128)} %source.1, f32[64,16,512]{2,1,0:T(8,128)S(1)} %copy-done, s32[64,16,512]{2,1,0:T(8,128)S(1)} %copy-done.1, s32[4,16]{1,0:T(4,128)S(1)} %copy-done.3, f32[96,512]{1,0:T(8,128)S(1)} %collective-permute-done.2.near, ...), custom_call_target="tpu_custom_call" | custom-call | flops 268435456 | bytes 8388608 | tf_op jit(solution)/shard_map/stencil/pallas_call | solution.py:404
  29.6 0.0 copy-done.2
  29.6 1.2 %feed.1 = f32[520,512]{1,0:T(8,128)S(1)} custom-call(s32[8,8]{1,0:T(8,128)S(1)} %bitcast.7, f32[64,512]{1,0:T(8,128)S(1)} %slice_add_fusion.refs_0_, f32[64,512]{1,0:T(8,128)S(1)} %collective-permute-done.3.refs_1_, f32[64,512]{1,0:T(8,128)S(1)} %collective-permute-done.4.refs_2_, f32[64,512]{1,0:T(8,128)S(1)} %collective-permute-done.5.refs_3_), custom_call_target="tpu_custom_call" | custom-call | flops 33554432 | bytes 1048576 | tf_op jit(solution)/shard_map/feed/pallas_call | solution.py:420
  30.7 0.0 collective-permute-done.far
  30.8 0.0 collective-permute-done.1.axial_low.axial_high
  30.8 0.0 collective-permute-done.6.other
  30.8 1.6 %finish.1 = f32[2,64,16,512]{3,2,1,0:T(8,128)} custom-call(f32[32,512]{1,0:T(8,128)S(1)} %collective-permute-done.far, f32[16,512]{1,0:T(8,128)S(1)} %slice_bitcast_fusion.speed, f32[2,64,512]{2,1,0:T(8,128)S(1)} %collective-permute-done.1.axial_low.axial_high, ...), custom_call_target="tpu_custom_call", output_to_operand_aliasing={{}: (10, {})} | custom-call | flops 67108864 | bytes 8388608 | tf_op jit(solution)/shard_map/finish/pallas_call | solution.py:432
  (18 shorter events, 0.2 us)
Async XLA Ops:
  0.0 8.4 %copy-start.4 = (f32[2,32]{1,0:T(2,128)S(1)}, f32[2,32]{1,0:T(2,128)}, u32[]{:S(2)}) copy-start(f32[2,32]{1,0:T(2,128)} %param.12) | copy-start | bytes 772
  0.2 23.7 %copy-start = (f32[64,16,512]{2,1,0:T(8,128)S(1)}, f32[64,16,512]{2,1,0:T(8,128)}, u32[]{:S(2)}) copy-start(f32[64,16,512]{2,1,0:T(8,128)} %swirl.1) | copy-start | bytes 6291460
  0.2 23.7 %copy-start.1 = (s32[64,16,512]{2,1,0:T(8,128)S(1)}, s32[64,16,512]{2,1,0:T(8,128)}, u32[]{:S(2)}) copy-start(s32[64,16,512]{2,1,0:T(8,128)} %mask.1) | copy-start | bytes 6291460
  0.2 23.7 %copy-start.3 = (s32[4,16]{1,0:T(4,128)S(1)}, s32[4,16]{1,0:T(4,128)}, u32[]{:S(2)}) copy-start(s32[4,16]{1,0:T(4,128)} %flags.1) | copy-start | bytes 772
  2.4 21.5 %collective-permute-start.7 = (f32[2,8,128]{2,1,0:T(8,128)S(1)}, f32[2,8,128]{2,1,0:T(8,128)S(1)}, u32[]{:S(2)}, u32[]{:S(2)}) collective-permute-start(f32[2,8,128]{2,1,0:T(8,128)S(1)} %bitcast.6), channel_id=1, source_target_pairs={{0,1},{1,0},{2,3},{3,2},{4,5},{5,4},{6,7},{7,6},{8,9},{9,8},{10,11... | collective-permute-start | bytes 24584 | tf_op jit(solution)/shard_map/ppermute | solution.py:384
  5.4 25.3 %collective-permute-start = (f32[32,512]{1,0:T(8,128)S(1)}, f32[32,512]{1,0:T(8,128)S(1)}, u32[]{:S(2)}, u32[]{:S(2)}) collective-permute-start(f32[32,512]{1,0:T(8,128)S(1)} %get-tuple-element.13), channel_id=1, source_target_pairs={{0,28},{4,8},{8,4},{12,16},{16,12},{20,24},{24,20},{28,0},{1,29},{... | collective-permute-start | bytes 196616 | tf_op jit(solution)/shard_map/ppermute | solution.py:391
  8.2 1.4 %collective-permute-start.2 = (f32[96,512]{1,0:T(8,128)S(1)}, f32[96,512]{1,0:T(8,128)S(1)}, u32[]{:S(2)}, u32[]{:S(2)}) collective-permute-start(f32[96,512]{1,0:T(8,128)S(1)} %get-tuple-element.17), channel_id=1, source_target_pairs={{0,4},{4,0},{8,12},{12,8},{16,20},{20,16},{24,28},{28,24},{1,5},{5... | collective-permute-start | bytes 589832 | tf_op jit(solution)/shard_map/ppermute | solution.py:379
  9.7 14.0 %collective-permute-start.4 = (f32[64,512]{1,0:T(8,128)S(1)}, f32[64,512]{1,0:T(8,128)S(1)}, u32[]{:S(2)}, u32[]{:S(2)}) collective-permute-start(f32[64,512]{1,0:T(8,128)S(1)} %pad_maximum_fusion.1), channel_id=1, source_target_pairs={{0,16},{4,20},{8,24},{12,28},{16,0},{20,4},{24,8},{28,12},{1,17},{... | collective-permute-start | bytes 393224 | tf_op jit(solution)/shard_map/ppermute | solution.py:379
  11.0 11.2 %collective-permute-start.3 = (f32[64,512]{1,0:T(8,128)S(1)}, f32[64,512]{1,0:T(8,128)S(1)}, u32[]{:S(2)}, u32[]{:S(2)}) collective-permute-start(f32[64,512]{1,0:T(8,128)S(1)} %pad_maximum_fusion), channel_id=1, source_target_pairs={{0,8},{4,12},{8,0},{12,4},{16,24},{20,28},{24,16},{28,20},{1,9},{5... | collective-permute-start | bytes 393224 | tf_op jit(solution)/shard_map/ppermute | solution.py:379
  11.3 12.4 %collective-permute-start.5 = (f32[64,512]{1,0:T(8,128)S(1)}, f32[64,512]{1,0:T(8,128)S(1)}, u32[]{:S(2)}, u32[]{:S(2)}) collective-permute-start(f32[64,512]{1,0:T(8,128)S(1)} %pad_maximum_fusion.2), channel_id=1, source_target_pairs={{0,24},{4,28},{8,16},{12,20},{16,8},{20,12},{24,0},{28,4},{1,25},{... | collective-permute-start | bytes 393224 | tf_op jit(solution)/shard_map/ppermute | solution.py:379
  22.1 8.7 %collective-permute-start.1 = (f32[2,64,512]{2,1,0:T(8,128)S(1)}, f32[2,64,512]{2,1,0:T(8,128)S(1)}, u32[]{:S(2)}, u32[]{:S(2)}) collective-permute-start(f32[2,64,512]{2,1,0:T(8,128)S(1)} %get-tuple-element.14), channel_id=1, source_target_pairs={{0,2},{2,0},{1,3},{3,1},{4,6},{6,4},{5,7},{7,5},{8,10},{10,8},{9,1... | collective-permute-start | bytes 786440 | tf_op jit(solution)/shard_map/ppermute | solution.py:384
  23.8 7.0 %collective-permute-start.6 = (f32[64,512]{1,0:T(8,128)S(1)}, f32[64,512]{1,0:T(8,128)S(1)}, u32[]{:S(2)}, u32[]{:S(2)}) collective-permute-start(f32[64,512]{1,0:T(8,128)S(1)} %fusion.1.own), channel_id=1, source_target_pairs={{0,4},{4,0},{8,12},{12,8},{16,20},{20,16},{24,28},{28,24},{1,5},{5... | collective-permute-start | bytes 393224 | tf_op jit(solution)/shard_map/ppermute | solution.py:379
  23.9 5.7 %copy-start.2 = (s32[1,8,8]{2,1,0:T(8,128)S(1)}, s32[1,8,8]{2,1,0:T(8,128)}, u32[]{:S(2)}) copy-start(s32[1,8,8]{2,1,0:T(8,128)} %param.15) | copy-start | bytes 772
